TPU v7x, 128 devices: a whole 4x4x4 slice. The times are simulated.
128 devices in a mesh: dp: 16 (over x, z), expert: 8 (over y, core).
Axes of the slice: x: 4, y: 4, z: 4, core: 2. Of those that a mesh axis runs over, the one named last changes fastest.
Arguments:
- tokens: bfloat16 [16384, 4096], P(('dp', 'expert')), may hold values from -6 to 6
- select: int32 [8, 512], P(None, ('dp', 'expert')), may hold values from -1 to 127, as said below
- gates: float32 [8, 512], P(None, ('dp', 'expert')), may hold values from 0.1 to 1
- w_gate: bfloat16 [8, 4096, 8192], P('expert', None, 'dp'), may hold values from -0.09375 to 0.09375
- w_up: bfloat16 [8, 4096, 8192], P('expert', None, 'dp'), may hold values from -0.09375 to 0.09375
- w_down: bfloat16 [8, 8192, 4096], P('expert', 'dp'), may hold values from -0.0625 to 0.0625
Outputs:
- mixed: bfloat16 [16384, 4096], P(('dp', 'expert'))
Inputs may be any that keep to these rules, and one draw needn't show every extreme that they name: `select`: in each block of 4 slots of a row, the live entries come first, distinct and ascending, below 128, followed by -1; every block holds at least one live entry, and every expert fills all 4 slots of some source device.
All inputs are finite; a program needn't handle non-finite values.
Results may differ from a plain program's by a relative error of at most 0.0085.
Values may be sent and summed in bfloat16 or wider, within the bound.
A program may use at most 64 MiB of HBM per device.

v0:
```python
import jax
import jax.numpy as jnp
from jax import lax
from jax.sharding import PartitionSpec as P


def split_up(array, dim, devices):
    lengths = array.shape
    parts = array.reshape(*lengths[:dim], devices, lengths[dim] // devices, *lengths[dim + 1 :])
    return jnp.moveaxis(parts, dim, 0)


def summed_on_arrival(array, axis, dim):
    parts = split_up(array, dim, lax.axis_size(axis))
    arrived = lax.all_to_all(parts, axis, split_axis=0, concat_axis=0, tiled=True)
    return arrived.astype(jnp.float32).sum(axis=0)


def expert_ffn(block_rows, w_gate, w_up, w_down):
    gate_val = jnp.einsum("erd,edf->erf", block_rows, w_gate, preferred_element_type=jnp.float32)
    up_val = jnp.einsum("erd,edf->erf", block_rows, w_up, preferred_element_type=jnp.float32)
    hidden = (jax.nn.silu(gate_val) * up_val).astype(jnp.bfloat16)
    return jnp.einsum("erf,efd->erd", hidden, w_down, preferred_element_type=jnp.float32)


def per_device(tokens, select, gates, w_gate, w_up, w_down):
    experts, slot_count = select.shape
    tok_dev, width = tokens.shape
    is_live = select >= 0
    safe_idx = jnp.where(is_live, select, 0)
    sel_rows = jnp.take(tokens, safe_idx.reshape(-1), axis=0).reshape(experts, slot_count, width)
    sel_rows = jnp.where(is_live[:, :, None], sel_rows, 0)
    arrived = lax.all_to_all(sel_rows, "expert", split_axis=0, concat_axis=1, tiled=True)
    partial_value = expert_ffn(
        lax.all_gather(arrived, "dp", axis=1, tiled=True), w_gate, w_up, w_down
    )
    summed = summed_on_arrival(partial_value.astype(jnp.bfloat16), "dp", 1)
    returned = lax.all_to_all(
        summed.astype(jnp.bfloat16), "expert", split_axis=1, concat_axis=0, tiled=True
    )
    weight_flat = jnp.where(is_live, gates, 0.0).reshape(-1)
    token_ids = jnp.arange(tok_dev, dtype=jnp.int32)
    combine = jnp.where(
        safe_idx.reshape(-1)[None, :] == token_ids[:, None], weight_flat[None, :], 0.0
    )
    mixed = jnp.dot(
        combine, returned.reshape(-1, width).astype(jnp.float32), precision=lax.Precision.HIGHEST
    )
    return mixed.astype(jnp.bfloat16)


def solution(mesh):
    return jax.shard_map(
        per_device,
        mesh=mesh,
        in_specs=(
            P(("dp", "expert"), None),
            P(None, ("dp", "expert")),
            P(None, ("dp", "expert")),
            P("expert", None, "dp"),
            P("expert", None, "dp"),
            P("expert", "dp", None),
        ),
        out_specs=P(("dp", "expert"), None),
        check_vma=False,
    )
```

profile of v0, /device:TPU:1, one launch (start us, length us, event | category | flops | bytes accessed | tf_op | source)
XLA Modules:
  0.0 169.2 jit_solution(1057768432333072971)
XLA Ops:
  6.5 0.0 copy-start
  6.5 0.0 all-gather.2.cloned.1.call-start
  6.5 0.8 broadcast_select_fusion
  7.3 0.1 copy.25
  7.4 0.7 compare_and_fusion
  8.1 0.1 copy.26
  8.2 0.1 copy.23
  8.3 0.1 reshape.84
  8.4 0.0 copy-done
  8.4 0.7 gather_fusion
  9.1 0.1 gather.7
  9.2 0.2 select_select_fusion
  9.5 12.2 %all_to_all.26 = bf16[8,4,4096]{2,1,0:T(4,128)(2,1)S(1)} all-to-all(bf16[8,4,4096]{2,1,0:T(4,128)(2,1)S(1)} %select_select_fusion), channel_id=1, replica_groups=mesh['dp'=16,'expert'=8] {'expert'}, dimensions={0} | all-to-all | bytes 524288 | tf_op jit(solution)/shard_map/all_to_all | solution.py:33
  21.7 0.8 all_to_all.9
  22.5 0.0 all-gather.2.cloned.1.call-update
  22.5 52.2 %all-gather.2.cloned.1.call-done = bf16[1,512,4096]{2,1,0:T(8,128)(2,1)} async-done(((bf16[1,32,4096]{2,1,0:T(8,128)(2,1)}), bf16[1,512,4096]{2,1,0:T(8,128)(2,1)}) %all-gather.2.cloned.1.call-update) | async-done | bytes 4194320 | tf_op jit(solution)/shard_map/all_gather | solution.py:35
  74.7 0.0 copy-start.1
  74.7 0.0 copy-start.3
  74.7 5.9 %fusion.3 = f32[512,512]{1,0:T(8,128)S(1)} fusion(bf16[1,4096,512]{2,1,0:T(8,128)(2,1)} %param.9, bf16[1,512,4096]{2,1,0:T(8,128)(2,1)} %all-gather.2.cloned.1.call-done), kind=kOutput, calls=%fused_computation.6 | convolution fusion | flops 2147483648 | bytes 9437184 | tf_op jit(solution)/shard_map/erd,edf->erf/dot_general | solution.py:20
  80.6 0.0 copy-done.1
  80.6 0.0 copy-done.3
  80.6 0.0 copy-start.2
  80.7 2.4 %fusion.12 = bf16[512,512]{1,0:T(8,128)(2,1)S(1)} fusion(bf16[1,4096,512]{2,1,0:T(8,128)(2,1)S(1)} %copy-done.1, bf16[1,512,4096]{2,1,0:T(8,128)(2,1)S(1)} %copy-done.3, f32[512,512]{1,0:T(8,128)S(1)} %fusion.3), kind=kOutput, calls=%fused_computation.11 | convolution fusion | flops 2149056512 | bytes 9961472 | tf_op jit(solution)/shard_map/erd,edf->erf/dot_general | solution.py:21
  83.1 0.0 copy-done.2
  83.1 2.3 %convolution_convert_fusion = bf16[512,4096]{1,0:T(8,128)(2,1)S(1)} fusion(bf16[512,512]{1,0:T(8,128)(2,1)S(1)} %fusion.12, bf16[1,512,4096]{2,1,0:T(8,128)(2,1)S(1)} %copy-done.2), kind=kOutput, calls=%fused_computation.1 | convolution fusion | flops 2149580800 | bytes 8912896 | tf_op jit(solution)/shard_map/erf,efd->erd/dot_general | solution.py:23
  85.4 54.5 %all_to_all.27 = bf16[16,1,32,4096]{3,2,1,0:T(8,128)(2,1)} all-to-all(bf16[16,1,32,4096]{3,2,1,0:T(8,128)(2,1)S(1)} %bitcast.36), channel_id=1, replica_groups=mesh['dp'=16,'expert'=8] {'dp'}, dimensions={0} | all-to-all | bytes 8388608 | tf_op jit(solution)/shard_map/all_to_all | solution.py:15
  139.9 3.0 %reduce_sum.14 = bf16[32,4096]{1,0:T(8,128)(2,1)S(1)} reduce(bf16[16,1,32,4096]{3,2,1,0:T(8,128)(2,1)} %all_to_all.27, bf16[]{:T(256)} %constant.24.clone.1), dimensions={0,1}, to_apply=%region_0.1 | reduce | flops 1966080 | bytes 4456450 | tf_op jit(solution)/shard_map/reduce_sum | solution.py:16
  142.9 0.5 copy.36
  143.5 0.5 broadcast.40
  144.0 2.2 %reduce.2 = bf16[32,4096]{1,0:T(8,128)(2,1)S(1)} reduce(bf16[32,1,4096]{2,1,0:T(2,128)(2,1)S(1)} %bitcast.37, bf16[]{:T(256)} %broadcast.40), dimensions={1}, to_apply=%bitcast.35.reduce_sub_computation | reduce | bytes 524290
  146.2 0.9 reshape.98
  147.2 6.4 %all-to-all-start.2 = ((bf16[8,2,8192]{2,1,0:T(2,128)(2,1)}), bf16[8,2,8192]{2,1,0:T(2,128)(2,1)S(1)}, u32[]{:S(2)}, u32[]{:S(2)}) async-start(bf16[8,2,8192]{2,1,0:T(2,128)(2,1)} %reshape.98), calls=%async_computation.2 | async-start | bytes 524288 | tf_op jit(solution)/shard_map/all_to_all | solution.py:38
  153.6 0.1 eq.15
  153.7 0.1 copy.24
  153.8 0.1 broadcast_in_dim.45
  153.8 6.2 %all-to-all-done.2 = bf16[8,2,8192]{2,1,0:T(2,128)(2,1)S(1)} async-done(((bf16[8,2,8192]{2,1,0:T(2,128)(2,1)}), bf16[8,2,8192]{2,1,0:T(2,128)(2,1)S(1)}, u32[]{:S(2)}, u32[]{:S(2)}) %all-to-all-start.2) | async-done | bytes 262176 | tf_op jit(solution)/shard_map/all_to_all | solution.py:38
  160.1 0.3 reshape.99
  160.3 2.0 %convolution_convert_fusion.1 = bf16[128,4096]{1,0:T(8,128)(2,1)} fusion(bf16[1,32,4096]{2,0,1:T(2,128)(2,1)S(1)} %bitcast.38, f32[32]{0:T(128)S(1)} %broadcast_in_dim.45, s32[32]{0:T(128)S(1)} %eq.15), kind=kOutput, calls=%fused_computation.2 | convolution fusion | flops 201859072 | bytes 1310976 | tf_op jit(solution)/shard_map/dot_general | solution.py:46
  (2 shorter events, 0.0 us)
Async XLA Ops:
  6.5 1.9 %copy-start = (bf16[128,4096]{1,0:T(8,128)(2,1)S(1)}, bf16[128,4096]{1,0:T(8,128)(2,1)}, u32[]{:S(2)}) copy-start(bf16[128,4096]{1,0:T(8,128)(2,1)} %param.6) | copy-start | bytes 3145732
  6.5 68.2 %all-gather.2.cloned.1.call-start = ((), (), s32[]{:S(2)}) async-start(), calls=%async_computation.3 | async-start | bytes 4456448 | tf_op jit(solution)/shard_map/all_gather | solution.py:35
  74.7 5.9 %copy-start.1 = (bf16[1,4096,512]{2,1,0:T(8,128)(2,1)S(1)}, bf16[1,4096,512]{2,1,0:T(8,128)(2,1)}, u32[]{:S(2)}) copy-start(bf16[1,4096,512]{2,1,0:T(8,128)(2,1)} %param.10) | copy-start | bytes 12582916
  74.7 5.9 %copy-start.3 = (bf16[1,512,4096]{2,1,0:T(8,128)(2,1)S(1)}, bf16[1,512,4096]{2,1,0:T(8,128)(2,1)}, u32[]{:S(2)}) copy-start(bf16[1,512,4096]{2,1,0:T(8,128)(2,1)} %all-gather.2.cloned.1.call-done) | copy-start | bytes 12582916
  80.6 2.4 %copy-start.2 = (bf16[1,512,4096]{2,1,0:T(8,128)(2,1)S(1)}, bf16[1,512,4096]{2,1,0:T(8,128)(2,1)}, u32[]{:S(2)}) copy-start(bf16[1,512,4096]{2,1,0:T(8,128)(2,1)} %param.11) | copy-start | bytes 12582916
  147.2 12.9 %all-to-all-start.2 = ((bf16[8,2,8192]{2,1,0:T(2,128)(2,1)}), bf16[8,2,8192]{2,1,0:T(2,128)(2,1)S(1)}, u32[]{:S(2)}, u32[]{:S(2)}) async-start(bf16[8,2,8192]{2,1,0:T(2,128)(2,1)} %reshape.98), calls=%async_computation.2 | async-start | bytes 524288 | tf_op jit(solution)/shard_map/all_to_all | solution.py:38
Sparse Core Ops, SparseCore 0:
  22.6 52.0 all-gather.1
where the time goes:
time: 170 us; the launch traced here: 169 us
  blocking collectives  66.7 us (39%)
  waiting for transfers between devices  58.4 us (34%)
  between operations  13.5 us (8%)
  matrix products  12.7 us (7%)
  other arithmetic  6.98 us (4%)
  starting transfers between devices  6.45 us (4%)
  local copies, waits for them, and re-layouts  4.44 us (3%)
    all_to_all x1, blocking collectives, summed_on_arrival(): lax.all_to_all(parts, axis, split_axis=0, concat_axis=0, tiled=True)  54.5 us
    all_gather x1, waiting for transfers between devices, per_device(): lax.all_gather(arrived, 'dp', axis=1, tiled=True)  52.2 us
    all_to_all x1, blocking collectives, per_device(): lax.all_to_all(sel_rows, 'expert', split_axis=0, concat_axis=1, tiled=True)  12.2 us
    all_to_all x1, starting transfers between devices, per_device(): lax.all_to_all(summed.astype(jnp.bfloat16), 'expert', split_axis=1, conca...  6.45 us
    all_to_all x1, waiting for transfers between devices, per_device(): lax.all_to_all(summed.astype(jnp.bfloat16), 'expert', split_axis=1, conca...  6.23 us
    dot_general x1, matrix products, expert_ffn(): jnp.einsum('erd,edf->erf', block_rows, w_gate, preferred_element_type=jnp...  5.92 us
  transfers between devices with their start and end apart: 2, of which 2 were waited for; matrix products, arithmetic and copies ran while one was open for 0% of the time, Pallas kernels for 0%

commit v1 on v0

v1 whole, which is shorter than its diff:
```python
import functools

import jax
import jax.numpy as jnp
from jax import lax
from jax.experimental import pallas as pl
from jax.experimental.pallas import tpu as pltpu
from jax.sharding import PartitionSpec as P

MESH = pl.DeviceIdType.MESH
BF16, F32 = jnp.bfloat16, jnp.float32
RING = 4
N_SEM = 256
RSET, LSET = (0, 3), (2, 1)


def kernel(
    sel_ref, gate_ref, tok_ref, wg_ref, wu_ref, wd_ref, out_ref,
    wg_v, wu_v, wd_v, send4, recv4, ret4, rows, part, hid, relay, fin_l, fin_r, summed,
    relay1, fin1_l, fin1_r, slots32, comb, send_sem, recv_sem, w_sem,
):
    slot = sel_ref.shape[1]
    tok_dev, width = tok_ref.shape
    groups = 2 * RING
    n_slots = groups * slot
    halfw = width // 2
    quart = width // 4
    chunk = rows.shape[2]

    dp = lax.axis_index("dp")
    ex = lax.axis_index("expert")
    my_x, my_z = dp // RING, dp % RING
    my_y, my_c = ex // 2, ex % 2

    def at_x(step):
        return (((my_x + step + RING) % RING) * RING + my_z, ex)

    def at_z(step):
        return (my_x * RING + (my_z + step + RING) % RING, ex)

    def expert_at(g):
        return ((my_y + g // 2) % RING) * 2 + (my_c + g % 2) % 2

    def at_group(g):
        return (dp, expert_at(g))

    def back(g):
        return ((RING - g // 2) % RING) * 2 + g % 2

    barrier = pltpu.get_barrier_semaphore()
    partners = [at_x(1), at_x(-1), at_z(1), at_z(-1)] + [at_group(g) for g in range(1, groups)]
    for who in partners:
        pl.semaphore_signal(barrier, inc=1, device_id=who, device_id_type=MESH)

    loads = [
        pltpu.make_async_copy(wg_ref, wg_v, w_sem.at[0]),
        pltpu.make_async_copy(wu_ref, wu_v, w_sem.at[1]),
        pltpu.make_async_copy(wd_ref, wd_v, w_sem.at[2]),
    ]
    for load in loads:
        load.start()

    used = []

    def remote(src, dst, who):
        i = len(used)
        copy = pltpu.make_async_remote_copy(
            src_ref=src, dst_ref=dst, send_sem=send_sem.at[i], recv_sem=recv_sem.at[i],
            device_id=who, device_id_type=MESH,
        )
        used.append(copy)
        copy.start()
        return copy

    row_id = lax.broadcasted_iota(jnp.int32, (n_slots, tok_dev), 0)
    lane_id = lax.broadcasted_iota(jnp.int32, (n_slots, tok_dev), 1)
    idx = jnp.full((n_slots, tok_dev), -1, jnp.int32)
    lane8 = lax.broadcasted_iota(jnp.int32, (8, 128), 1)
    idx_l = jnp.full((8, 128), -1, jnp.int32)
    gate_l = jnp.zeros((8, 128), F32)
    for g in range(groups):
        e = expert_at(g)
        for j in range(slot):
            k = g * slot + j
            v = sel_ref[e, j]
            idx = jnp.where(row_id == k, v, idx)
            here = lane8 % n_slots == k
            idx_l = jnp.where(here, v, idx_l)
            gate_l = jnp.where(here, gate_ref[e, j], gate_l)
    onehot = jnp.where(lane_id == idx, 1.0, 0.0).astype(BF16)
    for c in range(0, width, 1024):
        cols = slice(c, c + 1024)
        slots32[:, cols] = jnp.dot(onehot, tok_ref[:, cols], preferred_element_type=F32)
    recv4[0] = slots32[0:slot, :].astype(BF16)
    for g in range(1, groups):
        send4[g] = slots32[g * slot : (g + 1) * slot, :].astype(BF16)

    pl.semaphore_wait(barrier, len(partners))
    near = [1, 6, 7]
    far = [4, 5, 2, 3]
    sent = {}
    for g in near + far:
        sent[g] = remote(send4.at[g], recv4.at[back(g)], at_group(g))

    g1 = gate_l.astype(BF16).astype(F32)
    rest = gate_l - g1
    g2 = rest.astype(BF16).astype(F32)
    g3 = (rest - g2).astype(BF16).astype(F32)
    term = lane8 // n_slots
    gate3 = jnp.where(term == 0, g1, jnp.where(term == 1, g2, jnp.where(term == 2, g3, 0.0)))
    tok_id = lax.broadcasted_iota(jnp.int32, (tok_dev, 128), 0)
    hit = tok_id == idx_l[0:1, :]
    comb[...] = jnp.where(hit, gate3[0:1, :], 0.0).astype(BF16)

    def cut(p, lo=0, n=halfw):
        return pl.ds(p * halfw + lo, n)

    def pos(p, d1, d2):
        d1, d2 = d1 % RING, d2 % RING
        return d2 * RING + d1 if p == 0 else d1 * RING + d2

    def first(p, step):
        return at_x(step) if p == 0 else at_z(step)

    def second(p, step):
        return at_z(step) if p == 0 else at_x(step)

    def to_first(h, p, d1, step, lo=0, n=halfw):
        return remote(
            rows.at[h, pos(p, d1, 0), :, cut(p, lo, n)],
            rows.at[h, pos(p, d1 - step, 0), :, cut(p, lo, n)], first(p, step),
        )

    def to_second(h, p, d1, d2, step):
        return remote(
            rows.at[h, pos(p, d1, d2), :, cut(p)],
            rows.at[h, pos(p, d1, d2 - step), :, cut(p)], second(p, step),
        )

    got = {}

    def enter(h):
        for g in range(4 * h, 4 * h + 4):
            if g > 0:
                sent[back(g)].wait_recv()
        for i in range(4):
            slots32[i * slot : (i + 1) * slot, :] = recv4[4 * h + i].astype(F32)
        rows[h, 0] = slots32[0:chunk, :].astype(BF16)

    def gather0(h):
        for p in range(2):
            for step in (1, -1):
                got[h, p, "f", step] = to_first(h, p, 0, step)
        for p in range(2):
            for step in (1, -1):
                got[h, p, "s", 0, step] = to_second(h, p, 0, 0, step)

    def gather1(h):
        for p in range(2):
            for step, lo in ((1, 0), (-1, quart)):
                got[h, p, "f", step].wait_recv()
                got[h, p, "r", step] = to_first(h, p, -step, step, lo, quart)
        for p in range(2):
            for d1 in (-1, 1):
                for step in (1, -1):
                    got[h, p, "s", d1 % RING, step] = to_second(h, p, d1, 0, step)

    def relay2(h, p, d1):
        step = 1 if d1 in RSET else -1
        got[h, p, "s", d1, step].wait_recv()
        got[h, p, "t", d1] = to_second(h, p, d1, -step, step)

    def gather2(h):
        for p in range(2):
            for step in (1, -1):
                got[h, p, "r", step].wait_recv()
            for step in (1, -1):
                got[h, p, "s", 2, step] = to_second(h, p, 2, 0, step)

    def relays(h, which):
        for d1 in which:
            for p in range(2):
                relay2(h, p, d1)

    def gathered(h):
        for p in range(2):
            for d1 in range(RING):
                step = -1 if d1 in RSET else 1
                got[h, p, "s", d1, step].wait_recv()
        for p in range(2):
            for d1 in range(RING):
                got[h, p, "t", d1].wait_recv()

    ff = hid.shape[1]
    tn = 256

    def up_piece(h, n):
        lhs = rows[h].reshape(RING * RING * chunk, width)
        gate_val = jnp.dot(lhs, wg_v[:, n * tn : (n + 1) * tn], preferred_element_type=F32)
        up_val = jnp.dot(lhs, wu_v[:, n * tn : (n + 1) * tn], preferred_element_type=F32)
        act = gate_val / (1.0 + jnp.exp(-gate_val)) * up_val
        hid[:, n * tn : (n + 1) * tn] = act.astype(BF16)

    dn = 512

    def down_piece(h, n):
        cols = slice(n * dn, (n + 1) * dn)
        val = jnp.dot(hid[...], wd_v[:, cols], preferred_element_type=F32)
        part[h, :, :, cols] = val.astype(BF16).reshape(RING * RING, chunk, dn)

    red = {}

    def scatter0(h, p):
        for d1r, d1l in zip(RSET, LSET):
            red[h, p, "far", d1r] = remote(
                part.at[h, pos(p, d1r, 2), :, cut(p)], relay.at[h, p, d1r], second(p, 1))
            red[h, p, "far", d1l] = remote(
                part.at[h, pos(p, d1l, 2), :, cut(p)], relay.at[h, p, d1l], second(p, -1))
        for d1r, d1l in zip(RSET, LSET):
            red[h, p, "l", d1l] = remote(
                part.at[h, pos(p, d1l, 1), :, cut(p)], fin_l.at[h, p, d1l], second(p, 1))
            red[h, p, "r", d1r] = remote(
                part.at[h, pos(p, d1r, 3), :, cut(p)], fin_r.at[h, p, d1r], second(p, -1))

    def scatter1(h, p, d1):
        red[h, p, "far", d1].wait_recv()
        right = d1 in RSET
        own = part[h, pos(p, d1, 1 if right else 3), :, cut(p)]
        relay[h, p, d1] = (relay[h, p, d1].astype(F32) + own.astype(F32)).astype(BF16)
        if right:
            red[h, p, "l", d1] = remote(relay.at[h, p, d1], fin_l.at[h, p, d1], second(p, 1))
        else:
            red[h, p, "r", d1] = remote(relay.at[h, p, d1], fin_r.at[h, p, d1], second(p, -1))

    def scatter2(h, p, d1):
        red[h, p, "l", d1].wait_recv()
        red[h, p, "r", d1].wait_recv()
        own = part[h, pos(p, d1, 0), :, cut(p)]
        total = own.astype(F32) + fin_l[h, p, d1].astype(F32) + fin_r[h, p, d1].astype(F32)
        summed[h, p, d1] = total.astype(BF16)
        lo, hi = pl.ds(0, quart), pl.ds(quart, quart)
        if d1 == 2:
            red[h, p, "far1", 1] = remote(
                summed.at[h, p, 2, :, lo], relay1.at[h, p, :, lo], first(p, 1))
            red[h, p, "far1", -1] = remote(
                summed.at[h, p, 2, :, hi], relay1.at[h, p, :, hi], first(p, -1))
        elif d1 == 1:
            red[h, p, "l1", 1] = remote(
                summed.at[h, p, 1, :, hi], fin1_l.at[h, p, :, hi], first(p, 1))
        elif d1 == 3:
            red[h, p, "r1", 0] = remote(
                summed.at[h, p, 3, :, lo], fin1_r.at[h, p, :, lo], first(p, -1))

    def scatter3(h, p):
        for step, at, d1 in ((1, 0, 1), (-1, quart, 3)):
            cols = pl.ds(at, quart)
            red[h, p, "far1", step].wait_recv()
            relay1[h, p, :, cols] = (
                relay1[h, p, :, cols].astype(F32) + summed[h, p, d1, :, cols].astype(F32)
            ).astype(BF16)
            if step == 1:
                red[h, p, "l1", 0] = remote(
                    relay1.at[h, p, :, cols], fin1_l.at[h, p, :, cols], first(p, 1))
            else:
                red[h, p, "r1", 1] = remote(
                    relay1.at[h, p, :, cols], fin1_r.at[h, p, :, cols], first(p, -1))

    def scatter4(h, p):
        for i in range(2):
            red[h, p, "l1", i].wait_recv()
            red[h, p, "r1", i].wait_recv()
        total = (
            summed[h, p, 0].astype(F32) + fin1_l[h, p].astype(F32) + fin1_r[h, p].astype(F32)
        )
        slots32[0:chunk, cut(p)] = total

    returned = {}

    def leave(h):
        for i in range(4):
            g = 4 * h + i
            value = slots32[i * slot : (i + 1) * slot, :].astype(BF16)
            if g == 0:
                ret4[0] = value
            else:
                send4[g] = value
                returned[g] = remote(send4.at[g], ret4.at[back(g)], at_group(g))

    def sums(h, d1s):
        for d1 in d1s:
            for p in range(2):
                scatter2(h, p, d1)

    enter(0)
    gather0(0)
    enter(1)
    gather0(1)
    gather1(0)
    relays(0, (0,))
    gather2(0)
    relays(0, (3, 1, 2))
    gather1(1)
    relays(1, (0,))
    gathered(0)
    for load in loads:
        load.wait()
    up_piece(0, 0)
    gather2(1)
    relays(1, (3, 1))
    up_piece(0, 1)
    relays(1, (2,))
    n_down = width // dn
    for n in range(n_down // 2):
        down_piece(0, n)
    scatter0(0, 0)
    for n in range(n_down // 2, n_down):
        down_piece(0, n)
    scatter0(0, 1)
    gathered(1)
    up_piece(1, 0)
    for d1 in (2, 3, 1, 0):
        for p in range(2):
            scatter1(0, p, d1)
    up_piece(1, 1)
    for n in range(n_down // 2):
        down_piece(1, n)
    scatter0(1, 0)
    for n in range(n_down // 2, n_down):
        down_piece(1, n)
    scatter0(1, 1)
    sums(0, (2, 1, 3, 0))
    for p in range(2):
        scatter3(0, p)
    for d1 in (2, 3, 1, 0):
        for p in range(2):
            scatter1(1, p, d1)
    for p in range(2):
        scatter4(0, p)
    for g in range(1, groups):
        sent[g].wait_send()
    leave(0)
    sums(1, (2, 1, 3, 0))
    for p in range(2):
        scatter3(1, p)
    for p in range(2):
        scatter4(1, p)
    leave(1)

    for g in range(1, groups):
        returned[g].wait_recv()
    for g in range(groups):
        slots32[g * slot : (g + 1) * slot, :] = ret4[g].astype(F32)
    for c in range(0, width, 512):
        cols = slice(c, c + 512)
        value = slots32[:, cols].astype(BF16)
        stack = jnp.concatenate([value, value, value, jnp.zeros_like(value)], axis=0)
        out_ref[:, cols] = jnp.dot(comb[...], stack, preferred_element_type=F32).astype(BF16)

    firsts = [sent[g] for g in range(1, groups)]
    for copy in used:
        if not any(copy is f for f in firsts):
            copy.wait_send()


def per_device(tokens, select, gates, w_gate, w_up, w_down):
    tok_dev, width = tokens.shape
    slot = select.shape[1]
    ff = w_gate.shape[2]
    chunk = RING * slot
    halfw, quart = width // 2, width // 4
    vmem, any_ = pl.BlockSpec(memory_space=pltpu.VMEM), pl.BlockSpec(memory_space=pl.ANY)
    smem = pl.BlockSpec(memory_space=pltpu.SMEM)
    return pl.pallas_call(
        kernel,
        out_shape=jax.ShapeDtypeStruct((tok_dev, width), BF16),
        in_specs=[smem, smem, vmem, any_, any_, any_],
        out_specs=vmem,
        scratch_shapes=[
            pltpu.VMEM((width, ff), BF16),
            pltpu.VMEM((width, ff), BF16),
            pltpu.VMEM((ff, width), BF16),
            pltpu.VMEM((8, slot, width), BF16),
            pltpu.VMEM((8, slot, width), BF16),
            pltpu.VMEM((8, slot, width), BF16),
            pltpu.VMEM((2, 16, chunk, width), BF16),
            pltpu.VMEM((2, 16, chunk, width), BF16),
            pltpu.VMEM((16 * chunk, ff), BF16),
            pltpu.VMEM((2, 2, 4, chunk, halfw), BF16),
            pltpu.VMEM((2, 2, 4, chunk, halfw), BF16),
            pltpu.VMEM((2, 2, 4, chunk, halfw), BF16),
            pltpu.VMEM((2, 2, 4, chunk, halfw), BF16),
            pltpu.VMEM((2, 2, chunk, halfw), BF16),
            pltpu.VMEM((2, 2, chunk, halfw), BF16),
            pltpu.VMEM((2, 2, chunk, halfw), BF16),
            pltpu.VMEM((8 * slot, width), F32),
            pltpu.VMEM((tok_dev, 128), BF16),
            pltpu.SemaphoreType.DMA((N_SEM,)),
            pltpu.SemaphoreType.DMA((N_SEM,)),
            pltpu.SemaphoreType.DMA((3,)),
        ],
        compiler_params=pltpu.CompilerParams(
            collective_id=0, has_side_effects=True, vmem_limit_bytes=60 * 1024 * 1024
        ),
        name="moe",
    )(
        select, gates, tokens, w_gate[0], w_up[0], w_down[0],
    )


def solution(mesh):
    return jax.shard_map(
        per_device,
        mesh=mesh,
        in_specs=(
            P(("dp", "expert"), None),
            P(None, ("dp", "expert")),
            P(None, ("dp", "expert")),
            P("expert", None, "dp"),
            P("expert", None, "dp"),
            P("expert", "dp", None),
        ),
        out_specs=P(("dp", "expert"), None),
        check_vma=False,
    )
```

time: 170 us -> 79.3 us (0.47)
  Pallas kernels: 0 us -> 73.9 us
  blocking collectives: 66.7 us -> 0 us
  waiting for transfers between devices: 58.4 us -> 0 us
  between operations: 13.5 us -> 0.01 us
  matrix products: 12.7 us -> 0 us
  other arithmetic: 6.98 us -> 0 us
  starting transfers between devices: 6.45 us -> 0 us
    pallas_call x0 -> x1, Pallas kernels: none -> 73.9 us  [per_device(): pl.pallas_call(kernel, out_shape=jax.ShapeDtypeStruct((tok_dev, width), B...]
    all_to_all x2 -> x0, blocking collectives: 66.7 us -> none  [the longest x1 54.5 us: summed_on_arrival(): lax.all_to_all(parts, axis, split_axis=0, concat_axis=0, tiled=True)]
    all_gather x1 -> x0, waiting for transfers between devices: 52.2 us -> none  [per_device(): lax.all_gather(arrived, 'dp', axis=1, tiled=True)]
    dot_general x4 -> x0, matrix products: 12.7 us -> none  [the longest x1 5.92 us: expert_ffn(): jnp.einsum('erd,edf->erf', block_rows, w_gate, preferred_element_type=jnp...]
    all_to_all x1 -> x0, starting transfers between devices: 6.45 us -> none  [per_device(): lax.all_to_all(summed.astype(jnp.bfloat16), 'expert', split_axis=1, conca...]
    all_to_all x1 -> x0, waiting for transfers between devices: 6.23 us -> none  [per_device(): lax.all_to_all(summed.astype(jnp.bfloat16), 'expert', split_axis=1, conca...]
    unnamed x11 -> x3, local copies, waits for them, and re-layouts: 1.72 us -> 4.98 us
    reduce_sum x1 -> x0, other arithmetic: 2.98 us -> none  [summed_on_arrival(): return arrived.astype(jnp.float32).sum(axis=0)]
  transfers between devices with their start and end apart: 2 -> 0, of which waited for: 2 -> 0; matrix products, arithmetic and copies ran while one was open for 0% -> 0% of each run, Pallas kernels for 0% -> 0%
where the time goes in v1:
time: 79.3 us; the launch traced here: 78.9 us
  Pallas kernels  73.9 us (93%)
  local copies, waits for them, and re-layouts  4.98 us (6%)
    pallas_call x1, Pallas kernels, per_device(): pl.pallas_call(kernel, out_shape=jax.ShapeDtypeStruct((tok_dev, width), B...  73.9 us
    unnamed x3, local copies, waits for them, and re-layouts  4.98 us

profile of v1, /device:TPU:1, one launch (start us, length us, event | category | flops | bytes accessed | tf_op | source)
XLA Modules:
  0.0 78.9 jit_solution(12668741571246774533)
XLA Ops:
  0.0 1.3 %copy.7.sel_ref = s32[8,4]{1,0:T(8,128)} copy(s32[8,4]{0,1:T(4,128)} %param.7) | data formatting | bytes 256 | tf_op args[1]
  1.3 1.3 %copy.8.gate_ref = f32[8,4]{1,0:T(8,128)} copy(f32[8,4]{0,1:T(4,128)} %param.8) | data formatting | bytes 256 | tf_op args[2]
  2.7 73.9 %moe.1 = bf16[128,4096]{1,0:T(8,128)(2,1)} custom-call(s32[8,4]{1,0:T(8,128)} %copy.7.sel_ref, f32[8,4]{1,0:T(8,128)} %copy.8.gate_ref, bf16[128,4096]{1,0:T(8,128)(2,1)} %tok_ref.1, bf16[4096,512]{1,0:T(8,128)(2,1)} %bitcast.3, bf16[4096,512]{1,0:T(8,128)(2,1)} %bitcast.4, bf16[512,4096]{1,0:T(8,128)(2,1)} %bitcast.5), custom_call_target="tpu_custom_call" | custom-call | tf_op jit(solution)/shard_map/moe/pallas_call | solution.py:373
  76.6 2.3 %copy.10 = bf16[128,4096]{1,0:T(8,128)(2,1)} copy(bf16[128,4096]{1,0:T(8,128)(2,1)} %moe.1) | data formatting | bytes 2097152

commit v2 on v1

--- a/solution.py
+++ b/solution.py
@@ -19,7 +19,7 @@
     wg_v, wu_v, wd_v, send4, recv4, ret4, rows, part, hid, relay, fin_l, fin_r, summed,
     relay1, fin1_l, fin1_r, slots32, comb, send_sem, recv_sem, w_sem,
 ):
-    slot = sel_ref.shape[1]
+    slot = sel_ref.shape[0]
     tok_dev, width = tok_ref.shape
     groups = 2 * RING
     n_slots = groups * slot
@@ -82,11 +82,11 @@
         e = expert_at(g)
         for j in range(slot):
             k = g * slot + j
-            v = sel_ref[e, j]
+            v = sel_ref[j, e]
             idx = jnp.where(row_id == k, v, idx)
             here = lane8 % n_slots == k
             idx_l = jnp.where(here, v, idx_l)
-            gate_l = jnp.where(here, gate_ref[e, j], gate_l)
+            gate_l = jnp.where(here, gate_ref[j, e], gate_l)
     onehot = jnp.where(lane_id == idx, 1.0, 0.0).astype(BF16)
     for c in range(0, width, 1024):
         cols = slice(c, c + 1024)
@@ -95,7 +95,8 @@
     for g in range(1, groups):
         send4[g] = slots32[g * slot : (g + 1) * slot, :].astype(BF16)
 
-    pl.semaphore_wait(barrier, len(partners))
+    with jax.named_scope("barrier"):
+        pl.semaphore_wait(barrier, len(partners))
     near = [1, 6, 7]
     far = [4, 5, 2, 3]
     sent = {}
@@ -291,63 +292,73 @@
             for p in range(2):
                 scatter2(h, p, d1)
 
-    enter(0)
-    gather0(0)
-    enter(1)
-    gather0(1)
-    gather1(0)
-    relays(0, (0,))
-    gather2(0)
-    relays(0, (3, 1, 2))
-    gather1(1)
-    relays(1, (0,))
-    gathered(0)
-    for load in loads:
-        load.wait()
-    up_piece(0, 0)
-    gather2(1)
-    relays(1, (3, 1))
-    up_piece(0, 1)
-    relays(1, (2,))
     n_down = width // dn
-    for n in range(n_down // 2):
-        down_piece(0, n)
-    scatter0(0, 0)
-    for n in range(n_down // 2, n_down):
-        down_piece(0, n)
-    scatter0(0, 1)
-    gathered(1)
-    up_piece(1, 0)
-    for d1 in (2, 3, 1, 0):
-        for p in range(2):
-            scatter1(0, p, d1)
-    up_piece(1, 1)
-    for n in range(n_down // 2):
-        down_piece(1, n)
-    scatter0(1, 0)
-    for n in range(n_down // 2, n_down):
-        down_piece(1, n)
-    scatter0(1, 1)
-    sums(0, (2, 1, 3, 0))
-    for p in range(2):
-        scatter3(0, p)
-    for d1 in (2, 3, 1, 0):
-        for p in range(2):
-            scatter1(1, p, d1)
-    for p in range(2):
-        scatter4(0, p)
-    for g in range(1, groups):
-        sent[g].wait_send()
-    leave(0)
-    sums(1, (2, 1, 3, 0))
-    for p in range(2):
-        scatter3(1, p)
-    for p in range(2):
-        scatter4(1, p)
-    leave(1)
-
-    for g in range(1, groups):
-        returned[g].wait_recv()
+
+    def downs(h, p):
+        for n in range(p * n_down // 2, (p + 1) * n_down // 2):
+            down_piece(h, n)
+        scatter0(h, p)
+
+    def weights():
+        for load in loads:
+            load.wait()
+
+    def relay_adds(h):
+        for d1 in (2, 3, 1, 0):
+            for p in range(2):
+                scatter1(h, p, d1)
+
+    def both(step, h):
+        for p in range(2):
+            step(h, p)
+
+    def sent_slots():
+        for g in range(1, groups):
+            sent[g].wait_send()
+
+    for name, step, *args in (
+        ("enter0", enter, 0),
+        ("g0_0", gather0, 0),
+        ("enter1", enter, 1),
+        ("g0_1", gather0, 1),
+        ("g1_0", gather1, 0),
+        ("rel0_0", relays, 0, (0,)),
+        ("g2_0", gather2, 0),
+        ("rel0", relays, 0, (3, 1, 2)),
+        ("g1_1", gather1, 1),
+        ("rel1_0", relays, 1, (0,)),
+        ("gathered0", gathered, 0),
+        ("weights", weights),
+        ("up0_0", up_piece, 0, 0),
+        ("g2_1", gather2, 1),
+        ("rel1_31", relays, 1, (3, 1)),
+        ("up0_1", up_piece, 0, 1),
+        ("rel1_2", relays, 1, (2,)),
+        ("down0_0", downs, 0, 0),
+        ("down0_1", downs, 0, 1),
+        ("gathered1", gathered, 1),
+        ("up1_0", up_piece, 1, 0),
+        ("add0", relay_adds, 0),
+        ("up1_1", up_piece, 1, 1),
+        ("down1_0", downs, 1, 0),
+        ("down1_1", downs, 1, 1),
+        ("sums0", sums, 0, (2, 1, 3, 0)),
+        ("s3_0", both, scatter3, 0),
+        ("add1", relay_adds, 1),
+        ("s4_0", both, scatter4, 0),
+        ("sent", sent_slots),
+        ("leave0", leave, 0),
+        ("sums1", sums, 1, (2, 1, 3, 0)),
+        ("s3_1", both, scatter3, 1),
+        ("s4_1", both, scatter4, 1),
+        ("leave1", leave, 1),
+    ):
+        with jax.named_scope(name):
+            step(*args)
+
+    with jax.named_scope("returned"):
+        for g in range(1, groups):
+            returned[g].wait_recv()
     for g in range(groups):
         slots32[g * slot : (g + 1) * slot, :] = ret4[g].astype(F32)
     for c in range(0, width, 512):
@@ -403,7 +414,7 @@
         ),
         name="moe",
     )(
-        select, gates, tokens, w_gate[0], w_up[0], w_down[0],
+        select.T, gates.T, tokens, w_gate[0], w_up[0], w_down[0],
     )
 
 

time: 79.3 us -> 76.5 us (0.965)
  local copies, waits for them, and re-layouts: 4.98 us -> 2.29 us
    unnamed x3 -> x1, local copies, waits for them, and re-layouts: 4.98 us -> 2.29 us
where the time goes in v2:
time: 76.5 us; the launch traced here: 76.2 us
  Pallas kernels  73.9 us (97%)
  local copies, waits for them, and re-layouts  2.29 us (3%)
    pallas_call x1, Pallas kernels, per_device(): pl.pallas_call(kernel, out_shape=jax.ShapeDtypeStruct((tok_dev, width), B...  73.9 us
    unnamed x1, local copies, waits for them, and re-layouts  2.29 us

profile of v2, /device:TPU:1, one launch (start us, length us, event | category | flops | bytes accessed | tf_op | source)
XLA Modules:
  0.0 76.2 jit_solution(2437697293191243391)
XLA Ops:
  0.0 73.9 %moe.1 = bf16[128,4096]{1,0:T(8,128)(2,1)} custom-call(s32[4,8]{1,0:T(4,128)} %bitcast.8, f32[4,8]{1,0:T(4,128)} %bitcast.9, bf16[128,4096]{1,0:T(8,128)(2,1)} %tok_ref.1, bf16[4096,512]{1,0:T(8,128)(2,1)} %bitcast.5, bf16[4096,512]{1,0:T(8,128)(2,1)} %bitcast.6, bf16[512,4096]{1,0:T(8,128)(2,1)} %bitcast.7), custom_call_target="tpu_custom_call" | custom-call | tf_op jit(solution)/shard_map/moe/pallas_call | solution.py:384
  73.9 2.3 %copy.8 = bf16[128,4096]{1,0:T(8,128)(2,1)} copy(bf16[128,4096]{1,0:T(8,128)(2,1)} %moe.1) | data formatting | bytes 2097152

commit v3 on v0

v3 whole, which is shorter than its diff:
```python
import jax
import jax.numpy as jnp
from jax import lax
from jax.experimental import pallas as pl
from jax.experimental.pallas import tpu as pltpu
from jax.sharding import PartitionSpec as P

MESH = pl.DeviceIdType.MESH
BF16, F32 = jnp.bfloat16, jnp.float32
RING = 4
SUB = 2
N_SEM = 320
RSET, LSET = (0, 3), (2, 1)
HALVES = ((0, 1, 2, 6), (3, 7, 4, 5))

ORDER = (
    ("own", 0), ("f", 0, 0, -1), ("f", 0, 1, -1), ("f", 0, 0, 1), ("f", 0, 1, 1), ("s", 0, 1, 0, 1),
    ("s", 0, 1, 0, -1), ("s", 0, 0, 0, -1), ("s", 0, 0, 0, 1), ("own", 1), ("s", 1, 1, 0, 1), ("f", 1, 1, -1),
    ("f", 1, 0, 1), ("s", 1, 0, 0, 1), ("f", 1, 0, -1), ("s", 1, 1, 0, -1), ("f", 1, 1, 1), ("s", 1, 0, 0, -1),
    ("r", 0, 0, -1), ("s", 0, 1, 1, -1), ("r", 0, 1, -1), ("r", 0, 0, 1), ("r", 0, 1, 1), ("s", 0, 1, 3, 1),
    ("s", 0, 1, 3, -1), ("s", 0, 0, 1, 1), ("s", 0, 1, 1, 1), ("s", 0, 0, 3, -1), ("s", 0, 0, 3, 1),
    ("s", 0, 0, 1, -1), ("t", 0, 1, 0), ("t", 0, 0, 0), ("r", 1, 0, -1), ("r", 1, 1, -1), ("s", 1, 1, 1, -1),
    ("t", 1, 1, 0), ("s", 1, 1, 1, 1), ("t", 1, 0, 0), ("s", 1, 0, 1, -1), ("s", 1, 0, 1, 1), ("s", 1, 0, 3, 1),
    ("s", 1, 1, 3, 1), ("r", 1, 1, 1), ("s", 1, 0, 3, -1), ("r", 1, 0, 1), ("s", 1, 1, 3, -1), ("s", 0, 0, 2, -1),
    ("s", 0, 0, 2, 1), ("s", 0, 1, 2, 1), ("s", 0, 1, 2, -1), ("t", 0, 1, 1), ("t", 0, 1, 3), ("t", 0, 0, 1),
    ("t", 0, 0, 3), ("t", 1, 1, 1), ("t", 1, 0, 1), ("t", 0, 1, 2), ("t", 0, 0, 2), ("t", 1, 1, 3), ("t", 1, 0, 3),
    ("s", 1, 0, 2, 1), ("s", 1, 1, 2, -1), ("s", 1, 0, 2, -1), ("s", 1, 1, 2, 1), ("up", 0, 0), ("up", 0, 1),
    ("t", 1, 1, 2), ("t", 1, 0, 2), ("down", 0, 0, 1), ("L", 0, 0, 2, 1), ("F", 0, 0, 0, 1), ("F", 0, 0, 3, 1),
    ("down", 0, 0, 0), ("F", 0, 0, 1, 0), ("F", 0, 0, 2, 0), ("R", 0, 0, 3, 1), ("L", 0, 0, 1, 1), ("R", 0, 0, 3, 0),
    ("F", 0, 0, 3, 0), ("R", 0, 0, 0, 1), ("down", 0, 1, 0), ("F", 0, 1, 2, 0), ("L", 0, 1, 1, 0), ("L", 0, 1, 2, 0),
    ("F", 0, 1, 1, 0), ("F", 0, 1, 3, 0), ("R", 0, 1, 0, 0), ("F", 0, 0, 2, 1), ("F", 0, 0, 1, 1), ("F", 0, 1, 0, 0),
    ("R", 0, 1, 3, 0), ("down", 0, 1, 1), ("F", 0, 1, 2, 1), ("R", 0, 1, 3, 1), ("L", 0, 1, 2, 1), ("L", 0, 1, 1, 1),
    ("F", 0, 1, 1, 1), ("F", 0, 1, 0, 1), ("L", 0, 0, 1, 0), ("R", 0, 1, 0, 1), ("L", 0, 0, 2, 0), ("F", 0, 0, 0, 0),
    ("F", 0, 1, 3, 1), ("R", 0, 0, 0, 0), ("up", 1, 0), ("A", 0, 0, 1, 0), ("up", 1, 1), ("down", 1, 1, 0),
    ("R", 1, 1, 3, 0), ("F", 1, 1, 3, 0), ("F", 1, 1, 0, 0), ("F", 1, 1, 2, 0), ("down", 1, 0, 1), ("F", 1, 0, 2, 1),
    ("R", 1, 0, 0, 1), ("F", 1, 0, 3, 1), ("L", 1, 0, 2, 1), ("down", 1, 0, 0), ("L", 1, 0, 2, 0), ("F", 1, 0, 3, 0),
    ("R", 1, 0, 3, 0), ("A", 0, 1, 2, 1), ("R", 1, 0, 0, 0), ("A", 0, 1, 1, 0), ("F", 1, 0, 2, 0), ("L", 1, 1, 2, 0),
    ("L", 1, 1, 1, 0), ("down", 1, 1, 1), ("A", 0, 0, 2, 1), ("L", 1, 1, 2, 1), ("F", 1, 1, 2, 1), ("F", 1, 1, 3, 1),
    ("L", 1, 1, 1, 1), ("A", 0, 0, 3, 1), ("R", 1, 1, 3, 1), ("F", 1, 1, 1, 0), ("R", 1, 0, 3, 1), ("F", 1, 0, 0, 1),
    ("A", 0, 0, 2, 0), ("L", 1, 0, 1, 0), ("F", 1, 0, 1, 0), ("F", 1, 1, 1, 1), ("A", 0, 1, 2, 0), ("L", 1, 0, 1, 1),
    ("F", 1, 1, 0, 1), ("F", 1, 0, 0, 0), ("F", 1, 0, 1, 1), ("R", 1, 1, 0, 1), ("R", 1, 1, 0, 0), ("A", 0, 1, 0, 0),
    ("A", 0, 0, 3, 0), ("A", 0, 0, 0, 0), ("A", 0, 0, 0, 1), ("A", 0, 1, 3, 0), ("A", 0, 1, 0, 1), ("A", 0, 1, 1, 1),
    ("A", 0, 0, 1, 1), ("A", 0, 1, 3, 1), ("A", 1, 1, 3, 0), ("S", 0, 0, 1, 0), ("A", 1, 0, 3, 1), ("A", 1, 1, 0, 0),
    ("A", 1, 1, 2, 0), ("A", 1, 0, 2, 1), ("S", 0, 1, 2, 1), ("S", 0, 1, 1, 0), ("A", 1, 0, 3, 0), ("A", 1, 1, 2, 1),
    ("S", 0, 0, 3, 1), ("A", 1, 1, 3, 1), ("A", 1, 0, 2, 0), ("A", 1, 0, 0, 1), ("A", 1, 1, 1, 0), ("S", 0, 0, 2, 1),
    ("A", 1, 1, 0, 1), ("A", 1, 1, 1, 1), ("S", 0, 1, 0, 0), ("S", 0, 1, 2, 0), ("S", 0, 0, 2, 0), ("A", 1, 0, 0, 0),
    ("S", 0, 1, 3, 0), ("A", 1, 0, 1, 0), ("S", 0, 0, 3, 0), ("S", 0, 1, 0, 1), ("A", 1, 0, 1, 1), ("S", 0, 0, 0, 0),
    ("S", 0, 1, 3, 1), ("S", 0, 1, 1, 1), ("S", 0, 0, 1, 1), ("S", 0, 0, 0, 1), ("S", 1, 1, 3, 0), ("S", 1, 1, 2, 0),
    ("S", 1, 0, 2, 1), ("S", 1, 0, 3, 1), ("B", 0, 1, -1, 1), ("B", 0, 1, 1, 1), ("S", 1, 1, 2, 1), ("S", 1, 1, 0, 0),
    ("S", 1, 0, 2, 0), ("B", 0, 1, -1, 0), ("S", 1, 0, 3, 0), ("S", 1, 1, 3, 1), ("S", 1, 1, 1, 0), ("B", 0, 0, 1, 1),
    ("B", 0, 0, -1, 1), ("S", 1, 0, 0, 1), ("S", 1, 0, 1, 0), ("B", 0, 1, 1, 0), ("S", 1, 1, 0, 1), ("S", 1, 1, 1, 1),
    ("B", 0, 0, 1, 0), ("B", 0, 0, -1, 0), ("S", 1, 0, 1, 1), ("S", 1, 0, 0, 0), ("B", 1, 0, 1, 1),
    ("B", 1, 0, -1, 1), ("B", 1, 1, 1, 0), ("B", 1, 0, 1, 0), ("B", 1, 1, -1, 0), ("B", 1, 0, -1, 0), ("Z", 0, 1, 1),
    ("B", 1, 1, 1, 1), ("B", 1, 1, -1, 1), ("Z", 0, 0, 1), ("Z", 0, 1, 0), ("Z", 0, 0, 0), ("Z", 1, 0, 1),
    ("Z", 1, 1, 0), ("Z", 1, 0, 0), ("X", 0, 1, 1), ("Z", 1, 1, 1), ("X", 0, 0, 1), ("X", 0, 1, 0), ("X", 0, 0, 0),
    ("X", 1, 0, 1), ("X", 1, 1, 0), ("X", 1, 0, 0), ("X", 1, 1, 1),
)


def kernel(
    sel_ref, gate_ref, tok_ref, wg_ref, wu_ref, wd_ref, slots_ref, comb_ref,
    tok_v, wg_v, wu_v, wd_v, send4, recv4, exit4, ret4, rows, part, hid, relay, fin_l, fin_r, summed,
    relay1, fin1_l, fin1_r, slots32, send_sem, recv_sem, load_sem,
):
    slot = sel_ref.shape[0]
    tok_dev, width = tok_ref.shape
    groups = 2 * RING
    n_slots = groups * slot
    halfw = width // 2
    quart = width // 4
    subw = halfw // SUB
    chunk = rows.shape[2]

    dp = lax.axis_index("dp")
    ex = lax.axis_index("expert")
    my_x, my_z = dp // RING, dp % RING
    my_y, my_c = ex // 2, ex % 2

    def at_x(step):
        return (((my_x + step + RING) % RING) * RING + my_z, ex)

    def at_z(step):
        return (my_x * RING + (my_z + step + RING) % RING, ex)

    def expert_at(g):
        return ((my_y + g // 2) % RING) * 2 + (my_c + g % 2) % 2

    def at_group(g):
        return (dp, expert_at(g))

    def back(g):
        return ((RING - g // 2) % RING) * 2 + g % 2

    barrier = pltpu.get_barrier_semaphore()
    partners = [at_x(1), at_x(-1), at_z(1), at_z(-1)] + [at_group(g) for g in range(1, groups)]
    for who in partners:
        pl.semaphore_signal(barrier, inc=1, device_id=who, device_id_type=MESH)

    loads = {}
    for i, (name, src, dst) in enumerate(
        (("tok", tok_ref, tok_v), ("wg", wg_ref, wg_v), ("wu", wu_ref, wu_v), ("wd", wd_ref, wd_v))
    ):
        loads[name] = pltpu.make_async_copy(src, dst, load_sem.at[i])
        loads[name].start()

    def loaded(*names):
        for name in names:
            if name in loads:
                loads.pop(name).wait()

    used = []
    copies = {}

    def remote(key, src, dst, who):
        i = len(used)
        copy = pltpu.make_async_remote_copy(
            src_ref=src, dst_ref=dst, send_sem=send_sem.at[i], recv_sem=recv_sem.at[i],
            device_id=who, device_id_type=MESH,
        )
        used.append(copy)
        copies[key] = copy
        copy.start()

    def need(*keys):
        for key in keys:
            if copies[key] is not None:
                copies[key].wait_recv()
                copies[key] = None

    row_id = lax.broadcasted_iota(jnp.int32, (n_slots, tok_dev), 0)
    lane_id = lax.broadcasted_iota(jnp.int32, (n_slots, tok_dev), 1)
    idx = jnp.full((n_slots, tok_dev), -1, jnp.int32)
    for g in range(groups):
        e = expert_at(g)
        for j in range(slot):
            idx = jnp.where(row_id == g * slot + j, sel_ref[j, e], idx)
    onehot = jnp.where(lane_id == idx, 1.0, 0.0).astype(BF16)
    loaded("tok")
    for c in range(0, width, 1024):
        cols = slice(c, c + 1024)
        slots32[:, cols] = jnp.dot(onehot, tok_v[:, cols], preferred_element_type=F32)
    recv4[0] = slots32[0:slot, :].astype(BF16)
    near = [back(g) for g in HALVES[0] if g > 0]
    far = [back(g) for g in HALVES[1]]
    for g in near + far:
        send4[g] = slots32[g * slot : (g + 1) * slot, :].astype(BF16)
    with jax.named_scope("barrier"):
        pl.semaphore_wait(barrier, len(partners))
    for g in near + far:
        remote(("in", back(g)), send4.at[g], recv4.at[back(g)], at_group(g))

    lane8 = lax.broadcasted_iota(jnp.int32, (8, 128), 1)
    idx_l = jnp.full((8, 128), -1, jnp.int32)
    gate_l = jnp.zeros((8, 128), F32)
    for g in range(groups):
        e = expert_at(g)
        for j in range(slot):
            here = lane8 % n_slots == g * slot + j
            idx_l = jnp.where(here, sel_ref[j, e], idx_l)
            gate_l = jnp.where(here, gate_ref[j, e], gate_l)
    g1 = gate_l.astype(BF16).astype(F32)
    rest = gate_l - g1
    g2 = rest.astype(BF16).astype(F32)
    g3 = (rest - g2).astype(BF16).astype(F32)
    term = lane8 // n_slots
    gate3 = jnp.where(term == 0, g1, jnp.where(term == 1, g2, jnp.where(term == 2, g3, 0.0)))
    tok_id = lax.broadcasted_iota(jnp.int32, (tok_dev, 128), 0)
    hit = tok_id == idx_l[0:1, :]
    comb_ref[...] = jnp.where(hit, gate3[0:1, :], 0.0).astype(BF16)

    def cut(p, lo=0, n=halfw):
        return pl.ds(p * halfw + lo, n)

    def pos(p, d1, d2):
        d1, d2 = d1 % RING, d2 % RING
        return d2 * RING + d1 if p == 0 else d1 * RING + d2

    def first(p, step):
        return at_x(step) if p == 0 else at_z(step)

    def second(p, step):
        return at_z(step) if p == 0 else at_x(step)

    def own(h):
        need(*[("in", g) for g in HALVES[h] if g > 0])
        for i, g in enumerate(HALVES[h]):
            slots32[i * slot : (i + 1) * slot, :] = recv4[g].astype(F32)
        rows[h, 0] = slots32[0:chunk, :].astype(BF16)

    def to_first(key, h, p, d1, step, lo, n):
        remote(
            key, rows.at[h, pos(p, d1, 0), :, cut(p, lo, n)],
            rows.at[h, pos(p, d1 - step, 0), :, cut(p, lo, n)], first(p, step),
        )

    def to_second(key, h, p, d1, d2, step):
        remote(
            key, rows.at[h, pos(p, d1, d2), :, cut(p)],
            rows.at[h, pos(p, d1, d2 - step), :, cut(p)], second(p, step),
        )

    def send_first(h, p, step):
        to_first(("f", h, p, step), h, p, 0, step, 0, halfw)

    def pass_first(h, p, step):
        need(("f", h, p, step))
        to_first(("r", h, p, step), h, p, -step, step, 0 if step == 1 else quart, quart)

    def send_second(h, p, d1, step):
        if d1 == 2:
            need(("r", h, p, 1), ("r", h, p, -1))
        elif d1 != 0:
            need(("f", h, p, 1 if d1 == 3 else -1))
        to_second(("s", h, p, d1, step), h, p, d1, 0, step)

    def pass_second(h, p, d1):
        step = 1 if d1 in RSET else -1
        need(("s", h, p, d1, step))
        to_second(("t", h, p, d1), h, p, d1, -step, step)

    tn = hid.shape[1] // 2

    def up(h, n):
        for p in range(2):
            for d1 in range(RING):
                need(("s", h, p, d1, 1), ("s", h, p, d1, -1), ("t", h, p, d1))
        loaded("wg", "wu")
        lhs = rows[h].reshape(RING * RING * chunk, width)
        cols = slice(n * tn, (n + 1) * tn)
        gate_val = jnp.dot(lhs, wg_v[:, cols], preferred_element_type=F32)
        up_val = jnp.dot(lhs, wu_v[:, cols], preferred_element_type=F32)
        hid[:, cols] = (gate_val / (1.0 + jnp.exp(-gate_val)) * up_val).astype(BF16)

    dn = 512

    def down(h, p, i):
        loaded("wd")
        start = p * halfw + i * subw
        for c in range(start, start + subw, dn):
            cols = slice(c, c + dn)
            val = jnp.dot(hid[...], wd_v[:, cols], preferred_element_type=F32)
            part[h, :, :, cols] = val.astype(BF16).reshape(RING * RING, chunk, dn)

    def sub(i, lo=0, n=subw):
        return pl.ds(i * subw + lo, n)

    def psub(p, i):
        return cut(p, i * subw, subw)

    def send_far(h, p, d1, i):
        step = 1 if d1 in RSET else -1
        remote(
            ("F", h, p, d1, i), part.at[h, pos(p, d1, 2), :, psub(p, i)],
            relay.at[h, p, d1, :, sub(i)], second(p, step),
        )

    def send_left_of(h, p, d1, i):
        remote(
            ("L", h, p, d1, i), part.at[h, pos(p, d1, 1), :, psub(p, i)],
            fin_l.at[h, p, d1, :, sub(i)], second(p, 1),
        )

    def send_right_of(h, p, d1, i):
        remote(
            ("R", h, p, d1, i), part.at[h, pos(p, d1, 3), :, psub(p, i)],
            fin_r.at[h, p, d1, :, sub(i)], second(p, -1),
        )

    def add_far(h, p, d1, i):
        need(("F", h, p, d1, i))
        right = d1 in RSET
        mine = part[h, pos(p, d1, 1 if right else 3), :, psub(p, i)]
        here = relay.at[h, p, d1, :, sub(i)]
        here[...] = (here[...].astype(F32) + mine.astype(F32)).astype(BF16)
        if right:
            remote(("L", h, p, d1, i), here, fin_l.at[h, p, d1, :, sub(i)], second(p, 1))
        else:
            remote(("R", h, p, d1, i), here, fin_r.at[h, p, d1, :, sub(i)], second(p, -1))

    def add_up(h, p, d1, i):
        need(("L", h, p, d1, i), ("R", h, p, d1, i))
        mine = part[h, pos(p, d1, 0), :, psub(p, i)]
        total = (
            mine.astype(F32)
            + fin_l[h, p, d1, :, sub(i)].astype(F32)
            + fin_r[h, p, d1, :, sub(i)].astype(F32)
        )
        summed[h, p, d1, :, sub(i)] = total.astype(BF16)
        lo, hi = sub(i, 0, subw // 2), sub(i, subw // 2, subw // 2)
        if d1 == 2:
            remote(("F1", h, p, 1, i), summed.at[h, p, 2, :, lo], relay1.at[h, p, :, lo], first(p, 1))
            remote(("F1", h, p, -1, i), summed.at[h, p, 2, :, hi], relay1.at[h, p, :, hi], first(p, -1))
        elif d1 == 1:
            remote(("l1", h, p, i), summed.at[h, p, 1, :, hi], fin1_l.at[h, p, :, hi], first(p, 1))
        elif d1 == 3:
            remote(("r1", h, p, i), summed.at[h, p, 3, :, lo], fin1_r.at[h, p, :, lo], first(p, -1))

    def add_first(h, p, step, i):
        need(("F1", h, p, step, i))
        d1 = 1 if step == 1 else 3
        cols = sub(i, 0 if step == 1 else subw // 2, subw // 2)
        here = relay1.at[h, p, :, cols]
        here[...] = (here[...].astype(F32) + summed[h, p, d1, :, cols].astype(F32)).astype(BF16)
        dst = fin1_l if step == 1 else fin1_r
        remote(("b", h, p, step, i), here, dst.at[h, p, :, cols], first(p, step))

    def finish(h, p, i):
        need(("l1", h, p, i), ("r1", h, p, i), ("b", h, p, 1, i), ("b", h, p, -1, i))
        slots32[0:chunk, psub(p, i)] = (
            summed[h, p, 0, :, sub(i)].astype(F32)
            + fin1_l[h, p, :, sub(i)].astype(F32)
            + fin1_r[h, p, :, sub(i)].astype(F32)
        )
        for r, g in enumerate(HALVES[h]):
            value = slots32[r * slot : (r + 1) * slot, psub(p, i)].astype(BF16)
            if g == 0:
                ret4[0, :, psub(p, i)] = value
            else:
                exit4[g, :, psub(p, i)] = value
                remote(
                    ("X", h, p, i, back(g)), exit4.at[g, :, psub(p, i)],
                    ret4.at[back(g), :, psub(p, i)], at_group(g),
                )

    def take(h, p, i):
        for g in HALVES[h]:
            if g > 0:
                need(("X", h, p, i, g))
            slots_ref[g * slot : (g + 1) * slot, psub(p, i)] = ret4[g, :, psub(p, i)].astype(F32)

    steps = {
        "own": own, "f": send_first, "r": pass_first, "s": send_second, "t": pass_second,
        "up": up, "down": down, "F": send_far, "L": send_left_of, "R": send_right_of,
        "A": add_far, "S": add_up, "B": add_first, "Z": finish, "X": take,
    }
    last = max(i for i, entry in enumerate(ORDER) if entry[0] == "Z")
    for at, (name, *args) in enumerate(ORDER):
        with jax.named_scope("_".join(str(a) for a in (name, *args))):
            steps[name](*args)
        if at == last:
            drained = len(used)
            for copy in used[: drained - 24]:
                copy.wait_send()
    for copy in used[drained - 24 :]:
        copy.wait_send()


def combine_kernel(slots_ref, comb_ref, out_ref, out_v, out_sem):
    width = slots_ref.shape[1]
    n = 1024
    stores = []
    for k, c in enumerate(range(0, width, n)):
        value = slots_ref[:, c : c + n].astype(BF16)
        stack = jnp.concatenate([value, value, value, jnp.zeros_like(value)], axis=0)
        out_v[:, c : c + n] = jnp.dot(
            comb_ref[...], stack, preferred_element_type=F32).astype(BF16)
        store = pltpu.make_async_copy(
            out_v.at[:, pl.ds(c, n)], out_ref.at[:, pl.ds(c, n)], out_sem.at[k])
        store.start()
        stores.append(store)
    for store in stores:
        store.wait()


def per_device(tokens, select, gates, w_gate, w_up, w_down):
    tok_dev, width = tokens.shape
    slot = select.shape[1]
    ff = w_gate.shape[2]
    chunk = RING * slot
    halfw = width // 2
    vmem, hbm = pl.BlockSpec(memory_space=pltpu.VMEM), pl.BlockSpec(memory_space=pltpu.HBM)
    smem = pl.BlockSpec(memory_space=pltpu.SMEM)
    slots, comb = pl.pallas_call(
        kernel,
        out_shape=(pltpu.VMEM((8 * slot, width), F32), pltpu.VMEM((tok_dev, 128), BF16)),
        in_specs=[smem, smem, hbm, hbm, hbm, hbm],
        out_specs=(vmem, vmem),
        scratch_shapes=[
            pltpu.VMEM((tok_dev, width), BF16),
            pltpu.VMEM((width, ff), BF16),
            pltpu.VMEM((width, ff), BF16),
            pltpu.VMEM((ff, width), BF16),
            pltpu.VMEM((8, slot, width), BF16),
            pltpu.VMEM((8, slot, width), BF16),
            pltpu.VMEM((8, slot, width), BF16),
            pltpu.VMEM((8, slot, width), BF16),
            pltpu.VMEM((2, 16, chunk, width), BF16),
            pltpu.VMEM((2, 16, chunk, width), BF16),
            pltpu.VMEM((16 * chunk, ff), BF16),
            pltpu.VMEM((2, 2, 4, chunk, halfw), BF16),
            pltpu.VMEM((2, 2, 4, chunk, halfw), BF16),
            pltpu.VMEM((2, 2, 4, chunk, halfw), BF16),
            pltpu.VMEM((2, 2, 4, chunk, halfw), BF16),
            pltpu.VMEM((2, 2, chunk, halfw), BF16),
            pltpu.VMEM((2, 2, chunk, halfw), BF16),
            pltpu.VMEM((2, 2, chunk, halfw), BF16),
            pltpu.VMEM((8 * slot, width), F32),
            pltpu.SemaphoreType.DMA((N_SEM,)),
            pltpu.SemaphoreType.DMA((N_SEM,)),
            pltpu.SemaphoreType.DMA((4,)),
        ],
        compiler_params=pltpu.CompilerParams(
            collective_id=0, has_side_effects=True, vmem_limit_bytes=56 * 1024 * 1024
        ),
        name="moe",
    )(
        select.T, gates.T, tokens, w_gate[0], w_up[0], w_down[0],
    )
    return pl.pallas_call(
        combine_kernel,
        out_shape=jax.ShapeDtypeStruct((tok_dev, width), BF16),
        in_specs=[vmem, vmem],
        out_specs=hbm,
        scratch_shapes=[pltpu.VMEM((tok_dev, width), BF16), pltpu.SemaphoreType.DMA((4,))],
        compiler_params=pltpu.CompilerParams(vmem_limit_bytes=8 * 1024 * 1024),
        name="combine",
    )(slots, comb)


def solution(mesh):
    return jax.shard_map(
        per_device,
        mesh=mesh,
        in_specs=(
            P(("dp", "expert"), None),
            P(None, ("dp", "expert")),
            P(None, ("dp", "expert")),
            P("expert", None, "dp"),
            P("expert", None, "dp"),
            P("expert", "dp", None),
        ),
        out_specs=P(("dp", "expert"), None),
        check_vma=False,
    )
```

time: 170 us -> 73.3 us (0.43)
  Pallas kernels: 0 us -> 73.2 us
  blocking collectives: 66.7 us -> 0 us
  waiting for transfers between devices: 58.4 us -> 0 us
  between operations: 13.5 us -> 0.01 us
  matrix products: 12.7 us -> 0 us
  other arithmetic: 6.98 us -> 0 us
  starting transfers between devices: 6.45 us -> 0 us
  local copies, waits for them, and re-layouts: 4.44 us -> 0 us
    pallas_call x0 -> x2, Pallas kernels: none -> 73.2 us  [the longest x1 72 us: per_device(): pl.pallas_call(kernel, out_shape=(pltpu.VMEM((8 * slot, width), F32), plt...]
    all_to_all x2 -> x0, blocking collectives: 66.7 us -> none  [the longest x1 54.5 us: summed_on_arrival(): lax.all_to_all(parts, axis, split_axis=0, concat_axis=0, tiled=True)]
    all_gather x1 -> x0, waiting for transfers between devices: 52.2 us -> none  [per_device(): lax.all_gather(arrived, 'dp', axis=1, tiled=True)]
    dot_general x4 -> x0, matrix products: 12.7 us -> none  [the longest x1 5.92 us: expert_ffn(): jnp.einsum('erd,edf->erf', block_rows, w_gate, preferred_element_type=jnp...]
    all_to_all x1 -> x0, starting transfers between devices: 6.45 us -> none  [per_device(): lax.all_to_all(summed.astype(jnp.bfloat16), 'expert', split_axis=1, conca...]
    all_to_all x1 -> x0, waiting for transfers between devices: 6.23 us -> none  [per_device(): lax.all_to_all(summed.astype(jnp.bfloat16), 'expert', split_axis=1, conca...]
    reduce_sum x1 -> x0, other arithmetic: 2.98 us -> none  [summed_on_arrival(): return arrived.astype(jnp.float32).sum(axis=0)]
    unnamed x1 -> x0, other arithmetic: 2.25 us -> none
  transfers between devices with their start and end apart: 2 -> 0, of which waited for: 2 -> 0; matrix products, arithmetic and copies ran while one was open for 0% -> 0% of each run, Pallas kernels for 0% -> 0%
where the time goes in v3:
time: 73.3 us; the launch traced here: 73.2 us
  Pallas kernels  73.2 us (100%)
    pallas_call x1, Pallas kernels, per_device(): pl.pallas_call(kernel, out_shape=(pltpu.VMEM((8 * slot, width), F32), plt...  72 us

profile of v3, /device:TPU:1, one launch (start us, length us, event | category | flops | bytes accessed | tf_op | source)
XLA Modules:
  0.0 73.2 jit_solution(11329108521838325754)
XLA Ops:
  0.0 72.0 %moe.1 = (f32[32,4096]{1,0:T(8,128)S(1)}, bf16[128,128]{1,0:T(8,128)(2,1)S(1)}) custom-call(s32[4,8]{1,0:T(4,128)} %bitcast.8, f32[4,8]{1,0:T(4,128)} %bitcast.9, bf16[128,4096]{1,0:T(8,128)(2,1)} %tok_ref.1, bf16[4096,512]{1,0:T(8,128)(2,1)} %bitcast.5, bf16[4096,512]{1,0:T(8,128)(2,1)} %bitcast.6, bf16[512,4096]{1,0:T(8,128)(2,1)} %bitcast.7), custom_call_target="tpu_custom_call" | custom-call | tf_op jit(solution)/shard_map/moe/pallas_call | solution.py:373
  72.0 1.2 %combine.1 = bf16[128,4096]{1,0:T(8,128)(2,1)} custom-call(f32[32,4096]{1,0:T(8,128)S(1)} %get-tuple-element.7.slots_ref, bf16[128,128]{1,0:T(8,128)(2,1)S(1)} %get-tuple-element.8.comb_ref), custom_call_target="tpu_custom_call" | custom-call | tf_op jit(solution)/shard_map/combine/pallas_call | solution.py:409

commit v4 on v3

--- a/solution.py
+++ b/solution.py
@@ -9,7 +9,7 @@
 BF16, F32 = jnp.bfloat16, jnp.float32
 RING = 4
 SUB = 2
-N_SEM = 320
+N_RECV = 128
 RSET, LSET = (0, 3), (2, 1)
 HALVES = ((0, 1, 2, 6), (3, 7, 4, 5))
 
@@ -108,24 +108,65 @@
             if name in loads:
                 loads.pop(name).wait()
 
-    used = []
-    copies = {}
+    recv_of, recv_bytes, send_bytes = {}, {}, {}
+
+    def together(key):
+        kind, h = key[0], key[1]
+        if kind == "in":
+            return ("own", 0 if h in HALVES[0] else 1)
+        if kind == "r":
+            return key[:3]
+        if kind == "t" or (kind == "s" and key[4] != (1 if key[3] in RSET else -1)):
+            return ("up", h)
+        if kind in ("L", "R"):
+            return ("S", *key[1:])
+        if kind in ("l1", "r1"):
+            return ("Z", *key[1:])
+        if kind == "b":
+            return ("Z", h, key[2], key[4])
+        return key[:4] if kind == "X" else key
+
+    def outbox(key):
+        kind, h = key[0], key[1]
+        if kind == "in":
+            return 0
+        return (1 if kind in "fsrt" else 3 if kind != "X" else 5) + h
+
+    def size(ref):
+        n = 2
+        for dim in ref.shape:
+            n *= dim
+        return n
+
+    def wait_for(sem, n):
+        row = 2 * chunk * width
+        if n % row == 0:
+            ref = rows.at[0, pl.ds(0, n // row)]
+        elif n % (row // 4) == 0:
+            ref = exit4.at[pl.ds(0, 4 * n // row)]
+        else:
+            ref = exit4.at[pl.ds(0, 16 * n // row), :, pl.ds(0, width // 4)]
+        assert size(ref) == n
+        pltpu.make_async_copy(ref, ref, sem).wait()
 
     def remote(key, src, dst, who):
-        i = len(used)
-        copy = pltpu.make_async_remote_copy(
-            src_ref=src, dst_ref=dst, send_sem=send_sem.at[i], recv_sem=recv_sem.at[i],
+        name, box = together(key), outbox(key)
+        i = recv_of.setdefault(name, len(recv_of))
+        recv_bytes[name] = recv_bytes.get(name, 0) + size(dst)
+        send_bytes[box] = send_bytes.get(box, 0) + size(src)
+        pltpu.make_async_remote_copy(
+            src_ref=src, dst_ref=dst, send_sem=send_sem.at[box], recv_sem=recv_sem.at[i],
             device_id=who, device_id_type=MESH,
-        )
-        used.append(copy)
-        copies[key] = copy
-        copy.start()
-
-    def need(*keys):
-        for key in keys:
-            if copies[key] is not None:
-                copies[key].wait_recv()
-                copies[key] = None
+        ).start()
+
+    def need(*names):
+        for name in names:
+            if name in recv_bytes:
+                wait_for(recv_sem.at[recv_of[name]], recv_bytes.pop(name))
+
+    def drain(*boxes):
+        for box in boxes:
+            wait_for(send_sem.at[box], send_bytes.pop(box))
 
     row_id = lax.broadcasted_iota(jnp.int32, (n_slots, tok_dev), 0)
     lane_id = lax.broadcasted_iota(jnp.int32, (n_slots, tok_dev), 1)
@@ -182,7 +223,7 @@
         return at_z(step) if p == 0 else at_x(step)
 
     def own(h):
-        need(*[("in", g) for g in HALVES[h] if g > 0])
+        need(("own", h))
         for i, g in enumerate(HALVES[h]):
             slots32[i * slot : (i + 1) * slot, :] = recv4[g].astype(F32)
         rows[h, 0] = slots32[0:chunk, :].astype(BF16)
@@ -208,7 +249,7 @@
 
     def send_second(h, p, d1, step):
         if d1 == 2:
-            need(("r", h, p, 1), ("r", h, p, -1))
+            need(("r", h, p))
         elif d1 != 0:
             need(("f", h, p, 1 if d1 == 3 else -1))
         to_second(("s", h, p, d1, step), h, p, d1, 0, step)
@@ -221,9 +262,7 @@
     tn = hid.shape[1] // 2
 
     def up(h, n):
-        for p in range(2):
-            for d1 in range(RING):
-                need(("s", h, p, d1, 1), ("s", h, p, d1, -1), ("t", h, p, d1))
+        need(("up", h))
         loaded("wg", "wu")
         lhs = rows[h].reshape(RING * RING * chunk, width)
         cols = slice(n * tn, (n + 1) * tn)
@@ -278,7 +317,7 @@
             remote(("R", h, p, d1, i), here, fin_r.at[h, p, d1, :, sub(i)], second(p, -1))
 
     def add_up(h, p, d1, i):
-        need(("L", h, p, d1, i), ("R", h, p, d1, i))
+        need(("S", h, p, d1, i))
         mine = part[h, pos(p, d1, 0), :, psub(p, i)]
         total = (
             mine.astype(F32)
@@ -305,7 +344,7 @@
         remote(("b", h, p, step, i), here, dst.at[h, p, :, cols], first(p, step))
 
     def finish(h, p, i):
-        need(("l1", h, p, i), ("r1", h, p, i), ("b", h, p, 1, i), ("b", h, p, -1, i))
+        need(("Z", h, p, i))
         slots32[0:chunk, psub(p, i)] = (
             summed[h, p, 0, :, sub(i)].astype(F32)
             + fin1_l[h, p, :, sub(i)].astype(F32)
@@ -323,9 +362,8 @@
                 )
 
     def take(h, p, i):
+        need(("X", h, p, i))
         for g in HALVES[h]:
-            if g > 0:
-                need(("X", h, p, i, g))
             slots_ref[g * slot : (g + 1) * slot, psub(p, i)] = ret4[g, :, psub(p, i)].astype(F32)
 
     steps = {
@@ -333,16 +371,15 @@
         "up": up, "down": down, "F": send_far, "L": send_left_of, "R": send_right_of,
         "A": add_far, "S": add_up, "B": add_first, "Z": finish, "X": take,
     }
-    last = max(i for i, entry in enumerate(ORDER) if entry[0] == "Z")
+    ends = [i for i, entry in enumerate(ORDER) if entry[0] == "Z"]
     for at, (name, *args) in enumerate(ORDER):
         with jax.named_scope("_".join(str(a) for a in (name, *args))):
             steps[name](*args)
-        if at == last:
-            drained = len(used)
-            for copy in used[: drained - 24]:
-                copy.wait_send()
-    for copy in used[drained - 24 :]:
-        copy.wait_send()
+        if at == ends[-1]:
+            with jax.named_scope("drain"):
+                drain(0, 1, 2, 3, 4, 5)
+    with jax.named_scope("last_sends"):
+        drain(6)
 
 
 def combine_kernel(slots_ref, comb_ref, out_ref, out_v, out_sem):
@@ -395,8 +432,8 @@
             pltpu.VMEM((2, 2, chunk, halfw), BF16),
             pltpu.VMEM((2, 2, chunk, halfw), BF16),
             pltpu.VMEM((8 * slot, width), F32),
-            pltpu.SemaphoreType.DMA((N_SEM,)),
-            pltpu.SemaphoreType.DMA((N_SEM,)),
+            pltpu.SemaphoreType.DMA((7,)),
+            pltpu.SemaphoreType.DMA((N_RECV,)),
             pltpu.SemaphoreType.DMA((4,)),
         ],
         compiler_params=pltpu.CompilerParams(

time: 73.3 us -> 68.7 us (0.937)
  Pallas kernels: 73.2 us -> 68.6 us
    pallas_call x1, Pallas kernels: 72 us -> 67.4 us  [per_device(): pl.pallas_call(kernel, out_shape=(pltpu.VMEM((8 * slot, width), F32), plt...]
where the time goes in v4:
time: 68.7 us; the launch traced here: 68.6 us
  Pallas kernels  68.6 us (100%)
    pallas_call x1, Pallas kernels, per_device(): pl.pallas_call(kernel, out_shape=(pltpu.VMEM((8 * slot, width), F32), plt...  67.4 us

profile of v4, /device:TPU:1, one launch (start us, length us, event | category | flops | bytes accessed | tf_op | source)
XLA Modules:
  0.0 68.6 jit_solution(13192791797245463668)
XLA Ops:
  0.0 67.4 %moe.1 = (f32[32,4096]{1,0:T(8,128)S(1)}, bf16[128,128]{1,0:T(8,128)(2,1)S(1)}) custom-call(s32[4,8]{1,0:T(4,128)} %bitcast.8, f32[4,8]{1,0:T(4,128)} %bitcast.9, bf16[128,4096]{1,0:T(8,128)(2,1)} %tok_ref.1, bf16[4096,512]{1,0:T(8,128)(2,1)} %bitcast.5, bf16[4096,512]{1,0:T(8,128)(2,1)} %bitcast.6, bf16[512,4096]{1,0:T(8,128)(2,1)} %bitcast.7), custom_call_target="tpu_custom_call" | custom-call | tf_op jit(solution)/shard_map/moe/pallas_call | solution.py:410
  67.4 1.2 %combine.1 = bf16[128,4096]{1,0:T(8,128)(2,1)} custom-call(f32[32,4096]{1,0:T(8,128)S(1)} %get-tuple-element.7.slots_ref, bf16[128,128]{1,0:T(8,128)(2,1)S(1)} %get-tuple-element.8.comb_ref), custom_call_target="tpu_custom_call" | custom-call | tf_op jit(solution)/shard_map/combine/pallas_call | solution.py:446

commit v5 on v4

--- a/solution.py
+++ b/solution.py
@@ -9,60 +9,66 @@
 BF16, F32 = jnp.bfloat16, jnp.float32
 RING = 4
 SUB = 2
-N_RECV = 128
+N_RECV = 130
 RSET, LSET = (0, 3), (2, 1)
+EARLY = tuple((z, x) for z in (0, 1, 3) for x in (0, 1, 3))
+LATE = tuple((z, x) for z in range(RING) for x in range(RING) if 2 in (z, x))
+PLACE = {at: i for i, at in enumerate(EARLY + LATE)}
 HALVES = ((0, 1, 2, 6), (3, 7, 4, 5))
 
 ORDER = (
-    ("own", 0), ("f", 0, 0, -1), ("f", 0, 1, -1), ("f", 0, 0, 1), ("f", 0, 1, 1), ("s", 0, 1, 0, 1),
-    ("s", 0, 1, 0, -1), ("s", 0, 0, 0, -1), ("s", 0, 0, 0, 1), ("own", 1), ("s", 1, 1, 0, 1), ("f", 1, 1, -1),
-    ("f", 1, 0, 1), ("s", 1, 0, 0, 1), ("f", 1, 0, -1), ("s", 1, 1, 0, -1), ("f", 1, 1, 1), ("s", 1, 0, 0, -1),
-    ("r", 0, 0, -1), ("s", 0, 1, 1, -1), ("r", 0, 1, -1), ("r", 0, 0, 1), ("r", 0, 1, 1), ("s", 0, 1, 3, 1),
-    ("s", 0, 1, 3, -1), ("s", 0, 0, 1, 1), ("s", 0, 1, 1, 1), ("s", 0, 0, 3, -1), ("s", 0, 0, 3, 1),
-    ("s", 0, 0, 1, -1), ("t", 0, 1, 0), ("t", 0, 0, 0), ("r", 1, 0, -1), ("r", 1, 1, -1), ("s", 1, 1, 1, -1),
-    ("t", 1, 1, 0), ("s", 1, 1, 1, 1), ("t", 1, 0, 0), ("s", 1, 0, 1, -1), ("s", 1, 0, 1, 1), ("s", 1, 0, 3, 1),
-    ("s", 1, 1, 3, 1), ("r", 1, 1, 1), ("s", 1, 0, 3, -1), ("r", 1, 0, 1), ("s", 1, 1, 3, -1), ("s", 0, 0, 2, -1),
-    ("s", 0, 0, 2, 1), ("s", 0, 1, 2, 1), ("s", 0, 1, 2, -1), ("t", 0, 1, 1), ("t", 0, 1, 3), ("t", 0, 0, 1),
-    ("t", 0, 0, 3), ("t", 1, 1, 1), ("t", 1, 0, 1), ("t", 0, 1, 2), ("t", 0, 0, 2), ("t", 1, 1, 3), ("t", 1, 0, 3),
-    ("s", 1, 0, 2, 1), ("s", 1, 1, 2, -1), ("s", 1, 0, 2, -1), ("s", 1, 1, 2, 1), ("up", 0, 0), ("up", 0, 1),
-    ("t", 1, 1, 2), ("t", 1, 0, 2), ("down", 0, 0, 1), ("L", 0, 0, 2, 1), ("F", 0, 0, 0, 1), ("F", 0, 0, 3, 1),
-    ("down", 0, 0, 0), ("F", 0, 0, 1, 0), ("F", 0, 0, 2, 0), ("R", 0, 0, 3, 1), ("L", 0, 0, 1, 1), ("R", 0, 0, 3, 0),
-    ("F", 0, 0, 3, 0), ("R", 0, 0, 0, 1), ("down", 0, 1, 0), ("F", 0, 1, 2, 0), ("L", 0, 1, 1, 0), ("L", 0, 1, 2, 0),
-    ("F", 0, 1, 1, 0), ("F", 0, 1, 3, 0), ("R", 0, 1, 0, 0), ("F", 0, 0, 2, 1), ("F", 0, 0, 1, 1), ("F", 0, 1, 0, 0),
-    ("R", 0, 1, 3, 0), ("down", 0, 1, 1), ("F", 0, 1, 2, 1), ("R", 0, 1, 3, 1), ("L", 0, 1, 2, 1), ("L", 0, 1, 1, 1),
-    ("F", 0, 1, 1, 1), ("F", 0, 1, 0, 1), ("L", 0, 0, 1, 0), ("R", 0, 1, 0, 1), ("L", 0, 0, 2, 0), ("F", 0, 0, 0, 0),
-    ("F", 0, 1, 3, 1), ("R", 0, 0, 0, 0), ("up", 1, 0), ("A", 0, 0, 1, 0), ("up", 1, 1), ("down", 1, 1, 0),
-    ("R", 1, 1, 3, 0), ("F", 1, 1, 3, 0), ("F", 1, 1, 0, 0), ("F", 1, 1, 2, 0), ("down", 1, 0, 1), ("F", 1, 0, 2, 1),
-    ("R", 1, 0, 0, 1), ("F", 1, 0, 3, 1), ("L", 1, 0, 2, 1), ("down", 1, 0, 0), ("L", 1, 0, 2, 0), ("F", 1, 0, 3, 0),
-    ("R", 1, 0, 3, 0), ("A", 0, 1, 2, 1), ("R", 1, 0, 0, 0), ("A", 0, 1, 1, 0), ("F", 1, 0, 2, 0), ("L", 1, 1, 2, 0),
-    ("L", 1, 1, 1, 0), ("down", 1, 1, 1), ("A", 0, 0, 2, 1), ("L", 1, 1, 2, 1), ("F", 1, 1, 2, 1), ("F", 1, 1, 3, 1),
-    ("L", 1, 1, 1, 1), ("A", 0, 0, 3, 1), ("R", 1, 1, 3, 1), ("F", 1, 1, 1, 0), ("R", 1, 0, 3, 1), ("F", 1, 0, 0, 1),
-    ("A", 0, 0, 2, 0), ("L", 1, 0, 1, 0), ("F", 1, 0, 1, 0), ("F", 1, 1, 1, 1), ("A", 0, 1, 2, 0), ("L", 1, 0, 1, 1),
-    ("F", 1, 1, 0, 1), ("F", 1, 0, 0, 0), ("F", 1, 0, 1, 1), ("R", 1, 1, 0, 1), ("R", 1, 1, 0, 0), ("A", 0, 1, 0, 0),
-    ("A", 0, 0, 3, 0), ("A", 0, 0, 0, 0), ("A", 0, 0, 0, 1), ("A", 0, 1, 3, 0), ("A", 0, 1, 0, 1), ("A", 0, 1, 1, 1),
-    ("A", 0, 0, 1, 1), ("A", 0, 1, 3, 1), ("A", 1, 1, 3, 0), ("S", 0, 0, 1, 0), ("A", 1, 0, 3, 1), ("A", 1, 1, 0, 0),
-    ("A", 1, 1, 2, 0), ("A", 1, 0, 2, 1), ("S", 0, 1, 2, 1), ("S", 0, 1, 1, 0), ("A", 1, 0, 3, 0), ("A", 1, 1, 2, 1),
-    ("S", 0, 0, 3, 1), ("A", 1, 1, 3, 1), ("A", 1, 0, 2, 0), ("A", 1, 0, 0, 1), ("A", 1, 1, 1, 0), ("S", 0, 0, 2, 1),
-    ("A", 1, 1, 0, 1), ("A", 1, 1, 1, 1), ("S", 0, 1, 0, 0), ("S", 0, 1, 2, 0), ("S", 0, 0, 2, 0), ("A", 1, 0, 0, 0),
-    ("S", 0, 1, 3, 0), ("A", 1, 0, 1, 0), ("S", 0, 0, 3, 0), ("S", 0, 1, 0, 1), ("A", 1, 0, 1, 1), ("S", 0, 0, 0, 0),
-    ("S", 0, 1, 3, 1), ("S", 0, 1, 1, 1), ("S", 0, 0, 1, 1), ("S", 0, 0, 0, 1), ("S", 1, 1, 3, 0), ("S", 1, 1, 2, 0),
-    ("S", 1, 0, 2, 1), ("S", 1, 0, 3, 1), ("B", 0, 1, -1, 1), ("B", 0, 1, 1, 1), ("S", 1, 1, 2, 1), ("S", 1, 1, 0, 0),
-    ("S", 1, 0, 2, 0), ("B", 0, 1, -1, 0), ("S", 1, 0, 3, 0), ("S", 1, 1, 3, 1), ("S", 1, 1, 1, 0), ("B", 0, 0, 1, 1),
-    ("B", 0, 0, -1, 1), ("S", 1, 0, 0, 1), ("S", 1, 0, 1, 0), ("B", 0, 1, 1, 0), ("S", 1, 1, 0, 1), ("S", 1, 1, 1, 1),
-    ("B", 0, 0, 1, 0), ("B", 0, 0, -1, 0), ("S", 1, 0, 1, 1), ("S", 1, 0, 0, 0), ("B", 1, 0, 1, 1),
-    ("B", 1, 0, -1, 1), ("B", 1, 1, 1, 0), ("B", 1, 0, 1, 0), ("B", 1, 1, -1, 0), ("B", 1, 0, -1, 0), ("Z", 0, 1, 1),
-    ("B", 1, 1, 1, 1), ("B", 1, 1, -1, 1), ("Z", 0, 0, 1), ("Z", 0, 1, 0), ("Z", 0, 0, 0), ("Z", 1, 0, 1),
-    ("Z", 1, 1, 0), ("Z", 1, 0, 0), ("X", 0, 1, 1), ("Z", 1, 1, 1), ("X", 0, 0, 1), ("X", 0, 1, 0), ("X", 0, 0, 0),
-    ("X", 1, 0, 1), ("X", 1, 1, 0), ("X", 1, 0, 0), ("X", 1, 1, 1),
+    ("own", 0), ("s", 0, 1, 0, -1), ("s", 0, 0, 0, -1), ("f", 0, 0, -1), ("s", 0, 0, 0, 1), ("f", 0, 0, 1),
+    ("f", 0, 1, -1), ("s", 0, 1, 0, 1), ("f", 0, 1, 1), ("own", 1), ("f", 1, 1, -1), ("s", 1, 0, 0, 1),
+    ("s", 1, 1, 0, -1), ("f", 1, 1, 1), ("s", 1, 0, 0, -1), ("f", 1, 0, -1), ("s", 1, 1, 0, 1), ("f", 1, 0, 1),
+    ("t", 0, 0, 0), ("s", 0, 0, 3, -1), ("r", 0, 0, 1), ("s", 0, 0, 3, 1), ("s", 0, 0, 1, 1), ("s", 0, 0, 1, -1),
+    ("s", 0, 1, 1, -1), ("r", 0, 0, -1), ("s", 0, 1, 3, 1), ("s", 0, 1, 3, -1), ("s", 0, 1, 1, 1), ("r", 0, 1, -1),
+    ("t", 0, 1, 0), ("r", 0, 1, 1), ("r", 1, 1, -1), ("s", 1, 1, 1, -1), ("s", 1, 1, 1, 1), ("t", 1, 0, 0),
+    ("t", 1, 1, 0), ("s", 1, 0, 1, -1), ("s", 1, 0, 1, 1), ("r", 1, 0, -1), ("s", 1, 1, 3, -1), ("s", 1, 0, 3, 1),
+    ("s", 1, 0, 3, -1), ("r", 1, 0, 1), ("r", 1, 1, 1), ("s", 1, 1, 3, 1), ("t", 0, 1, 1), ("s", 0, 0, 2, 1),
+    ("s", 0, 0, 2, -1), ("t", 0, 1, 3), ("t", 0, 0, 1), ("t", 0, 0, 3), ("up", 0, 0, 0), ("s", 0, 1, 2, -1),
+    ("up", 0, 0, 1), ("t", 1, 0, 1), ("s", 0, 1, 2, 1), ("t", 1, 1, 1), ("down", 0, 0, 0, 1), ("L", 0, 0, 1, 1),
+    ("down", 0, 0, 1, 1), ("L", 0, 1, 1, 1), ("R", 0, 1, 0, 1), ("R", 0, 1, 3, 1), ("R", 0, 0, 0, 1),
+    ("R", 0, 0, 3, 1), ("down", 0, 0, 1, 0), ("R", 0, 1, 0, 0), ("R", 0, 1, 3, 0), ("L", 0, 1, 1, 0),
+    ("down", 0, 0, 0, 0), ("R", 0, 0, 3, 0), ("L", 0, 0, 1, 0), ("R", 0, 0, 0, 0), ("t", 0, 0, 2), ("s", 1, 0, 2, 1),
+    ("s", 1, 0, 2, -1), ("t", 1, 0, 3), ("t", 0, 1, 2), ("s", 1, 1, 2, 1), ("s", 1, 1, 2, -1), ("up", 1, 0, 0),
+    ("up", 1, 0, 1), ("down", 1, 0, 0, 0), ("R", 1, 0, 0, 0), ("R", 1, 0, 3, 0), ("down", 1, 0, 1, 1),
+    ("R", 1, 1, 0, 1), ("L", 1, 1, 1, 1), ("L", 1, 0, 1, 0), ("down", 1, 0, 1, 0), ("L", 1, 1, 1, 0),
+    ("R", 1, 1, 0, 0), ("R", 1, 1, 3, 1), ("R", 1, 1, 3, 0), ("t", 1, 1, 3), ("down", 1, 0, 0, 1), ("R", 1, 0, 3, 1),
+    ("R", 1, 0, 0, 1), ("L", 1, 0, 1, 1), ("up", 0, 1, 0), ("up", 0, 1, 1), ("down", 0, 1, 0, 0), ("F", 0, 0, 0, 0),
+    ("t", 1, 0, 2), ("t", 1, 1, 2), ("F", 0, 0, 2, 0), ("down", 0, 1, 0, 1), ("F", 0, 0, 3, 1), ("L", 0, 0, 2, 1),
+    ("F", 0, 0, 2, 1), ("down", 0, 1, 1, 0), ("F", 0, 1, 2, 0), ("F", 0, 1, 3, 0), ("L", 0, 1, 2, 0),
+    ("F", 0, 1, 1, 0), ("F", 0, 1, 0, 0), ("L", 0, 0, 2, 0), ("F", 0, 0, 0, 1), ("F", 0, 0, 1, 0), ("F", 0, 0, 3, 0),
+    ("down", 0, 1, 1, 1), ("F", 0, 1, 0, 1), ("F", 0, 1, 2, 1), ("F", 0, 1, 3, 1), ("L", 0, 1, 2, 1),
+    ("F", 0, 1, 1, 1), ("F", 0, 0, 1, 1), ("A", 0, 0, 0, 0), ("A", 0, 1, 3, 0), ("A", 0, 0, 3, 1), ("up", 1, 1, 0),
+    ("up", 1, 1, 1), ("down", 1, 1, 1, 0), ("A", 0, 0, 2, 1), ("F", 1, 1, 0, 0), ("F", 1, 1, 1, 0), ("L", 1, 1, 2, 0),
+    ("down", 1, 1, 0, 0), ("F", 1, 0, 0, 0), ("F", 1, 0, 2, 0), ("down", 1, 1, 1, 1), ("F", 1, 1, 0, 1),
+    ("L", 1, 1, 2, 1), ("L", 1, 0, 2, 0), ("F", 1, 1, 3, 1), ("A", 0, 1, 1, 0), ("A", 0, 0, 1, 0), ("A", 0, 1, 2, 1),
+    ("F", 1, 1, 2, 0), ("A", 0, 0, 0, 1), ("F", 1, 1, 2, 1), ("F", 1, 0, 1, 0), ("F", 1, 0, 3, 0), ("F", 1, 1, 3, 0),
+    ("A", 0, 1, 3, 1), ("A", 0, 1, 0, 0), ("down", 1, 1, 0, 1), ("F", 1, 0, 2, 1), ("F", 1, 0, 0, 1),
+    ("F", 1, 0, 1, 1), ("L", 1, 0, 2, 1), ("F", 1, 0, 3, 1), ("A", 0, 1, 2, 0), ("F", 1, 1, 1, 1), ("A", 0, 0, 2, 0),
+    ("A", 0, 0, 3, 0), ("A", 0, 1, 0, 1), ("A", 0, 1, 1, 1), ("A", 0, 0, 1, 1), ("S", 0, 0, 0, 0), ("S", 0, 1, 3, 0),
+    ("S", 0, 0, 3, 1), ("S", 0, 0, 2, 1), ("A", 1, 1, 0, 0), ("A", 1, 1, 1, 0), ("A", 1, 0, 0, 0), ("A", 1, 0, 2, 0),
+    ("S", 0, 1, 1, 0), ("S", 0, 0, 1, 0), ("S", 0, 1, 2, 1), ("A", 1, 1, 0, 1), ("S", 0, 0, 0, 1), ("A", 1, 0, 1, 0),
+    ("A", 1, 1, 2, 0), ("A", 1, 0, 3, 0), ("A", 1, 0, 2, 1), ("A", 1, 1, 3, 1), ("A", 1, 1, 2, 1), ("A", 1, 0, 0, 1),
+    ("A", 1, 0, 1, 1), ("A", 1, 1, 3, 0), ("S", 0, 1, 2, 0), ("S", 0, 0, 2, 0), ("S", 0, 1, 3, 1), ("A", 1, 1, 1, 1),
+    ("A", 1, 0, 3, 1), ("S", 0, 0, 1, 1), ("S", 0, 1, 1, 1), ("S", 0, 1, 0, 0), ("S", 0, 0, 3, 0), ("S", 0, 1, 0, 1),
+    ("B", 0, 0, -1, 1), ("S", 1, 0, 0, 0), ("S", 1, 0, 2, 0), ("B", 0, 0, 1, 1), ("B", 0, 1, -1, 1),
+    ("S", 1, 1, 1, 0), ("B", 0, 1, 1, 1), ("S", 1, 1, 0, 0), ("S", 1, 0, 1, 0), ("S", 1, 1, 2, 0), ("S", 1, 0, 3, 0),
+    ("S", 1, 0, 2, 1), ("S", 1, 1, 2, 1), ("S", 1, 1, 0, 1), ("S", 1, 0, 0, 1), ("B", 0, 0, -1, 0), ("B", 0, 1, 1, 0),
+    ("S", 1, 0, 1, 1), ("S", 1, 1, 3, 1), ("B", 0, 1, -1, 0), ("S", 1, 1, 1, 1), ("S", 1, 0, 3, 1), ("S", 1, 1, 3, 0),
+    ("B", 0, 0, 1, 0), ("B", 1, 1, -1, 0), ("B", 1, 0, -1, 0), ("Z", 0, 1, 1), ("B", 1, 0, 1, 0), ("B", 1, 1, 1, 0),
+    ("B", 1, 1, -1, 1), ("Z", 0, 0, 1), ("B", 1, 0, -1, 1), ("B", 1, 1, 1, 1), ("B", 1, 0, 1, 1), ("Z", 0, 1, 0),
+    ("Z", 0, 0, 0), ("Z", 1, 0, 0), ("Z", 1, 1, 0), ("Z", 1, 1, 1), ("Z", 1, 0, 1), ("X", 0, 1, 1), ("X", 0, 0, 1),
+    ("X", 0, 1, 0), ("X", 0, 0, 0), ("X", 1, 0, 0), ("X", 1, 1, 0), ("X", 1, 1, 1), ("X", 1, 0, 1),
 )
 
 
 def kernel(
-    sel_ref, gate_ref, tok_ref, wg_ref, wu_ref, wd_ref, slots_ref, comb_ref,
-    tok_v, wg_v, wu_v, wd_v, send4, recv4, exit4, ret4, rows, part, hid, relay, fin_l, fin_r, summed,
+    sel_hbm, gate_hbm, tok_ref, wg_ref, wu_ref, wd_ref, slots_ref, comb_ref,
+    sel_ref, gate_ref, tok_v, wg_v, wu_v, wd_v, send4, recv4, exit4, ret4, rows, part, hid, relay, fin_l, fin_r, summed,
     relay1, fin1_l, fin1_r, slots32, send_sem, recv_sem, load_sem,
 ):
-    slot = sel_ref.shape[0]
+    slot = sel_hbm.shape[0]
     tok_dev, width = tok_ref.shape
     groups = 2 * RING
     n_slots = groups * slot
@@ -97,11 +103,21 @@
         pl.semaphore_signal(barrier, inc=1, device_id=who, device_id_type=MESH)
 
     loads = {}
+    loads["sel"] = pltpu.make_async_copy(sel_hbm, sel_ref, load_sem.at[7])
+    loads["gate"] = pltpu.make_async_copy(gate_hbm, gate_ref, load_sem.at[8])
+    loads["sel"].start()
+    tokw = width // 4
+    for i in range(4):
+        cols = pl.ds(i * tokw, tokw)
+        loads[i] = pltpu.make_async_copy(tok_ref.at[:, cols], tok_v.at[:, cols], load_sem.at[i])
+        loads[i].start()
     for i, (name, src, dst) in enumerate(
-        (("tok", tok_ref, tok_v), ("wg", wg_ref, wg_v), ("wu", wu_ref, wu_v), ("wd", wd_ref, wd_v))
+        (("wg", wg_ref, wg_v), ("wu", wu_ref, wu_v), ("wd", wd_ref, wd_v)), 4
     ):
         loads[name] = pltpu.make_async_copy(src, dst, load_sem.at[i])
         loads[name].start()
+
+    loads["gate"].start()
 
     def loaded(*names):
         for name in names:
@@ -116,8 +132,10 @@
             return ("own", 0 if h in HALVES[0] else 1)
         if kind == "r":
             return key[:3]
-        if kind == "t" or (kind == "s" and key[4] != (1 if key[3] in RSET else -1)):
-            return ("up", h)
+        if kind == "t":
+            return ("up", h, 1)
+        if kind == "s" and key[4] != (1 if key[3] in RSET else -1):
+            return ("up", h, int(key[3] == 2))
         if kind in ("L", "R"):
             return ("S", *key[1:])
         if kind in ("l1", "r1"):
@@ -168,27 +186,35 @@
         for box in boxes:
             wait_for(send_sem.at[box], send_bytes.pop(box))
 
-    row_id = lax.broadcasted_iota(jnp.int32, (n_slots, tok_dev), 0)
-    lane_id = lax.broadcasted_iota(jnp.int32, (n_slots, tok_dev), 1)
-    idx = jnp.full((n_slots, tok_dev), -1, jnp.int32)
-    for g in range(groups):
-        e = expert_at(g)
-        for j in range(slot):
-            idx = jnp.where(row_id == g * slot + j, sel_ref[j, e], idx)
-    onehot = jnp.where(lane_id == idx, 1.0, 0.0).astype(BF16)
-    loaded("tok")
-    for c in range(0, width, 1024):
-        cols = slice(c, c + 1024)
-        slots32[:, cols] = jnp.dot(onehot, tok_v[:, cols], preferred_element_type=F32)
-    recv4[0] = slots32[0:slot, :].astype(BF16)
     near = [back(g) for g in HALVES[0] if g > 0]
     far = [back(g) for g in HALVES[1]]
-    for g in near + far:
-        send4[g] = slots32[g * slot : (g + 1) * slot, :].astype(BF16)
+    with jax.named_scope("pick"):
+        loaded("sel")
+        row_id = lax.broadcasted_iota(jnp.int32, (n_slots, tok_dev), 0)
+        lane_id = lax.broadcasted_iota(jnp.int32, (n_slots, tok_dev), 1)
+        idx = jnp.full((n_slots, tok_dev), -1, jnp.int32)
+        for g in range(groups):
+            e = expert_at(g)
+            for j in range(slot):
+                idx = jnp.where(row_id == g * slot + j, sel_ref[j, e], idx)
+        onehot = jnp.where(lane_id == idx, 1.0, 0.0).astype(BF16)
+    for i in range(4):
+        with jax.named_scope("tok"):
+            loaded(i)
+        with jax.named_scope("sel"):
+            cols = slice(i * tokw, (i + 1) * tokw)
+            slots32[:, cols] = jnp.dot(onehot, tok_v[:, cols], preferred_element_type=F32)
+            for g in near:
+                send4[g, :, cols] = slots32[g * slot : (g + 1) * slot, cols].astype(BF16)
     with jax.named_scope("barrier"):
         pl.semaphore_wait(barrier, len(partners))
-    for g in near + far:
+    for g in near:
         remote(("in", back(g)), send4.at[g], recv4.at[back(g)], at_group(g))
+    for g in far:
+        send4[g] = slots32[g * slot : (g + 1) * slot, :].astype(BF16)
+        remote(("in", back(g)), send4.at[g], recv4.at[back(g)], at_group(g))
+    recv4[0] = slots32[0:slot, :].astype(BF16)
+    loaded("gate")
 
     lane8 = lax.broadcasted_iota(jnp.int32, (8, 128), 1)
     idx_l = jnp.full((8, 128), -1, jnp.int32)
@@ -214,7 +240,7 @@
 
     def pos(p, d1, d2):
         d1, d2 = d1 % RING, d2 % RING
-        return d2 * RING + d1 if p == 0 else d1 * RING + d2
+        return PLACE[(d2, d1) if p == 0 else (d1, d2)]
 
     def first(p, step):
         return at_x(step) if p == 0 else at_z(step)
@@ -259,26 +285,38 @@
         need(("s", h, p, d1, step))
         to_second(("t", h, p, d1), h, p, d1, -step, step)
 
-    tn = hid.shape[1] // 2
-
-    def up(h, n):
-        need(("up", h))
+    tn = hid.shape[2] // 2
+    batches = (slice(0, len(EARLY)), slice(len(EARLY), RING * RING))
+
+    def held(b):
+        return slice(batches[b].start * chunk, batches[b].stop * chunk)
+
+    def up(h, b, n):
+        for p in range(2):
+            if b == 1:
+                need(("r", h, p))
+            for step in (1, -1):
+                need(("f", h, p, step))
+                for d1 in RSET if step == 1 else LSET:
+                    if b == 1 or d1 != 2:
+                        need(("s", h, p, d1, step))
+        need(("up", h, b))
         loaded("wg", "wu")
-        lhs = rows[h].reshape(RING * RING * chunk, width)
+        lhs = rows[h, batches[b]].reshape(-1, width)
         cols = slice(n * tn, (n + 1) * tn)
         gate_val = jnp.dot(lhs, wg_v[:, cols], preferred_element_type=F32)
         up_val = jnp.dot(lhs, wu_v[:, cols], preferred_element_type=F32)
-        hid[:, cols] = (gate_val / (1.0 + jnp.exp(-gate_val)) * up_val).astype(BF16)
+        hid[h, held(b), cols] = (gate_val / (1.0 + jnp.exp(-gate_val)) * up_val).astype(BF16)
 
     dn = 512
 
-    def down(h, p, i):
+    def down(h, b, p, i):
         loaded("wd")
         start = p * halfw + i * subw
         for c in range(start, start + subw, dn):
             cols = slice(c, c + dn)
-            val = jnp.dot(hid[...], wd_v[:, cols], preferred_element_type=F32)
-            part[h, :, :, cols] = val.astype(BF16).reshape(RING * RING, chunk, dn)
+            val = jnp.dot(hid[h, held(b), :], wd_v[:, cols], preferred_element_type=F32)
+            part[h, batches[b], :, cols] = val.astype(BF16).reshape(-1, chunk, dn)
 
     def sub(i, lo=0, n=subw):
         return pl.ds(i * subw + lo, n)
@@ -406,13 +444,14 @@
     chunk = RING * slot
     halfw = width // 2
     vmem, hbm = pl.BlockSpec(memory_space=pltpu.VMEM), pl.BlockSpec(memory_space=pltpu.HBM)
-    smem = pl.BlockSpec(memory_space=pltpu.SMEM)
     slots, comb = pl.pallas_call(
         kernel,
         out_shape=(pltpu.VMEM((8 * slot, width), F32), pltpu.VMEM((tok_dev, 128), BF16)),
-        in_specs=[smem, smem, hbm, hbm, hbm, hbm],
+        in_specs=[hbm] * 6,
         out_specs=(vmem, vmem),
         scratch_shapes=[
+            pltpu.SMEM((slot, 8), jnp.int32),
+            pltpu.SMEM((slot, 8), F32),
             pltpu.VMEM((tok_dev, width), BF16),
             pltpu.VMEM((width, ff), BF16),
             pltpu.VMEM((width, ff), BF16),
@@ -423,7 +462,7 @@
             pltpu.VMEM((8, slot, width), BF16),
             pltpu.VMEM((2, 16, chunk, width), BF16),
             pltpu.VMEM((2, 16, chunk, width), BF16),
-            pltpu.VMEM((16 * chunk, ff), BF16),
+            pltpu.VMEM((2, 16 * chunk, ff), BF16),
             pltpu.VMEM((2, 2, 4, chunk, halfw), BF16),
             pltpu.VMEM((2, 2, 4, chunk, halfw), BF16),
             pltpu.VMEM((2, 2, 4, chunk, halfw), BF16),
@@ -434,7 +473,7 @@
             pltpu.VMEM((8 * slot, width), F32),
             pltpu.SemaphoreType.DMA((7,)),
             pltpu.SemaphoreType.DMA((N_RECV,)),
-            pltpu.SemaphoreType.DMA((4,)),
+            pltpu.SemaphoreType.DMA((9,)),
         ],
         compiler_params=pltpu.CompilerParams(
             collective_id=0, has_side_effects=True, vmem_limit_bytes=56 * 1024 * 1024

time: 68.7 us -> 65.8 us (0.958)
  Pallas kernels: 68.6 us -> 65.7 us
    pallas_call x1, Pallas kernels: 67.4 us -> 64.5 us  [per_device(): pl.pallas_call(kernel, out_shape=(pltpu.VMEM((8 * slot, width), F32), plt...]
where the time goes in v5:
time: 65.8 us; the launch traced here: 65.7 us
  Pallas kernels  65.7 us (100%)
    pallas_call x1, Pallas kernels, per_device(): pl.pallas_call(kernel, out_shape=(pltpu.VMEM((8 * slot, width), F32), plt...  64.5 us

profile of v5, /device:TPU:1, one launch (start us, length us, event | category | flops | bytes accessed | tf_op | source)
XLA Modules:
  0.0 65.7 jit_solution(13158544263398207665)
XLA Ops:
  0.0 64.5 %moe.1 = (f32[32,4096]{1,0:T(8,128)S(1)}, bf16[128,128]{1,0:T(8,128)(2,1)S(1)}) custom-call(s32[4,8]{1,0:T(4,128)} %bitcast.8, f32[4,8]{1,0:T(4,128)} %bitcast.9, bf16[128,4096]{1,0:T(8,128)(2,1)} %tok_ref.1, bf16[4096,512]{1,0:T(8,128)(2,1)} %bitcast.5, bf16[4096,512]{1,0:T(8,128)(2,1)} %bitcast.6, bf16[512,4096]{1,0:T(8,128)(2,1)} %bitcast.7), custom_call_target="tpu_custom_call" | custom-call | tf_op jit(solution)/shard_map/moe/pallas_call | solution.py:447
  64.5 1.2 %combine.1 = bf16[128,4096]{1,0:T(8,128)(2,1)} custom-call(f32[32,4096]{1,0:T(8,128)S(1)} %get-tuple-element.7.slots_ref, bf16[128,128]{1,0:T(8,128)(2,1)S(1)} %get-tuple-element.8.comb_ref), custom_call_target="tpu_custom_call" | custom-call | tf_op jit(solution)/shard_map/combine/pallas_call | solution.py:485

commit v6 on v5

--- a/solution.py
+++ b/solution.py
@@ -9,7 +9,8 @@
 BF16, F32 = jnp.bfloat16, jnp.float32
 RING = 4
 SUB = 2
-N_RECV = 130
+N_RECV = 122
+DIRECT = (1,)
 RSET, LSET = (0, 3), (2, 1)
 EARLY = tuple((z, x) for z in (0, 1, 3) for x in (0, 1, 3))
 LATE = tuple((z, x) for z in range(RING) for x in range(RING) if 2 in (z, x))
@@ -17,49 +18,48 @@
 HALVES = ((0, 1, 2, 6), (3, 7, 4, 5))
 
 ORDER = (
-    ("own", 0), ("s", 0, 1, 0, -1), ("s", 0, 0, 0, -1), ("f", 0, 0, -1), ("s", 0, 0, 0, 1), ("f", 0, 0, 1),
-    ("f", 0, 1, -1), ("s", 0, 1, 0, 1), ("f", 0, 1, 1), ("own", 1), ("f", 1, 1, -1), ("s", 1, 0, 0, 1),
-    ("s", 1, 1, 0, -1), ("f", 1, 1, 1), ("s", 1, 0, 0, -1), ("f", 1, 0, -1), ("s", 1, 1, 0, 1), ("f", 1, 0, 1),
-    ("t", 0, 0, 0), ("s", 0, 0, 3, -1), ("r", 0, 0, 1), ("s", 0, 0, 3, 1), ("s", 0, 0, 1, 1), ("s", 0, 0, 1, -1),
-    ("s", 0, 1, 1, -1), ("r", 0, 0, -1), ("s", 0, 1, 3, 1), ("s", 0, 1, 3, -1), ("s", 0, 1, 1, 1), ("r", 0, 1, -1),
-    ("t", 0, 1, 0), ("r", 0, 1, 1), ("r", 1, 1, -1), ("s", 1, 1, 1, -1), ("s", 1, 1, 1, 1), ("t", 1, 0, 0),
-    ("t", 1, 1, 0), ("s", 1, 0, 1, -1), ("s", 1, 0, 1, 1), ("r", 1, 0, -1), ("s", 1, 1, 3, -1), ("s", 1, 0, 3, 1),
-    ("s", 1, 0, 3, -1), ("r", 1, 0, 1), ("r", 1, 1, 1), ("s", 1, 1, 3, 1), ("t", 0, 1, 1), ("s", 0, 0, 2, 1),
-    ("s", 0, 0, 2, -1), ("t", 0, 1, 3), ("t", 0, 0, 1), ("t", 0, 0, 3), ("up", 0, 0, 0), ("s", 0, 1, 2, -1),
-    ("up", 0, 0, 1), ("t", 1, 0, 1), ("s", 0, 1, 2, 1), ("t", 1, 1, 1), ("down", 0, 0, 0, 1), ("L", 0, 0, 1, 1),
-    ("down", 0, 0, 1, 1), ("L", 0, 1, 1, 1), ("R", 0, 1, 0, 1), ("R", 0, 1, 3, 1), ("R", 0, 0, 0, 1),
-    ("R", 0, 0, 3, 1), ("down", 0, 0, 1, 0), ("R", 0, 1, 0, 0), ("R", 0, 1, 3, 0), ("L", 0, 1, 1, 0),
-    ("down", 0, 0, 0, 0), ("R", 0, 0, 3, 0), ("L", 0, 0, 1, 0), ("R", 0, 0, 0, 0), ("t", 0, 0, 2), ("s", 1, 0, 2, 1),
-    ("s", 1, 0, 2, -1), ("t", 1, 0, 3), ("t", 0, 1, 2), ("s", 1, 1, 2, 1), ("s", 1, 1, 2, -1), ("up", 1, 0, 0),
-    ("up", 1, 0, 1), ("down", 1, 0, 0, 0), ("R", 1, 0, 0, 0), ("R", 1, 0, 3, 0), ("down", 1, 0, 1, 1),
-    ("R", 1, 1, 0, 1), ("L", 1, 1, 1, 1), ("L", 1, 0, 1, 0), ("down", 1, 0, 1, 0), ("L", 1, 1, 1, 0),
-    ("R", 1, 1, 0, 0), ("R", 1, 1, 3, 1), ("R", 1, 1, 3, 0), ("t", 1, 1, 3), ("down", 1, 0, 0, 1), ("R", 1, 0, 3, 1),
-    ("R", 1, 0, 0, 1), ("L", 1, 0, 1, 1), ("up", 0, 1, 0), ("up", 0, 1, 1), ("down", 0, 1, 0, 0), ("F", 0, 0, 0, 0),
-    ("t", 1, 0, 2), ("t", 1, 1, 2), ("F", 0, 0, 2, 0), ("down", 0, 1, 0, 1), ("F", 0, 0, 3, 1), ("L", 0, 0, 2, 1),
-    ("F", 0, 0, 2, 1), ("down", 0, 1, 1, 0), ("F", 0, 1, 2, 0), ("F", 0, 1, 3, 0), ("L", 0, 1, 2, 0),
-    ("F", 0, 1, 1, 0), ("F", 0, 1, 0, 0), ("L", 0, 0, 2, 0), ("F", 0, 0, 0, 1), ("F", 0, 0, 1, 0), ("F", 0, 0, 3, 0),
-    ("down", 0, 1, 1, 1), ("F", 0, 1, 0, 1), ("F", 0, 1, 2, 1), ("F", 0, 1, 3, 1), ("L", 0, 1, 2, 1),
-    ("F", 0, 1, 1, 1), ("F", 0, 0, 1, 1), ("A", 0, 0, 0, 0), ("A", 0, 1, 3, 0), ("A", 0, 0, 3, 1), ("up", 1, 1, 0),
-    ("up", 1, 1, 1), ("down", 1, 1, 1, 0), ("A", 0, 0, 2, 1), ("F", 1, 1, 0, 0), ("F", 1, 1, 1, 0), ("L", 1, 1, 2, 0),
-    ("down", 1, 1, 0, 0), ("F", 1, 0, 0, 0), ("F", 1, 0, 2, 0), ("down", 1, 1, 1, 1), ("F", 1, 1, 0, 1),
-    ("L", 1, 1, 2, 1), ("L", 1, 0, 2, 0), ("F", 1, 1, 3, 1), ("A", 0, 1, 1, 0), ("A", 0, 0, 1, 0), ("A", 0, 1, 2, 1),
-    ("F", 1, 1, 2, 0), ("A", 0, 0, 0, 1), ("F", 1, 1, 2, 1), ("F", 1, 0, 1, 0), ("F", 1, 0, 3, 0), ("F", 1, 1, 3, 0),
-    ("A", 0, 1, 3, 1), ("A", 0, 1, 0, 0), ("down", 1, 1, 0, 1), ("F", 1, 0, 2, 1), ("F", 1, 0, 0, 1),
-    ("F", 1, 0, 1, 1), ("L", 1, 0, 2, 1), ("F", 1, 0, 3, 1), ("A", 0, 1, 2, 0), ("F", 1, 1, 1, 1), ("A", 0, 0, 2, 0),
-    ("A", 0, 0, 3, 0), ("A", 0, 1, 0, 1), ("A", 0, 1, 1, 1), ("A", 0, 0, 1, 1), ("S", 0, 0, 0, 0), ("S", 0, 1, 3, 0),
-    ("S", 0, 0, 3, 1), ("S", 0, 0, 2, 1), ("A", 1, 1, 0, 0), ("A", 1, 1, 1, 0), ("A", 1, 0, 0, 0), ("A", 1, 0, 2, 0),
-    ("S", 0, 1, 1, 0), ("S", 0, 0, 1, 0), ("S", 0, 1, 2, 1), ("A", 1, 1, 0, 1), ("S", 0, 0, 0, 1), ("A", 1, 0, 1, 0),
-    ("A", 1, 1, 2, 0), ("A", 1, 0, 3, 0), ("A", 1, 0, 2, 1), ("A", 1, 1, 3, 1), ("A", 1, 1, 2, 1), ("A", 1, 0, 0, 1),
-    ("A", 1, 0, 1, 1), ("A", 1, 1, 3, 0), ("S", 0, 1, 2, 0), ("S", 0, 0, 2, 0), ("S", 0, 1, 3, 1), ("A", 1, 1, 1, 1),
-    ("A", 1, 0, 3, 1), ("S", 0, 0, 1, 1), ("S", 0, 1, 1, 1), ("S", 0, 1, 0, 0), ("S", 0, 0, 3, 0), ("S", 0, 1, 0, 1),
-    ("B", 0, 0, -1, 1), ("S", 1, 0, 0, 0), ("S", 1, 0, 2, 0), ("B", 0, 0, 1, 1), ("B", 0, 1, -1, 1),
-    ("S", 1, 1, 1, 0), ("B", 0, 1, 1, 1), ("S", 1, 1, 0, 0), ("S", 1, 0, 1, 0), ("S", 1, 1, 2, 0), ("S", 1, 0, 3, 0),
-    ("S", 1, 0, 2, 1), ("S", 1, 1, 2, 1), ("S", 1, 1, 0, 1), ("S", 1, 0, 0, 1), ("B", 0, 0, -1, 0), ("B", 0, 1, 1, 0),
-    ("S", 1, 0, 1, 1), ("S", 1, 1, 3, 1), ("B", 0, 1, -1, 0), ("S", 1, 1, 1, 1), ("S", 1, 0, 3, 1), ("S", 1, 1, 3, 0),
-    ("B", 0, 0, 1, 0), ("B", 1, 1, -1, 0), ("B", 1, 0, -1, 0), ("Z", 0, 1, 1), ("B", 1, 0, 1, 0), ("B", 1, 1, 1, 0),
-    ("B", 1, 1, -1, 1), ("Z", 0, 0, 1), ("B", 1, 0, -1, 1), ("B", 1, 1, 1, 1), ("B", 1, 0, 1, 1), ("Z", 0, 1, 0),
-    ("Z", 0, 0, 0), ("Z", 1, 0, 0), ("Z", 1, 1, 0), ("Z", 1, 1, 1), ("Z", 1, 0, 1), ("X", 0, 1, 1), ("X", 0, 0, 1),
-    ("X", 0, 1, 0), ("X", 0, 0, 0), ("X", 1, 0, 0), ("X", 1, 1, 0), ("X", 1, 1, 1), ("X", 1, 0, 1),
+    ("own", 0), ("s", 0, 0, 0, -1), ("f", 0, 0, -1), ("f", 0, 0, 1), ("f", 0, 1, 1), ("s", 0, 1, 0, 1),
+    ("f", 0, 1, -1), ("s", 0, 1, 0, -1), ("s", 0, 0, 0, 1), ("own", 1), ("s", 1, 1, 0, 1), ("s", 1, 0, 0, 1),
+    ("f", 1, 0, -1), ("s", 1, 1, 0, -1), ("f", 1, 1, 1), ("f", 1, 1, -1), ("s", 1, 0, 0, -1), ("f", 1, 0, 1),
+    ("s", 0, 0, 1, 1), ("r", 0, 0, -1), ("s", 0, 0, 3, -1), ("r", 0, 1, 1), ("s", 0, 1, 3, -1), ("r", 0, 0, 1),
+    ("s", 0, 0, 1, -1), ("s", 0, 0, 3, 1), ("s", 0, 1, 3, 1), ("s", 0, 1, 1, 1), ("s", 0, 1, 1, -1), ("r", 0, 1, -1),
+    ("t", 0, 0, 0), ("t", 0, 1, 0), ("r", 1, 1, -1), ("s", 1, 0, 1, -1), ("t", 1, 1, 0), ("r", 1, 0, -1),
+    ("s", 1, 1, 1, -1), ("s", 1, 1, 1, 1), ("s", 1, 0, 1, 1), ("t", 1, 0, 0), ("r", 1, 0, 1), ("s", 1, 1, 3, 1),
+    ("r", 1, 1, 1), ("s", 1, 1, 3, -1), ("s", 1, 0, 3, -1), ("s", 1, 0, 3, 1), ("s", 0, 0, 2, -1), ("s", 0, 0, 2, 1),
+    ("t", 0, 1, 3), ("t", 0, 0, 1), ("s", 0, 1, 2, -1), ("t", 0, 1, 1), ("s", 0, 1, 2, 1), ("t", 0, 0, 3),
+    ("up", 0, 0, 0), ("up", 0, 0, 1), ("down", 0, 0, 0, 1), ("R", 0, 0, 3, 1), ("down", 0, 0, 1, 0),
+    ("down", 0, 0, 1, 1), ("R", 0, 1, 3, 1), ("R", 0, 1, 3, 0), ("R", 0, 1, 0, 0), ("L", 0, 1, 1, 1), ("t", 1, 1, 1),
+    ("down", 0, 0, 0, 0), ("R", 0, 0, 0, 0), ("R", 0, 0, 3, 0), ("L", 0, 1, 1, 0), ("R", 0, 1, 0, 1),
+    ("L", 0, 0, 1, 1), ("L", 0, 0, 1, 0), ("t", 1, 0, 1), ("R", 0, 0, 0, 1), ("t", 0, 0, 2), ("t", 0, 1, 2),
+    ("s", 1, 0, 2, 1), ("s", 1, 1, 2, -1), ("s", 1, 1, 2, 1), ("s", 1, 0, 2, -1), ("t", 1, 1, 3), ("up", 1, 0, 0),
+    ("t", 1, 0, 3), ("up", 1, 0, 1), ("down", 1, 0, 0, 1), ("L", 1, 0, 1, 1), ("down", 1, 0, 1, 0), ("R", 1, 1, 3, 0),
+    ("down", 1, 0, 0, 0), ("R", 1, 0, 0, 0), ("R", 1, 0, 0, 1), ("L", 1, 0, 1, 0), ("down", 1, 0, 1, 1),
+    ("R", 1, 1, 3, 1), ("L", 1, 1, 1, 0), ("R", 1, 1, 0, 1), ("R", 1, 1, 0, 0), ("L", 1, 1, 1, 1), ("R", 1, 0, 3, 1),
+    ("R", 1, 0, 3, 0), ("up", 0, 1, 0), ("up", 0, 1, 1), ("t", 1, 1, 2), ("t", 1, 0, 2), ("down", 0, 1, 1, 0),
+    ("F", 0, 1, 0, 0), ("down", 0, 1, 0, 1), ("F", 0, 0, 3, 1), ("F", 0, 0, 1, 1), ("F", 0, 0, 0, 1),
+    ("F", 0, 1, 3, 0), ("L", 0, 0, 2, 1), ("F", 0, 1, 2, 0), ("down", 0, 1, 1, 1), ("F", 0, 1, 2, 1),
+    ("F", 0, 1, 0, 1), ("L", 0, 1, 2, 1), ("F", 0, 1, 1, 1), ("F", 0, 0, 2, 1), ("L", 0, 1, 2, 0),
+    ("down", 0, 1, 0, 0), ("F", 0, 0, 0, 0), ("F", 0, 0, 3, 0), ("F", 0, 0, 1, 0), ("F", 0, 0, 2, 0),
+    ("L", 0, 0, 2, 0), ("F", 0, 1, 1, 0), ("F", 0, 1, 3, 1), ("A", 0, 1, 0, 0), ("A", 0, 0, 3, 1), ("up", 1, 1, 0),
+    ("A", 0, 0, 0, 1), ("A", 0, 1, 3, 0), ("A", 0, 1, 2, 0), ("A", 0, 0, 1, 1), ("up", 1, 1, 1), ("A", 0, 1, 2, 1),
+    ("A", 0, 0, 2, 1), ("A", 0, 1, 0, 1), ("down", 1, 1, 1, 0), ("F", 1, 1, 0, 0), ("F", 1, 1, 1, 0),
+    ("F", 1, 1, 3, 0), ("A", 0, 0, 0, 0), ("L", 1, 1, 2, 0), ("F", 1, 1, 2, 0), ("down", 1, 1, 0, 1),
+    ("F", 1, 0, 3, 1), ("L", 1, 0, 2, 1), ("F", 1, 0, 2, 1), ("A", 0, 0, 1, 0), ("down", 1, 1, 1, 1),
+    ("L", 1, 1, 2, 1), ("F", 1, 1, 2, 1), ("F", 1, 1, 1, 1), ("F", 1, 0, 0, 1), ("A", 0, 0, 3, 0), ("A", 0, 1, 1, 0),
+    ("A", 0, 0, 2, 0), ("down", 1, 1, 0, 0), ("L", 1, 0, 2, 0), ("F", 1, 0, 2, 0), ("F", 1, 1, 3, 1),
+    ("F", 1, 1, 0, 1), ("A", 0, 1, 3, 1), ("F", 1, 0, 3, 0), ("F", 1, 0, 1, 1), ("F", 1, 0, 0, 0), ("A", 0, 1, 1, 1),
+    ("F", 1, 0, 1, 0), ("S", 0, 1, 0, 0), ("S", 0, 0, 3, 1), ("S", 0, 1, 2, 0), ("S", 0, 0, 1, 1), ("S", 0, 1, 3, 0),
+    ("S", 0, 0, 0, 1), ("S", 0, 1, 2, 1), ("S", 0, 0, 2, 1), ("S", 0, 1, 0, 1), ("S", 0, 0, 0, 0), ("A", 1, 1, 1, 0),
+    ("A", 1, 0, 2, 1), ("A", 1, 1, 0, 0), ("A", 1, 0, 3, 1), ("A", 1, 1, 2, 0), ("S", 0, 0, 1, 0), ("A", 1, 1, 3, 0),
+    ("A", 1, 1, 2, 1), ("S", 0, 0, 2, 0), ("A", 1, 0, 0, 1), ("A", 1, 1, 1, 1), ("A", 1, 0, 2, 0), ("S", 0, 0, 3, 0),
+    ("S", 0, 1, 1, 0), ("A", 1, 0, 1, 1), ("A", 1, 1, 3, 1), ("S", 0, 1, 1, 1), ("A", 1, 0, 1, 0), ("A", 1, 1, 0, 1),
+    ("B", 0, 1, -1, 0), ("A", 1, 0, 3, 0), ("B", 0, 0, -1, 1), ("S", 0, 1, 3, 1), ("B", 0, 1, -1, 1),
+    ("A", 1, 0, 0, 0), ("S", 1, 1, 1, 0), ("B", 0, 1, 1, 0), ("B", 0, 0, 1, 1), ("S", 1, 0, 2, 1), ("B", 0, 1, 1, 1),
+    ("S", 1, 1, 2, 0), ("S", 1, 1, 0, 0), ("S", 1, 0, 2, 0), ("S", 1, 0, 3, 1), ("S", 1, 1, 2, 1), ("B", 0, 0, -1, 0),
+    ("S", 1, 0, 1, 1), ("S", 1, 0, 0, 1), ("S", 1, 1, 3, 0), ("B", 0, 0, 1, 0), ("S", 1, 1, 1, 1), ("S", 1, 0, 1, 0),
+    ("S", 1, 1, 3, 1), ("S", 1, 0, 3, 0), ("S", 1, 1, 0, 1), ("S", 1, 0, 0, 0), ("Z", 0, 0, 1), ("Z", 0, 1, 0),
+    ("Z", 0, 1, 1), ("Z", 1, 0, 1), ("Z", 0, 0, 0), ("Z", 1, 1, 0), ("Z", 1, 0, 0), ("Z", 1, 1, 1), ("X", 0, 0, 1),
+    ("X", 0, 1, 0), ("X", 0, 1, 1), ("X", 1, 0, 1), ("X", 0, 0, 0), ("X", 1, 1, 0), ("X", 1, 0, 0), ("X", 1, 1, 1),
 )
 
 
@@ -98,7 +98,7 @@
         return ((RING - g // 2) % RING) * 2 + g % 2
 
     barrier = pltpu.get_barrier_semaphore()
-    partners = [at_x(1), at_x(-1), at_z(1), at_z(-1)] + [at_group(g) for g in range(1, groups)]
+    partners = [at(step) for at in (at_x, at_z) for step in (1, -1, 2)] + [at_group(g) for g in range(1, groups)]
     for who in partners:
         pl.semaphore_signal(barrier, inc=1, device_id=who, device_id_type=MESH)
 
@@ -138,7 +138,7 @@
             return ("up", h, int(key[3] == 2))
         if kind in ("L", "R"):
             return ("S", *key[1:])
-        if kind in ("l1", "r1"):
+        if kind in ("l1", "r1") or (kind == "F1" and h in DIRECT):
             return ("Z", *key[1:])
         if kind == "b":
             return ("Z", h, key[2], key[4])
@@ -364,6 +364,14 @@
         )
         summed[h, p, d1, :, sub(i)] = total.astype(BF16)
         lo, hi = sub(i, 0, subw // 2), sub(i, subw // 2, subw // 2)
+        if h in DIRECT:
+            if d1 != 0:
+                name, dst, step = {2: ("F1", relay1, 2), 1: ("l1", fin1_l, 1), 3: ("r1", fin1_r, -1)}[d1]
+                remote(
+                    (name, h, p, i), summed.at[h, p, d1, :, sub(i)], dst.at[h, p, :, sub(i)],
+                    first(p, step),
+                )
+            return
         if d1 == 2:
             remote(("F1", h, p, 1, i), summed.at[h, p, 2, :, lo], relay1.at[h, p, :, lo], first(p, 1))
             remote(("F1", h, p, -1, i), summed.at[h, p, 2, :, hi], relay1.at[h, p, :, hi], first(p, -1))
@@ -383,11 +391,14 @@
 
     def finish(h, p, i):
         need(("Z", h, p, i))
-        slots32[0:chunk, psub(p, i)] = (
+        total = (
             summed[h, p, 0, :, sub(i)].astype(F32)
             + fin1_l[h, p, :, sub(i)].astype(F32)
             + fin1_r[h, p, :, sub(i)].astype(F32)
         )
+        if h in DIRECT:
+            total += relay1[h, p, :, sub(i)].astype(F32)
+        slots32[0:chunk, psub(p, i)] = total
         for r, g in enumerate(HALVES[h]):
             value = slots32[r * slot : (r + 1) * slot, psub(p, i)].astype(BF16)
             if g == 0:

time: 65.8 us -> 64.6 us (0.982)
  Pallas kernels: 65.7 us -> 64.5 us
    pallas_call x1, Pallas kernels: 64.5 us -> 63.3 us  [per_device(): pl.pallas_call(kernel, out_shape=(pltpu.VMEM((8 * slot, width), F32), plt...]
where the time goes in v6:
time: 64.6 us; the launch traced here: 64.5 us
  Pallas kernels  64.5 us (100%)
    pallas_call x1, Pallas kernels, per_device(): pl.pallas_call(kernel, out_shape=(pltpu.VMEM((8 * slot, width), F32), plt...  63.3 us

profile of v6, /device:TPU:1, one launch (start us, length us, event | category | flops | bytes accessed | tf_op | source)
XLA Modules:
  0.0 64.5 jit_solution(4649319520224653934)
XLA Ops:
  0.0 63.3 %moe.1 = (f32[32,4096]{1,0:T(8,128)S(1)}, bf16[128,128]{1,0:T(8,128)(2,1)S(1)}) custom-call(s32[4,8]{1,0:T(4,128)} %bitcast.8, f32[4,8]{1,0:T(4,128)} %bitcast.9, bf16[128,4096]{1,0:T(8,128)(2,1)} %tok_ref.1, bf16[4096,512]{1,0:T(8,128)(2,1)} %bitcast.5, bf16[4096,512]{1,0:T(8,128)(2,1)} %bitcast.6, bf16[512,4096]{1,0:T(8,128)(2,1)} %bitcast.7), custom_call_target="tpu_custom_call" | custom-call | tf_op jit(solution)/shard_map/moe/pallas_call | solution.py:458
  63.3 1.2 %combine.1 = bf16[128,4096]{1,0:T(8,128)(2,1)} custom-call(f32[32,4096]{1,0:T(8,128)S(1)} %get-tuple-element.7.slots_ref, bf16[128,128]{1,0:T(8,128)(2,1)S(1)} %get-tuple-element.8.comb_ref), custom_call_target="tpu_custom_call" | custom-call | tf_op jit(solution)/shard_map/combine/pallas_call | solution.py:496

commit v7 on v6

v7 whole, which is shorter than its diff:
```python
import jax
import jax.numpy as jnp
from jax import lax
from jax.experimental import pallas as pl
from jax.experimental.pallas import tpu as pltpu
from jax.sharding import PartitionSpec as P

MESH = pl.DeviceIdType.MESH
BF16, F32 = jnp.bfloat16, jnp.float32
RING = 4
N_RECV = 141
DIRECT = (2,)
RSET, LSET = (0, 3), (2, 1)
ROUND = tuple((z, x) for z in range(RING) for x in range(RING))
EARLY = tuple(at for at in ROUND if 2 not in at and at != (1, 3))
LATE = tuple(at for at in ROUND if at not in EARLY)
PLACE = {at: i for i, at in enumerate(EARLY + LATE)}
BATCHES = ((0, 1), (2, 6, 3, 7), (4, 5))
SUBS = (1, 2, 1)
SPLIT = (1,)

ORDER = (
    ("own", 0), ("f", 0, 0, -1), ("f", 0, 1, -1), ("s", 0, 1, 0, -1), ("f", 0, 1, 1), ("s", 0, 0, 0, -1),
    ("f", 0, 0, 1), ("s", 0, 0, 0, 1), ("s", 0, 1, 0, 1), ("s", 0, 0, 1, -1), ("s", 0, 1, 1, -1), ("s", 0, 0, 1, 1),
    ("s", 0, 1, 1, 1), ("s", 0, 1, 3, -1), ("r", 0, 1, 1), ("r", 0, 0, 1), ("s", 0, 0, 3, 1), ("s", 0, 0, 3, -1),
    ("s", 0, 1, 3, 1), ("r", 0, 1, -1), ("r", 0, 0, -1), ("own", 1), ("f", 1, 0, -1), ("f", 1, 0, 1),
    ("s", 1, 1, 0, -1), ("s", 1, 1, 0, 1), ("f", 1, 1, -1), ("s", 1, 0, 0, -1), ("f", 1, 1, 1), ("s", 1, 0, 0, 1),
    ("t", 0, 0, 0), ("t", 0, 1, 0), ("own", 2), ("f", 2, 0, -1), ("f", 2, 0, 1), ("f", 2, 1, 1), ("s", 2, 1, 0, 1),
    ("s", 2, 0, 0, 1), ("s", 2, 0, 0, -1), ("f", 2, 1, -1), ("s", 2, 1, 0, -1), ("t", 0, 0, 1), ("t", 0, 1, 1),
    ("s", 0, 1, 2, -1), ("s", 0, 0, 2, -1), ("s", 0, 1, 2, 1), ("t", 0, 0, 3), ("t", 0, 1, 3), ("s", 0, 0, 2, 1),
    ("r", 1, 1, -1), ("r", 1, 0, -1), ("r", 1, 1, 1), ("s", 1, 0, 3, 1), ("s", 1, 1, 3, 1), ("r", 1, 0, 1),
    ("s", 1, 0, 3, -1), ("s", 1, 1, 1, -1), ("s", 1, 0, 1, 1), ("s", 1, 1, 3, -1), ("s", 1, 0, 1, -1),
    ("s", 1, 1, 1, 1), ("t", 1, 0, 0), ("t", 1, 1, 0), ("s", 2, 0, 1, -1), ("s", 2, 0, 1, 1), ("r", 2, 0, -1),
    ("s", 2, 1, 1, -1), ("r", 2, 1, -1), ("r", 2, 1, 1), ("r", 2, 0, 1), ("s", 2, 0, 3, -1), ("s", 2, 1, 3, 1),
    ("s", 2, 0, 3, 1), ("s", 2, 1, 3, -1), ("s", 2, 1, 1, 1), ("t", 2, 0, 0), ("t", 2, 1, 0), ("t", 0, 0, 2),
    ("t", 0, 1, 2), ("s", 1, 1, 2, -1), ("s", 1, 1, 2, 1), ("t", 1, 1, 1), ("t", 1, 1, 3), ("t", 1, 0, 3),
    ("s", 1, 0, 2, -1), ("s", 1, 0, 2, 1), ("t", 1, 0, 1), ("t", 2, 0, 1), ("up", 1, 0, 0), ("t", 2, 1, 1),
    ("up", 1, 0, 1), ("down", 1, 0, 0, 1), ("s", 2, 0, 2, -1), ("up", 0, 2, 0), ("s", 2, 1, 2, -1),
    ("down", 1, 0, 0, 0), ("R", 1, 0, 3, 0), ("down", 1, 0, 1, 1), ("R", 1, 1, 3, 1), ("t", 2, 0, 3),
    ("L", 1, 1, 1, 1), ("t", 1, 0, 2), ("t", 1, 1, 2), ("R", 1, 1, 0, 1), ("R", 1, 0, 0, 0), ("s", 2, 0, 2, 1),
    ("t", 2, 1, 3), ("R", 1, 0, 3, 1), ("down", 1, 0, 1, 0), ("L", 1, 1, 1, 0), ("up", 0, 2, 1), ("down", 0, 2, 0, 0),
    ("F", 0, 0, 1, 0), ("L", 0, 0, 1, 0), ("F", 0, 0, 2, 0), ("F", 0, 0, 3, 0), ("R", 0, 0, 3, 0), ("R", 0, 0, 0, 0),
    ("down", 0, 2, 1, 0), ("t", 2, 0, 2), ("F", 0, 1, 3, 0), ("F", 0, 1, 0, 0), ("F", 0, 1, 2, 0), ("F", 0, 1, 1, 0),
    ("R", 0, 1, 0, 0), ("R", 1, 1, 0, 0), ("R", 1, 1, 3, 0), ("L", 0, 0, 2, 0), ("s", 2, 1, 2, 1), ("t", 2, 1, 2),
    ("R", 0, 1, 3, 0), ("L", 1, 0, 1, 0), ("L", 0, 1, 1, 0), ("R", 1, 0, 0, 1), ("L", 1, 0, 1, 1), ("F", 0, 0, 0, 0),
    ("L", 0, 1, 2, 0), ("up", 1, 1, 0), ("up", 1, 1, 1), ("A", 0, 1, 3, 0), ("down", 1, 1, 0, 1), ("F", 1, 0, 3, 1),
    ("F", 1, 0, 0, 1), ("down", 1, 1, 1, 0), ("F", 1, 1, 2, 0), ("F", 1, 1, 0, 0), ("F", 1, 1, 3, 0),
    ("down", 1, 1, 0, 0), ("F", 1, 0, 0, 0), ("F", 1, 0, 2, 0), ("F", 1, 0, 2, 1), ("down", 1, 1, 1, 1),
    ("L", 1, 1, 2, 1), ("A", 0, 0, 2, 0), ("F", 1, 1, 0, 1), ("F", 1, 1, 2, 1), ("A", 0, 0, 1, 0), ("A", 0, 1, 0, 0),
    ("A", 0, 1, 1, 0), ("L", 1, 1, 2, 0), ("A", 0, 1, 2, 0), ("F", 1, 1, 1, 1), ("L", 1, 0, 2, 0), ("A", 0, 0, 3, 0),
    ("F", 1, 0, 1, 1), ("F", 1, 1, 1, 0), ("F", 1, 0, 3, 0), ("F", 1, 0, 1, 0), ("L", 1, 0, 2, 1), ("F", 1, 1, 3, 1),
    ("A", 0, 0, 0, 0), ("up", 2, 2, 0), ("S", 0, 1, 3, 0), ("A", 1, 1, 0, 0), ("up", 2, 2, 1), ("A", 1, 0, 2, 0),
    ("A", 1, 1, 2, 0), ("down", 2, 2, 1, 0), ("A", 1, 0, 0, 0), ("F", 2, 1, 3, 0), ("R", 2, 1, 3, 0),
    ("A", 1, 0, 2, 1), ("F", 2, 1, 0, 0), ("F", 2, 1, 2, 0), ("L", 2, 1, 1, 0), ("R", 2, 1, 0, 0), ("L", 2, 1, 2, 0),
    ("A", 1, 0, 0, 1), ("A", 1, 1, 2, 1), ("down", 2, 2, 0, 0), ("F", 2, 0, 3, 0), ("S", 0, 0, 2, 0),
    ("F", 2, 0, 2, 0), ("S", 0, 0, 3, 0), ("L", 2, 0, 1, 0), ("R", 2, 0, 0, 0), ("F", 2, 0, 0, 0), ("A", 1, 1, 0, 1),
    ("R", 2, 0, 3, 0), ("F", 2, 0, 1, 0), ("L", 2, 0, 2, 0), ("A", 1, 1, 3, 0), ("F", 2, 1, 1, 0), ("A", 1, 0, 3, 1),
    ("S", 0, 1, 1, 0), ("S", 0, 1, 0, 0), ("S", 0, 0, 1, 0), ("S", 0, 1, 2, 0), ("A", 1, 0, 3, 0), ("A", 1, 0, 1, 1),
    ("A", 1, 1, 1, 1), ("A", 1, 0, 1, 0), ("A", 1, 1, 1, 0), ("A", 1, 1, 3, 1), ("S", 0, 0, 0, 0), ("S", 1, 1, 2, 0),
    ("S", 1, 1, 0, 0), ("S", 1, 0, 2, 0), ("S", 1, 0, 0, 0), ("A", 2, 1, 3, 0), ("S", 1, 0, 2, 1), ("S", 1, 0, 0, 1),
    ("A", 2, 1, 2, 0), ("A", 2, 1, 0, 0), ("A", 2, 0, 2, 0), ("A", 2, 0, 3, 0), ("S", 1, 1, 2, 1), ("A", 2, 0, 0, 0),
    ("B", 0, 0, 1, 0), ("B", 0, 0, -1, 0), ("A", 2, 0, 1, 0), ("S", 1, 1, 0, 1), ("B", 0, 1, -1, 0),
    ("A", 2, 1, 1, 0), ("S", 1, 0, 3, 1), ("S", 1, 1, 3, 0), ("S", 1, 0, 1, 1), ("S", 1, 1, 1, 1), ("B", 0, 1, 1, 0),
    ("S", 1, 0, 1, 0), ("S", 1, 1, 1, 0), ("S", 1, 1, 3, 1), ("B", 1, 1, -1, 0), ("S", 1, 0, 3, 0),
    ("B", 1, 0, -1, 0), ("B", 1, 0, 1, 0), ("B", 1, 1, 1, 0), ("B", 1, 0, -1, 1), ("S", 2, 0, 2, 0),
    ("S", 2, 1, 3, 0), ("B", 1, 1, -1, 1), ("S", 2, 0, 3, 0), ("S", 2, 1, 2, 0), ("B", 1, 0, 1, 1), ("B", 1, 1, 1, 1),
    ("S", 2, 0, 1, 0), ("S", 2, 1, 0, 0), ("S", 2, 0, 0, 0), ("Z", 0, 0, 0), ("S", 2, 1, 1, 0), ("Z", 0, 1, 0),
    ("Z", 1, 0, 0), ("Z", 1, 1, 0), ("Z", 1, 0, 1), ("Z", 1, 1, 1), ("Z", 2, 0, 0), ("Z", 2, 1, 0), ("X", 0, 0, 0),
    ("X", 0, 1, 0), ("X", 1, 0, 0), ("X", 1, 1, 0), ("X", 1, 0, 1), ("X", 1, 1, 1), ("X", 2, 0, 0), ("X", 2, 1, 0),
)


def kernel(
    sel_hbm, gate_hbm, tok_ref, wg_ref, wu_ref, wd_ref, slots_ref, comb_ref,
    sel_ref, gate_ref, tok_v, wg_v, wu_v, wd_v, send4, recv4, exit4, ret4, rows, part, hid, relay, fin_l, fin_r,
    summed, relay1, fin1_l, fin1_r, slots32, send_sem, recv_sem, load_sem,
):
    slot = sel_hbm.shape[0]
    tok_dev, width = tok_ref.shape
    groups = 2 * RING
    n_slots = groups * slot
    halfw = width // 2
    quart = width // 4
    subw = [halfw // n for n in SUBS]
    chunk = [r.shape[1] for r in rows]
    batch_of = {g: h for h, batch in enumerate(BATCHES) for g in batch}

    dp = lax.axis_index("dp")
    ex = lax.axis_index("expert")
    my_x, my_z = dp // RING, dp % RING
    my_y, my_c = ex // 2, ex % 2

    def at_x(step):
        return (((my_x + step + RING) % RING) * RING + my_z, ex)

    def at_z(step):
        return (my_x * RING + (my_z + step + RING) % RING, ex)

    def expert_at(g):
        return ((my_y + g // 2) % RING) * 2 + (my_c + g % 2) % 2

    def at_group(g):
        return (dp, expert_at(g))

    def back(g):
        return ((RING - g // 2) % RING) * 2 + g % 2

    barrier = pltpu.get_barrier_semaphore()
    partners = [at(step) for at in (at_x, at_z) for step in (1, -1, 2)] + [at_group(g) for g in range(1, groups)]
    for who in partners:
        pl.semaphore_signal(barrier, inc=1, device_id=who, device_id_type=MESH)

    loads = {}
    loads["sel"] = pltpu.make_async_copy(sel_hbm, sel_ref, load_sem.at[7])
    loads["gate"] = pltpu.make_async_copy(gate_hbm, gate_ref, load_sem.at[8])
    loads["sel"].start()
    tokw = width // 4
    for i in range(4):
        cols = pl.ds(i * tokw, tokw)
        loads[i] = pltpu.make_async_copy(tok_ref.at[:, cols], tok_v.at[:, cols], load_sem.at[i])
        loads[i].start()
    for i, (name, src, dst) in enumerate(
        (("wg", wg_ref, wg_v), ("wu", wu_ref, wu_v), ("wd", wd_ref, wd_v)), 4
    ):
        loads[name] = pltpu.make_async_copy(src, dst, load_sem.at[i])
        loads[name].start()

    loads["gate"].start()

    def loaded(*names):
        for name in names:
            if name in loads:
                loads.pop(name).wait()

    recv_of, recv_bytes, send_bytes = {}, {}, {}

    def together(key):
        kind, h = key[0], key[1]
        if kind == "in":
            return ("own", batch_of[h])
        if kind == "r":
            return key[:3]
        if kind == "t":
            return ("up", h, 1 if h in SPLIT else 2)
        if kind == "s" and key[4] != (1 if key[3] in RSET else -1):
            return ("up", h, int(key[3] == 2) if h in SPLIT else 2)
        if kind in ("L", "R"):
            return ("S", *key[1:])
        if kind in ("l1", "r1") or (kind == "F1" and h in DIRECT):
            return ("Z", *key[1:])
        if kind == "b":
            return ("Z", h, key[2], key[4])
        return key[:4] if kind == "X" else key

    def outbox(key):
        kind, h = key[0], key[1]
        if kind == "in":
            return 0
        return (1 if kind in "fsrt" else 4 if kind != "X" else 7) + h

    def size(ref):
        n = 2
        for dim in ref.shape:
            n *= dim
        return n

    def wait_for(sem, n):
        unit = 2 * slot * width
        if n % (4 * unit) == 0:
            ref = rows[1].at[pl.ds(0, n // (4 * unit))]
        elif n % (2 * unit) == 0 and n > 8 * unit:
            ref = rows[0].at[pl.ds(0, n // (2 * unit))]
        elif n % unit == 0:
            ref = exit4.at[pl.ds(0, n // unit)]
        else:
            ref = exit4.at[pl.ds(0, 2 * n // unit), :, pl.ds(0, halfw)]
        assert size(ref) == n
        pltpu.make_async_copy(ref, ref, sem).wait()

    def remote(key, src, dst, who):
        name, box = together(key), outbox(key)
        i = recv_of.setdefault(name, len(recv_of))
        recv_bytes[name] = recv_bytes.get(name, 0) + size(dst)
        send_bytes[box] = send_bytes.get(box, 0) + size(src)
        pltpu.make_async_remote_copy(
            src_ref=src, dst_ref=dst, send_sem=send_sem.at[box], recv_sem=recv_sem.at[i],
            device_id=who, device_id_type=MESH,
        ).start()

    def need(*names):
        for name in names:
            if name in recv_bytes:
                wait_for(recv_sem.at[recv_of[name]], recv_bytes.pop(name))

    def drain(*boxes):
        for box in boxes:
            wait_for(send_sem.at[box], send_bytes.pop(box))

    near = [back(g) for g in BATCHES[0] + BATCHES[1] if g > 0]
    far = [back(g) for g in BATCHES[2]]
    with jax.named_scope("pick"):
        loaded("sel")
        row_id = lax.broadcasted_iota(jnp.int32, (n_slots, tok_dev), 0)
        lane_id = lax.broadcasted_iota(jnp.int32, (n_slots, tok_dev), 1)
        idx = jnp.full((n_slots, tok_dev), -1, jnp.int32)
        for g in range(groups):
            e = expert_at(g)
            for j in range(slot):
                idx = jnp.where(row_id == g * slot + j, sel_ref[j, e], idx)
        onehot = jnp.where(lane_id == idx, 1.0, 0.0).astype(BF16)
    for i in range(4):
        with jax.named_scope("tok"):
            loaded(i)
        with jax.named_scope("sel"):
            cols = slice(i * tokw, (i + 1) * tokw)
            slots32[:, cols] = jnp.dot(onehot, tok_v[:, cols], preferred_element_type=F32)
            for g in near:
                send4[g, :, cols] = slots32[g * slot : (g + 1) * slot, cols].astype(BF16)
    with jax.named_scope("barrier"):
        pl.semaphore_wait(barrier, len(partners))
    for g in near:
        remote(("in", back(g)), send4.at[g], recv4.at[back(g)], at_group(g))
    for g in far:
        send4[g] = slots32[g * slot : (g + 1) * slot, :].astype(BF16)
        remote(("in", back(g)), send4.at[g], recv4.at[back(g)], at_group(g))
    recv4[0] = slots32[0:slot, :].astype(BF16)
    loaded("gate")

    lane8 = lax.broadcasted_iota(jnp.int32, (8, 128), 1)
    idx_l = jnp.full((8, 128), -1, jnp.int32)
    gate_l = jnp.zeros((8, 128), F32)
    for g in range(groups):
        e = expert_at(g)
        for j in range(slot):
            here = lane8 % n_slots == g * slot + j
            idx_l = jnp.where(here, sel_ref[j, e], idx_l)
            gate_l = jnp.where(here, gate_ref[j, e], gate_l)
    g1 = gate_l.astype(BF16).astype(F32)
    rest = gate_l - g1
    g2 = rest.astype(BF16).astype(F32)
    g3 = (rest - g2).astype(BF16).astype(F32)
    term = lane8 // n_slots
    gate3 = jnp.where(term == 0, g1, jnp.where(term == 1, g2, jnp.where(term == 2, g3, 0.0)))
    tok_id = lax.broadcasted_iota(jnp.int32, (tok_dev, 128), 0)
    hit = tok_id == idx_l[0:1, :]
    comb_ref[...] = jnp.where(hit, gate3[0:1, :], 0.0).astype(BF16)

    def cut(p, lo=0, n=halfw):
        return pl.ds(p * halfw + lo, n)

    def pos(p, d1, d2):
        d1, d2 = d1 % RING, d2 % RING
        return PLACE[(d2, d1) if p == 0 else (d1, d2)]

    def first(p, step):
        return at_x(step) if p == 0 else at_z(step)

    def second(p, step):
        return at_z(step) if p == 0 else at_x(step)

    def own(h):
        need(("own", h))
        for i, g in enumerate(BATCHES[h]):
            slots32[i * slot : (i + 1) * slot, :] = recv4[g].astype(F32)
        rows[h][0] = slots32[0 : chunk[h], :].astype(BF16)

    def to_first(key, h, p, d1, step, lo, n):
        remote(
            key, rows[h].at[pos(p, d1, 0), :, cut(p, lo, n)],
            rows[h].at[pos(p, d1 - step, 0), :, cut(p, lo, n)], first(p, step),
        )

    def to_second(key, h, p, d1, d2, step):
        remote(
            key, rows[h].at[pos(p, d1, d2), :, cut(p)],
            rows[h].at[pos(p, d1, d2 - step), :, cut(p)], second(p, step),
        )

    def send_first(h, p, step):
        to_first(("f", h, p, step), h, p, 0, step, 0, halfw)

    def pass_first(h, p, step):
        need(("f", h, p, step))
        to_first(("r", h, p, step), h, p, -step, step, 0 if step == 1 else quart, quart)

    def send_second(h, p, d1, step):
        if d1 == 2:
            need(("r", h, p))
        elif d1 != 0:
            need(("f", h, p, 1 if d1 == 3 else -1))
        to_second(("s", h, p, d1, step), h, p, d1, 0, step)

    def pass_second(h, p, d1):
        step = 1 if d1 in RSET else -1
        need(("s", h, p, d1, step))
        to_second(("t", h, p, d1), h, p, d1, -step, step)

    tn = hid[0].shape[1] // 2
    places = (slice(0, len(EARLY)), slice(len(EARLY), RING * RING), slice(0, RING * RING))

    def held(h, b):
        return slice(places[b].start * chunk[h], places[b].stop * chunk[h])

    def up(h, b, n):
        for p in range(2):
            if b >= 1:
                need(("r", h, p))
            for step in (1, -1):
                need(("f", h, p, step))
                for d1 in RSET if step == 1 else LSET:
                    if b >= 1 or d1 != 2:
                        need(("s", h, p, d1, step))
        need(("up", h, b))
        loaded("wg", "wu")
        lhs = rows[h][places[b]].reshape(-1, width)
        cols = slice(n * tn, (n + 1) * tn)
        gate_val = jnp.dot(lhs, wg_v[:, cols], preferred_element_type=F32)
        up_val = jnp.dot(lhs, wu_v[:, cols], preferred_element_type=F32)
        hid[h][held(h, b), cols] = (gate_val / (1.0 + jnp.exp(-gate_val)) * up_val).astype(BF16)

    dn = 512

    def down(h, b, p, i):
        loaded("wd")
        start = p * halfw + i * subw[h]
        for c in range(start, start + subw[h], dn):
            cols = slice(c, c + dn)
            val = jnp.dot(hid[h][held(h, b), :], wd_v[:, cols], preferred_element_type=F32)
            part[h][places[b], :, cols] = val.astype(BF16).reshape(-1, chunk[h], dn)

    def sub(h, i, lo=0, n=None):
        return pl.ds(i * subw[h] + lo, subw[h] if n is None else n)

    def psub(h, p, i):
        return cut(p, i * subw[h], subw[h])

    def send_far(h, p, d1, i):
        step = 1 if d1 in RSET else -1
        remote(
            ("F", h, p, d1, i), part[h].at[pos(p, d1, 2), :, psub(h, p, i)],
            relay[h].at[p, d1, :, sub(h, i)], second(p, step),
        )

    def send_left_of(h, p, d1, i):
        remote(
            ("L", h, p, d1, i), part[h].at[pos(p, d1, 1), :, psub(h, p, i)],
            fin_l[h].at[p, d1, :, sub(h, i)], second(p, 1),
        )

    def send_right_of(h, p, d1, i):
        remote(
            ("R", h, p, d1, i), part[h].at[pos(p, d1, 3), :, psub(h, p, i)],
            fin_r[h].at[p, d1, :, sub(h, i)], second(p, -1),
        )

    def add_far(h, p, d1, i):
        need(("F", h, p, d1, i))
        right = d1 in RSET
        mine = part[h][pos(p, d1, 1 if right else 3), :, psub(h, p, i)]
        here = relay[h].at[p, d1, :, sub(h, i)]
        here[...] = (here[...].astype(F32) + mine.astype(F32)).astype(BF16)
        if right:
            remote(("L", h, p, d1, i), here, fin_l[h].at[p, d1, :, sub(h, i)], second(p, 1))
        else:
            remote(("R", h, p, d1, i), here, fin_r[h].at[p, d1, :, sub(h, i)], second(p, -1))

    def add_up(h, p, d1, i):
        need(("S", h, p, d1, i))
        mine = part[h][pos(p, d1, 0), :, psub(h, p, i)]
        total = (
            mine.astype(F32)
            + fin_l[h][p, d1, :, sub(h, i)].astype(F32)
            + fin_r[h][p, d1, :, sub(h, i)].astype(F32)
        )
        summed[h][p, d1, :, sub(h, i)] = total.astype(BF16)
        lo, hi = sub(h, i, 0, subw[h] // 2), sub(h, i, subw[h] // 2, subw[h] // 2)
        if h in DIRECT:
            if d1 != 0:
                name, dst, step = {2: ("F1", relay1, 2), 1: ("l1", fin1_l, 1), 3: ("r1", fin1_r, -1)}[d1]
                remote(
                    (name, h, p, i), summed[h].at[p, d1, :, sub(h, i)], dst[h].at[p, :, sub(h, i)],
                    first(p, step),
                )
            return
        if d1 == 2:
            remote(("F1", h, p, 1, i), summed[h].at[p, 2, :, lo], relay1[h].at[p, :, lo], first(p, 1))
            remote(("F1", h, p, -1, i), summed[h].at[p, 2, :, hi], relay1[h].at[p, :, hi], first(p, -1))
        elif d1 == 1:
            remote(("l1", h, p, i), summed[h].at[p, 1, :, hi], fin1_l[h].at[p, :, hi], first(p, 1))
        elif d1 == 3:
            remote(("r1", h, p, i), summed[h].at[p, 3, :, lo], fin1_r[h].at[p, :, lo], first(p, -1))

    def add_first(h, p, step, i):
        need(("F1", h, p, step, i))
        d1 = 1 if step == 1 else 3
        cols = sub(h, i, 0 if step == 1 else subw[h] // 2, subw[h] // 2)
        here = relay1[h].at[p, :, cols]
        here[...] = (here[...].astype(F32) + summed[h][p, d1, :, cols].astype(F32)).astype(BF16)
        dst = fin1_l if step == 1 else fin1_r
        remote(("b", h, p, step, i), here, dst[h].at[p, :, cols], first(p, step))

    def finish(h, p, i):
        need(("Z", h, p, i))
        total = (
            summed[h][p, 0, :, sub(h, i)].astype(F32)
            + fin1_l[h][p, :, sub(h, i)].astype(F32)
            + fin1_r[h][p, :, sub(h, i)].astype(F32)
        )
        if h in DIRECT:
            total += relay1[h][p, :, sub(h, i)].astype(F32)
        slots32[0 : chunk[h], psub(h, p, i)] = total
        for r, g in enumerate(BATCHES[h]):
            value = slots32[r * slot : (r + 1) * slot, psub(h, p, i)].astype(BF16)
            if g == 0:
                ret4[0, :, psub(h, p, i)] = value
            else:
                exit4[g, :, psub(h, p, i)] = value
                remote(
                    ("X", h, p, i, back(g)), exit4.at[g, :, psub(h, p, i)],
                    ret4.at[back(g), :, psub(h, p, i)], at_group(g),
                )

    def take(h, p, i):
        need(("X", h, p, i))
        for g in BATCHES[h]:
            slots_ref[g * slot : (g + 1) * slot, psub(h, p, i)] = ret4[g, :, psub(h, p, i)].astype(F32)

    steps = {
        "own": own, "f": send_first, "r": pass_first, "s": send_second, "t": pass_second,
        "up": up, "down": down, "F": send_far, "L": send_left_of, "R": send_right_of,
        "A": add_far, "S": add_up, "B": add_first, "Z": finish, "X": take,
    }
    ends = [i for i, entry in enumerate(ORDER) if entry[0] == "Z"]
    for at, (name, *args) in enumerate(ORDER):
        with jax.named_scope("_".join(str(a) for a in (name, *args))):
            steps[name](*args)
        if at == ends[-1]:
            with jax.named_scope("drain"):
                drain(*range(9))
    assert len(recv_of) == N_RECV, len(recv_of)
    with jax.named_scope("last_sends"):
        drain(9)


def combine_kernel(slots_ref, comb_ref, out_ref, out_v, out_sem):
    width = slots_ref.shape[1]
    n = 1024
    stores = []
    for k, c in enumerate(range(0, width, n)):
        value = slots_ref[:, c : c + n].astype(BF16)
        stack = jnp.concatenate([value, value, value, jnp.zeros_like(value)], axis=0)
        out_v[:, c : c + n] = jnp.dot(
            comb_ref[...], stack, preferred_element_type=F32).astype(BF16)
        store = pltpu.make_async_copy(
            out_v.at[:, pl.ds(c, n)], out_ref.at[:, pl.ds(c, n)], out_sem.at[k])
        store.start()
        stores.append(store)
    for store in stores:
        store.wait()


def per_device(tokens, select, gates, w_gate, w_up, w_down):
    tok_dev, width = tokens.shape
    slot = select.shape[1]
    ff = w_gate.shape[2]
    halfw = width // 2

    def vmems(shape):
        return [pltpu.VMEM(shape(slot * len(batch)), BF16) for batch in BATCHES]

    vmem, hbm = pl.BlockSpec(memory_space=pltpu.VMEM), pl.BlockSpec(memory_space=pltpu.HBM)
    slots, comb = pl.pallas_call(
        kernel,
        out_shape=(pltpu.VMEM((8 * slot, width), F32), pltpu.VMEM((tok_dev, 128), BF16)),
        in_specs=[hbm] * 6,
        out_specs=(vmem, vmem),
        scratch_shapes=[
            pltpu.SMEM((slot, 8), jnp.int32),
            pltpu.SMEM((slot, 8), F32),
            pltpu.VMEM((tok_dev, width), BF16),
            pltpu.VMEM((width, ff), BF16),
            pltpu.VMEM((width, ff), BF16),
            pltpu.VMEM((ff, width), BF16),
            pltpu.VMEM((8, slot, width), BF16),
            pltpu.VMEM((8, slot, width), BF16),
            pltpu.VMEM((8, slot, width), BF16),
            pltpu.VMEM((8, slot, width), BF16),
            vmems(lambda c: (16, c, width)),
            vmems(lambda c: (16, c, width)),
            vmems(lambda c: (16 * c, ff)),
            vmems(lambda c: (2, 4, c, halfw)),
            vmems(lambda c: (2, 4, c, halfw)),
            vmems(lambda c: (2, 4, c, halfw)),
            vmems(lambda c: (2, 4, c, halfw)),
            vmems(lambda c: (2, c, halfw)),
            vmems(lambda c: (2, c, halfw)),
            vmems(lambda c: (2, c, halfw)),
            pltpu.VMEM((8 * slot, width), F32),
            pltpu.SemaphoreType.DMA((10,)),
            pltpu.SemaphoreType.DMA((N_RECV,)),
            pltpu.SemaphoreType.DMA((9,)),
        ],
        compiler_params=pltpu.CompilerParams(
            collective_id=0, has_side_effects=True, vmem_limit_bytes=56 * 1024 * 1024
        ),
        name="moe",
    )(
        select.T, gates.T, tokens, w_gate[0], w_up[0], w_down[0],
    )
    return pl.pallas_call(
        combine_kernel,
        out_shape=jax.ShapeDtypeStruct((tok_dev, width), BF16),
        in_specs=[vmem, vmem],
        out_specs=hbm,
        scratch_shapes=[pltpu.VMEM((tok_dev, width), BF16), pltpu.SemaphoreType.DMA((4,))],
        compiler_params=pltpu.CompilerParams(vmem_limit_bytes=8 * 1024 * 1024),
        name="combine",
    )(slots, comb)


def solution(mesh):
    return jax.shard_map(
        per_device,
        mesh=mesh,
        in_specs=(
            P(("dp", "expert"), None),
            P(None, ("dp", "expert")),
            P(None, ("dp", "expert")),
            P("expert", None, "dp"),
            P("expert", None, "dp"),
            P("expert", "dp", None),
        ),
        out_specs=P(("dp", "expert"), None),
        check_vma=False,
    )
```

time: 64.6 us -> 63.6 us (0.985)
  Pallas kernels: 64.5 us -> 63.5 us
    pallas_call x1, Pallas kernels: 63.3 us -> 62.2 us  [per_device(): pl.pallas_call(kernel, out_shape=(pltpu.VMEM((8 * slot, width), F32), plt...]
where the time goes in v7:
time: 63.6 us; the launch traced here: 63.5 us
  Pallas kernels  63.5 us (100%)
    pallas_call x1, Pallas kernels, per_device(): pl.pallas_call(kernel, out_shape=(pltpu.VMEM((8 * slot, width), F32), plt...  62.2 us

profile of v7, /device:TPU:1, one launch (start us, length us, event | category | flops | bytes accessed | tf_op | source)
XLA Modules:
  0.0 63.5 jit_solution(869029066864082545)
XLA Ops:
  0.0 62.2 %moe.1 = (f32[32,4096]{1,0:T(8,128)S(1)}, bf16[128,128]{1,0:T(8,128)(2,1)S(1)}) custom-call(s32[4,8]{1,0:T(4,128)} %bitcast.8, f32[4,8]{1,0:T(4,128)} %bitcast.9, bf16[128,4096]{1,0:T(8,128)(2,1)} %tok_ref.1, bf16[4096,512]{1,0:T(8,128)(2,1)} %bitcast.5, bf16[4096,512]{1,0:T(8,128)(2,1)} %bitcast.6, bf16[512,4096]{1,0:T(8,128)(2,1)} %bitcast.7), custom_call_target="tpu_custom_call" | custom-call | tf_op jit(solution)/shard_map/moe/pallas_call | solution.py:472
  62.3 1.2 %combine.1 = bf16[128,4096]{1,0:T(8,128)(2,1)} custom-call(f32[32,4096]{1,0:T(8,128)S(1)} %get-tuple-element.7.slots_ref, bf16[128,128]{1,0:T(8,128)(2,1)S(1)} %get-tuple-element.8.comb_ref), custom_call_target="tpu_custom_call" | custom-call | tf_op jit(solution)/shard_map/combine/pallas_call | solution.py:510

commit v8 on v7

--- a/solution.py
+++ b/solution.py
@@ -8,8 +8,8 @@
 MESH = pl.DeviceIdType.MESH
 BF16, F32 = jnp.bfloat16, jnp.float32
 RING = 4
-N_RECV = 141
-DIRECT = (2,)
+N_RECV = 137
+DIRECT = (0, 2)
 RSET, LSET = (0, 3), (2, 1)
 ROUND = tuple((z, x) for z in range(RING) for x in range(RING))
 EARLY = tuple(at for at in ROUND if 2 not in at and at != (1, 3))
@@ -20,53 +20,52 @@
 SPLIT = (1,)
 
 ORDER = (
-    ("own", 0), ("f", 0, 0, -1), ("f", 0, 1, -1), ("s", 0, 1, 0, -1), ("f", 0, 1, 1), ("s", 0, 0, 0, -1),
-    ("f", 0, 0, 1), ("s", 0, 0, 0, 1), ("s", 0, 1, 0, 1), ("s", 0, 0, 1, -1), ("s", 0, 1, 1, -1), ("s", 0, 0, 1, 1),
-    ("s", 0, 1, 1, 1), ("s", 0, 1, 3, -1), ("r", 0, 1, 1), ("r", 0, 0, 1), ("s", 0, 0, 3, 1), ("s", 0, 0, 3, -1),
-    ("s", 0, 1, 3, 1), ("r", 0, 1, -1), ("r", 0, 0, -1), ("own", 1), ("f", 1, 0, -1), ("f", 1, 0, 1),
-    ("s", 1, 1, 0, -1), ("s", 1, 1, 0, 1), ("f", 1, 1, -1), ("s", 1, 0, 0, -1), ("f", 1, 1, 1), ("s", 1, 0, 0, 1),
-    ("t", 0, 0, 0), ("t", 0, 1, 0), ("own", 2), ("f", 2, 0, -1), ("f", 2, 0, 1), ("f", 2, 1, 1), ("s", 2, 1, 0, 1),
-    ("s", 2, 0, 0, 1), ("s", 2, 0, 0, -1), ("f", 2, 1, -1), ("s", 2, 1, 0, -1), ("t", 0, 0, 1), ("t", 0, 1, 1),
-    ("s", 0, 1, 2, -1), ("s", 0, 0, 2, -1), ("s", 0, 1, 2, 1), ("t", 0, 0, 3), ("t", 0, 1, 3), ("s", 0, 0, 2, 1),
-    ("r", 1, 1, -1), ("r", 1, 0, -1), ("r", 1, 1, 1), ("s", 1, 0, 3, 1), ("s", 1, 1, 3, 1), ("r", 1, 0, 1),
-    ("s", 1, 0, 3, -1), ("s", 1, 1, 1, -1), ("s", 1, 0, 1, 1), ("s", 1, 1, 3, -1), ("s", 1, 0, 1, -1),
-    ("s", 1, 1, 1, 1), ("t", 1, 0, 0), ("t", 1, 1, 0), ("s", 2, 0, 1, -1), ("s", 2, 0, 1, 1), ("r", 2, 0, -1),
-    ("s", 2, 1, 1, -1), ("r", 2, 1, -1), ("r", 2, 1, 1), ("r", 2, 0, 1), ("s", 2, 0, 3, -1), ("s", 2, 1, 3, 1),
-    ("s", 2, 0, 3, 1), ("s", 2, 1, 3, -1), ("s", 2, 1, 1, 1), ("t", 2, 0, 0), ("t", 2, 1, 0), ("t", 0, 0, 2),
-    ("t", 0, 1, 2), ("s", 1, 1, 2, -1), ("s", 1, 1, 2, 1), ("t", 1, 1, 1), ("t", 1, 1, 3), ("t", 1, 0, 3),
-    ("s", 1, 0, 2, -1), ("s", 1, 0, 2, 1), ("t", 1, 0, 1), ("t", 2, 0, 1), ("up", 1, 0, 0), ("t", 2, 1, 1),
-    ("up", 1, 0, 1), ("down", 1, 0, 0, 1), ("s", 2, 0, 2, -1), ("up", 0, 2, 0), ("s", 2, 1, 2, -1),
-    ("down", 1, 0, 0, 0), ("R", 1, 0, 3, 0), ("down", 1, 0, 1, 1), ("R", 1, 1, 3, 1), ("t", 2, 0, 3),
-    ("L", 1, 1, 1, 1), ("t", 1, 0, 2), ("t", 1, 1, 2), ("R", 1, 1, 0, 1), ("R", 1, 0, 0, 0), ("s", 2, 0, 2, 1),
-    ("t", 2, 1, 3), ("R", 1, 0, 3, 1), ("down", 1, 0, 1, 0), ("L", 1, 1, 1, 0), ("up", 0, 2, 1), ("down", 0, 2, 0, 0),
-    ("F", 0, 0, 1, 0), ("L", 0, 0, 1, 0), ("F", 0, 0, 2, 0), ("F", 0, 0, 3, 0), ("R", 0, 0, 3, 0), ("R", 0, 0, 0, 0),
-    ("down", 0, 2, 1, 0), ("t", 2, 0, 2), ("F", 0, 1, 3, 0), ("F", 0, 1, 0, 0), ("F", 0, 1, 2, 0), ("F", 0, 1, 1, 0),
-    ("R", 0, 1, 0, 0), ("R", 1, 1, 0, 0), ("R", 1, 1, 3, 0), ("L", 0, 0, 2, 0), ("s", 2, 1, 2, 1), ("t", 2, 1, 2),
-    ("R", 0, 1, 3, 0), ("L", 1, 0, 1, 0), ("L", 0, 1, 1, 0), ("R", 1, 0, 0, 1), ("L", 1, 0, 1, 1), ("F", 0, 0, 0, 0),
-    ("L", 0, 1, 2, 0), ("up", 1, 1, 0), ("up", 1, 1, 1), ("A", 0, 1, 3, 0), ("down", 1, 1, 0, 1), ("F", 1, 0, 3, 1),
-    ("F", 1, 0, 0, 1), ("down", 1, 1, 1, 0), ("F", 1, 1, 2, 0), ("F", 1, 1, 0, 0), ("F", 1, 1, 3, 0),
-    ("down", 1, 1, 0, 0), ("F", 1, 0, 0, 0), ("F", 1, 0, 2, 0), ("F", 1, 0, 2, 1), ("down", 1, 1, 1, 1),
-    ("L", 1, 1, 2, 1), ("A", 0, 0, 2, 0), ("F", 1, 1, 0, 1), ("F", 1, 1, 2, 1), ("A", 0, 0, 1, 0), ("A", 0, 1, 0, 0),
-    ("A", 0, 1, 1, 0), ("L", 1, 1, 2, 0), ("A", 0, 1, 2, 0), ("F", 1, 1, 1, 1), ("L", 1, 0, 2, 0), ("A", 0, 0, 3, 0),
-    ("F", 1, 0, 1, 1), ("F", 1, 1, 1, 0), ("F", 1, 0, 3, 0), ("F", 1, 0, 1, 0), ("L", 1, 0, 2, 1), ("F", 1, 1, 3, 1),
-    ("A", 0, 0, 0, 0), ("up", 2, 2, 0), ("S", 0, 1, 3, 0), ("A", 1, 1, 0, 0), ("up", 2, 2, 1), ("A", 1, 0, 2, 0),
-    ("A", 1, 1, 2, 0), ("down", 2, 2, 1, 0), ("A", 1, 0, 0, 0), ("F", 2, 1, 3, 0), ("R", 2, 1, 3, 0),
-    ("A", 1, 0, 2, 1), ("F", 2, 1, 0, 0), ("F", 2, 1, 2, 0), ("L", 2, 1, 1, 0), ("R", 2, 1, 0, 0), ("L", 2, 1, 2, 0),
-    ("A", 1, 0, 0, 1), ("A", 1, 1, 2, 1), ("down", 2, 2, 0, 0), ("F", 2, 0, 3, 0), ("S", 0, 0, 2, 0),
-    ("F", 2, 0, 2, 0), ("S", 0, 0, 3, 0), ("L", 2, 0, 1, 0), ("R", 2, 0, 0, 0), ("F", 2, 0, 0, 0), ("A", 1, 1, 0, 1),
-    ("R", 2, 0, 3, 0), ("F", 2, 0, 1, 0), ("L", 2, 0, 2, 0), ("A", 1, 1, 3, 0), ("F", 2, 1, 1, 0), ("A", 1, 0, 3, 1),
-    ("S", 0, 1, 1, 0), ("S", 0, 1, 0, 0), ("S", 0, 0, 1, 0), ("S", 0, 1, 2, 0), ("A", 1, 0, 3, 0), ("A", 1, 0, 1, 1),
-    ("A", 1, 1, 1, 1), ("A", 1, 0, 1, 0), ("A", 1, 1, 1, 0), ("A", 1, 1, 3, 1), ("S", 0, 0, 0, 0), ("S", 1, 1, 2, 0),
-    ("S", 1, 1, 0, 0), ("S", 1, 0, 2, 0), ("S", 1, 0, 0, 0), ("A", 2, 1, 3, 0), ("S", 1, 0, 2, 1), ("S", 1, 0, 0, 1),
-    ("A", 2, 1, 2, 0), ("A", 2, 1, 0, 0), ("A", 2, 0, 2, 0), ("A", 2, 0, 3, 0), ("S", 1, 1, 2, 1), ("A", 2, 0, 0, 0),
-    ("B", 0, 0, 1, 0), ("B", 0, 0, -1, 0), ("A", 2, 0, 1, 0), ("S", 1, 1, 0, 1), ("B", 0, 1, -1, 0),
-    ("A", 2, 1, 1, 0), ("S", 1, 0, 3, 1), ("S", 1, 1, 3, 0), ("S", 1, 0, 1, 1), ("S", 1, 1, 1, 1), ("B", 0, 1, 1, 0),
-    ("S", 1, 0, 1, 0), ("S", 1, 1, 1, 0), ("S", 1, 1, 3, 1), ("B", 1, 1, -1, 0), ("S", 1, 0, 3, 0),
-    ("B", 1, 0, -1, 0), ("B", 1, 0, 1, 0), ("B", 1, 1, 1, 0), ("B", 1, 0, -1, 1), ("S", 2, 0, 2, 0),
-    ("S", 2, 1, 3, 0), ("B", 1, 1, -1, 1), ("S", 2, 0, 3, 0), ("S", 2, 1, 2, 0), ("B", 1, 0, 1, 1), ("B", 1, 1, 1, 1),
-    ("S", 2, 0, 1, 0), ("S", 2, 1, 0, 0), ("S", 2, 0, 0, 0), ("Z", 0, 0, 0), ("S", 2, 1, 1, 0), ("Z", 0, 1, 0),
-    ("Z", 1, 0, 0), ("Z", 1, 1, 0), ("Z", 1, 0, 1), ("Z", 1, 1, 1), ("Z", 2, 0, 0), ("Z", 2, 1, 0), ("X", 0, 0, 0),
-    ("X", 0, 1, 0), ("X", 1, 0, 0), ("X", 1, 1, 0), ("X", 1, 0, 1), ("X", 1, 1, 1), ("X", 2, 0, 0), ("X", 2, 1, 0),
+    ("own", 0), ("f", 0, 0, 1), ("f", 0, 1, -1), ("f", 0, 1, 1), ("f", 0, 0, -1), ("s", 0, 1, 0, -1),
+    ("s", 0, 0, 0, -1), ("s", 0, 1, 0, 1), ("s", 0, 0, 0, 1), ("r", 0, 0, 1), ("r", 0, 1, -1), ("s", 0, 0, 3, -1),
+    ("r", 0, 1, 1), ("r", 0, 0, -1), ("s", 0, 0, 1, -1), ("s", 0, 1, 3, 1), ("s", 0, 0, 1, 1), ("s", 0, 1, 1, 1),
+    ("s", 0, 1, 3, -1), ("s", 0, 1, 1, -1), ("own", 1), ("f", 1, 0, 1), ("f", 1, 1, 1), ("f", 1, 0, -1),
+    ("f", 1, 1, -1), ("s", 1, 1, 0, -1), ("s", 1, 0, 0, 1), ("s", 1, 0, 0, -1), ("s", 0, 0, 3, 1), ("s", 1, 1, 0, 1),
+    ("t", 0, 1, 0), ("t", 0, 0, 0), ("own", 2), ("f", 2, 1, 1), ("f", 2, 0, 1), ("s", 2, 1, 0, 1), ("s", 2, 0, 0, 1),
+    ("f", 2, 0, -1), ("f", 2, 1, -1), ("s", 2, 0, 0, -1), ("s", 0, 1, 2, -1), ("s", 0, 0, 2, -1), ("s", 0, 0, 2, 1),
+    ("s", 0, 1, 2, 1), ("t", 0, 1, 3), ("t", 0, 0, 1), ("t", 0, 1, 1), ("r", 1, 1, 1), ("s", 1, 1, 3, 1),
+    ("s", 1, 0, 3, -1), ("r", 1, 0, 1), ("s", 1, 1, 1, -1), ("s", 1, 0, 3, 1), ("s", 1, 0, 1, -1), ("r", 1, 0, -1),
+    ("s", 1, 0, 1, 1), ("t", 1, 0, 0), ("s", 1, 1, 1, 1), ("t", 1, 1, 0), ("t", 0, 0, 3), ("r", 1, 1, -1),
+    ("r", 2, 1, -1), ("s", 2, 1, 1, 1), ("s", 2, 1, 1, -1), ("r", 2, 0, -1), ("s", 2, 0, 1, -1), ("s", 2, 0, 1, 1),
+    ("s", 1, 1, 3, -1), ("r", 2, 0, 1), ("s", 2, 0, 3, -1), ("s", 2, 1, 3, -1), ("t", 0, 1, 2), ("r", 2, 1, 1),
+    ("s", 2, 0, 3, 1), ("t", 2, 1, 0), ("t", 0, 0, 2), ("t", 2, 0, 0), ("s", 2, 1, 0, -1), ("t", 1, 1, 3),
+    ("t", 1, 0, 3), ("t", 2, 1, 1), ("s", 1, 0, 2, 1), ("s", 1, 0, 2, -1), ("t", 1, 0, 1), ("s", 1, 1, 2, -1),
+    ("s", 2, 1, 3, 1), ("s", 1, 1, 2, 1), ("t", 1, 1, 1), ("up", 1, 0, 0), ("t", 2, 0, 1), ("up", 1, 0, 1),
+    ("down", 1, 0, 1, 1), ("up", 0, 2, 0), ("s", 2, 1, 2, 1), ("s", 2, 1, 2, -1), ("s", 2, 0, 2, -1), ("up", 0, 2, 1),
+    ("t", 2, 0, 3), ("t", 1, 0, 2), ("down", 0, 2, 0, 0), ("t", 1, 1, 2), ("L", 0, 0, 1, 0), ("F", 0, 0, 3, 0),
+    ("R", 0, 0, 0, 0), ("F", 0, 0, 2, 0), ("down", 1, 0, 0, 1), ("L", 1, 0, 1, 1), ("R", 1, 0, 0, 1),
+    ("s", 2, 0, 2, 1), ("F", 0, 0, 1, 0), ("down", 0, 2, 1, 0), ("F", 0, 1, 0, 0), ("R", 0, 1, 0, 0),
+    ("F", 0, 1, 2, 0), ("F", 0, 1, 3, 0), ("L", 0, 1, 1, 0), ("down", 1, 0, 0, 0), ("L", 1, 0, 1, 0), ("t", 2, 1, 3),
+    ("F", 0, 0, 0, 0), ("L", 0, 0, 2, 0), ("R", 1, 0, 0, 0), ("L", 1, 1, 1, 1), ("down", 1, 0, 1, 0),
+    ("R", 1, 1, 0, 0), ("L", 1, 1, 1, 0), ("R", 0, 1, 3, 0), ("R", 1, 0, 3, 1), ("R", 1, 1, 3, 1), ("L", 0, 1, 2, 0),
+    ("t", 2, 1, 2), ("t", 2, 0, 2), ("R", 1, 0, 3, 0), ("F", 0, 1, 1, 0), ("R", 0, 0, 3, 0), ("R", 1, 1, 3, 0),
+    ("up", 1, 1, 0), ("A", 0, 0, 3, 0), ("up", 1, 1, 1), ("down", 1, 1, 1, 1), ("F", 1, 1, 3, 1),
+    ("down", 1, 1, 1, 0), ("F", 1, 1, 3, 0), ("down", 1, 1, 0, 0), ("F", 1, 0, 3, 0), ("down", 1, 1, 0, 1),
+    ("F", 1, 0, 2, 1), ("L", 1, 1, 2, 1), ("F", 1, 0, 0, 0), ("F", 1, 1, 1, 0), ("F", 1, 1, 0, 1), ("F", 1, 1, 1, 1),
+    ("L", 1, 0, 2, 0), ("F", 1, 0, 3, 1), ("L", 1, 1, 2, 0), ("F", 1, 0, 1, 1), ("F", 1, 0, 2, 0), ("F", 1, 0, 1, 0),
+    ("F", 1, 1, 2, 0), ("F", 1, 1, 2, 1), ("L", 1, 0, 2, 1), ("A", 0, 1, 0, 0), ("F", 1, 0, 0, 1), ("up", 2, 2, 0),
+    ("up", 2, 2, 1), ("A", 0, 1, 1, 0), ("down", 2, 2, 1, 0), ("F", 2, 1, 3, 0), ("F", 2, 1, 2, 0), ("R", 2, 1, 0, 0),
+    ("L", 2, 1, 1, 0), ("A", 1, 0, 2, 1), ("A", 1, 0, 3, 0), ("down", 2, 2, 0, 0), ("F", 2, 0, 2, 0),
+    ("F", 2, 0, 1, 0), ("A", 1, 0, 1, 1), ("R", 2, 0, 3, 0), ("R", 2, 0, 0, 0), ("A", 1, 0, 0, 0), ("F", 2, 0, 3, 0),
+    ("F", 2, 0, 0, 0), ("F", 2, 1, 0, 0), ("L", 2, 0, 1, 0), ("L", 2, 1, 2, 0), ("F", 2, 1, 1, 0), ("L", 2, 0, 2, 0),
+    ("R", 2, 1, 3, 0), ("A", 1, 1, 0, 1), ("A", 0, 1, 3, 0), ("A", 1, 0, 2, 0), ("A", 1, 1, 2, 0), ("A", 1, 0, 3, 1),
+    ("A", 1, 1, 2, 1), ("S", 0, 1, 1, 0), ("A", 1, 1, 3, 1), ("A", 1, 0, 0, 1), ("A", 2, 1, 3, 0), ("S", 1, 0, 2, 1),
+    ("A", 2, 1, 2, 0), ("S", 1, 0, 3, 0), ("A", 2, 0, 2, 0), ("S", 1, 0, 0, 0), ("A", 2, 1, 0, 0), ("A", 2, 0, 1, 0),
+    ("A", 2, 1, 1, 0), ("A", 1, 1, 1, 0), ("A", 2, 0, 3, 0), ("A", 1, 1, 1, 1), ("S", 1, 0, 1, 1), ("A", 1, 1, 3, 0),
+    ("F", 1, 1, 0, 0), ("A", 2, 0, 0, 0), ("A", 1, 0, 1, 0), ("S", 1, 1, 2, 0), ("A", 0, 1, 2, 0), ("S", 1, 1, 2, 1),
+    ("S", 1, 1, 3, 1), ("S", 1, 0, 2, 0), ("S", 1, 0, 3, 1), ("S", 2, 1, 2, 0), ("B", 1, 0, -1, 1), ("S", 2, 1, 3, 0),
+    ("S", 2, 0, 2, 0), ("B", 1, 0, 1, 1), ("A", 0, 0, 2, 0), ("S", 2, 0, 1, 0), ("S", 2, 1, 1, 0), ("A", 0, 0, 1, 0),
+    ("S", 2, 1, 0, 0), ("S", 1, 0, 0, 1), ("S", 1, 0, 1, 0), ("S", 1, 1, 1, 0), ("S", 2, 0, 3, 0), ("S", 1, 1, 3, 0),
+    ("B", 1, 1, -1, 0), ("B", 1, 1, -1, 1), ("S", 1, 1, 1, 1), ("R", 1, 1, 0, 1), ("S", 2, 0, 0, 0),
+    ("A", 1, 1, 0, 0), ("B", 1, 1, 1, 0), ("S", 0, 1, 2, 0), ("B", 1, 0, 1, 0), ("B", 1, 1, 1, 1), ("B", 1, 0, -1, 0),
+    ("A", 0, 0, 0, 0), ("S", 0, 0, 3, 0), ("S", 0, 1, 3, 0), ("Z", 1, 0, 1), ("S", 0, 0, 2, 0), ("Z", 2, 1, 0),
+    ("S", 0, 0, 1, 0), ("Z", 2, 0, 0), ("S", 1, 1, 0, 1), ("S", 1, 1, 0, 0), ("Z", 1, 1, 0), ("Z", 1, 0, 0),
+    ("Z", 1, 1, 1), ("S", 0, 1, 0, 0), ("S", 0, 0, 0, 0), ("Z", 0, 1, 0), ("X", 1, 0, 1), ("Z", 0, 0, 0),
+    ("X", 2, 1, 0), ("X", 0, 1, 0), ("X", 1, 1, 0), ("X", 2, 0, 0), ("X", 1, 0, 0), ("X", 0, 0, 0), ("X", 1, 1, 1),
 )
 
 

time: 63.6 us -> 62.8 us (0.987)
  Pallas kernels: 63.5 us -> 62.7 us
    pallas_call x1, Pallas kernels: 62.2 us -> 61.4 us  [per_device(): pl.pallas_call(kernel, out_shape=(pltpu.VMEM((8 * slot, width), F32), plt...]
where the time goes in v8:
time: 62.8 us; the launch traced here: 62.7 us
  Pallas kernels  62.7 us (100%)
    pallas_call x1, Pallas kernels, per_device(): pl.pallas_call(kernel, out_shape=(pltpu.VMEM((8 * slot, width), F32), plt...  61.4 us

profile of v8, /device:TPU:1, one launch (start us, length us, event | category | flops | bytes accessed | tf_op | source)
XLA Modules:
  0.0 62.7 jit_solution(8945383550945872924)
XLA Ops:
  0.0 61.4 %moe.1 = (f32[32,4096]{1,0:T(8,128)S(1)}, bf16[128,128]{1,0:T(8,128)(2,1)S(1)}) custom-call(s32[4,8]{1,0:T(4,128)} %bitcast.8, f32[4,8]{1,0:T(4,128)} %bitcast.9, bf16[128,4096]{1,0:T(8,128)(2,1)} %tok_ref.1, bf16[4096,512]{1,0:T(8,128)(2,1)} %bitcast.5, bf16[4096,512]{1,0:T(8,128)(2,1)} %bitcast.6, bf16[512,4096]{1,0:T(8,128)(2,1)} %bitcast.7), custom_call_target="tpu_custom_call" | custom-call | tf_op jit(solution)/shard_map/moe/pallas_call | solution.py:471
  61.4 1.2 %combine.1 = bf16[128,4096]{1,0:T(8,128)(2,1)} custom-call(f32[32,4096]{1,0:T(8,128)S(1)} %get-tuple-element.7.slots_ref, bf16[128,128]{1,0:T(8,128)(2,1)S(1)} %get-tuple-element.8.comb_ref), custom_call_target="tpu_custom_call" | custom-call | tf_op jit(solution)/shard_map/combine/pallas_call | solution.py:509

commit v9 on v8

--- a/solution.py
+++ b/solution.py
@@ -20,52 +20,53 @@
 SPLIT = (1,)
 
 ORDER = (
-    ("own", 0), ("f", 0, 0, 1), ("f", 0, 1, -1), ("f", 0, 1, 1), ("f", 0, 0, -1), ("s", 0, 1, 0, -1),
-    ("s", 0, 0, 0, -1), ("s", 0, 1, 0, 1), ("s", 0, 0, 0, 1), ("r", 0, 0, 1), ("r", 0, 1, -1), ("s", 0, 0, 3, -1),
-    ("r", 0, 1, 1), ("r", 0, 0, -1), ("s", 0, 0, 1, -1), ("s", 0, 1, 3, 1), ("s", 0, 0, 1, 1), ("s", 0, 1, 1, 1),
-    ("s", 0, 1, 3, -1), ("s", 0, 1, 1, -1), ("own", 1), ("f", 1, 0, 1), ("f", 1, 1, 1), ("f", 1, 0, -1),
-    ("f", 1, 1, -1), ("s", 1, 1, 0, -1), ("s", 1, 0, 0, 1), ("s", 1, 0, 0, -1), ("s", 0, 0, 3, 1), ("s", 1, 1, 0, 1),
-    ("t", 0, 1, 0), ("t", 0, 0, 0), ("own", 2), ("f", 2, 1, 1), ("f", 2, 0, 1), ("s", 2, 1, 0, 1), ("s", 2, 0, 0, 1),
-    ("f", 2, 0, -1), ("f", 2, 1, -1), ("s", 2, 0, 0, -1), ("s", 0, 1, 2, -1), ("s", 0, 0, 2, -1), ("s", 0, 0, 2, 1),
-    ("s", 0, 1, 2, 1), ("t", 0, 1, 3), ("t", 0, 0, 1), ("t", 0, 1, 1), ("r", 1, 1, 1), ("s", 1, 1, 3, 1),
-    ("s", 1, 0, 3, -1), ("r", 1, 0, 1), ("s", 1, 1, 1, -1), ("s", 1, 0, 3, 1), ("s", 1, 0, 1, -1), ("r", 1, 0, -1),
-    ("s", 1, 0, 1, 1), ("t", 1, 0, 0), ("s", 1, 1, 1, 1), ("t", 1, 1, 0), ("t", 0, 0, 3), ("r", 1, 1, -1),
-    ("r", 2, 1, -1), ("s", 2, 1, 1, 1), ("s", 2, 1, 1, -1), ("r", 2, 0, -1), ("s", 2, 0, 1, -1), ("s", 2, 0, 1, 1),
-    ("s", 1, 1, 3, -1), ("r", 2, 0, 1), ("s", 2, 0, 3, -1), ("s", 2, 1, 3, -1), ("t", 0, 1, 2), ("r", 2, 1, 1),
-    ("s", 2, 0, 3, 1), ("t", 2, 1, 0), ("t", 0, 0, 2), ("t", 2, 0, 0), ("s", 2, 1, 0, -1), ("t", 1, 1, 3),
-    ("t", 1, 0, 3), ("t", 2, 1, 1), ("s", 1, 0, 2, 1), ("s", 1, 0, 2, -1), ("t", 1, 0, 1), ("s", 1, 1, 2, -1),
-    ("s", 2, 1, 3, 1), ("s", 1, 1, 2, 1), ("t", 1, 1, 1), ("up", 1, 0, 0), ("t", 2, 0, 1), ("up", 1, 0, 1),
-    ("down", 1, 0, 1, 1), ("up", 0, 2, 0), ("s", 2, 1, 2, 1), ("s", 2, 1, 2, -1), ("s", 2, 0, 2, -1), ("up", 0, 2, 1),
-    ("t", 2, 0, 3), ("t", 1, 0, 2), ("down", 0, 2, 0, 0), ("t", 1, 1, 2), ("L", 0, 0, 1, 0), ("F", 0, 0, 3, 0),
-    ("R", 0, 0, 0, 0), ("F", 0, 0, 2, 0), ("down", 1, 0, 0, 1), ("L", 1, 0, 1, 1), ("R", 1, 0, 0, 1),
-    ("s", 2, 0, 2, 1), ("F", 0, 0, 1, 0), ("down", 0, 2, 1, 0), ("F", 0, 1, 0, 0), ("R", 0, 1, 0, 0),
-    ("F", 0, 1, 2, 0), ("F", 0, 1, 3, 0), ("L", 0, 1, 1, 0), ("down", 1, 0, 0, 0), ("L", 1, 0, 1, 0), ("t", 2, 1, 3),
-    ("F", 0, 0, 0, 0), ("L", 0, 0, 2, 0), ("R", 1, 0, 0, 0), ("L", 1, 1, 1, 1), ("down", 1, 0, 1, 0),
-    ("R", 1, 1, 0, 0), ("L", 1, 1, 1, 0), ("R", 0, 1, 3, 0), ("R", 1, 0, 3, 1), ("R", 1, 1, 3, 1), ("L", 0, 1, 2, 0),
-    ("t", 2, 1, 2), ("t", 2, 0, 2), ("R", 1, 0, 3, 0), ("F", 0, 1, 1, 0), ("R", 0, 0, 3, 0), ("R", 1, 1, 3, 0),
-    ("up", 1, 1, 0), ("A", 0, 0, 3, 0), ("up", 1, 1, 1), ("down", 1, 1, 1, 1), ("F", 1, 1, 3, 1),
-    ("down", 1, 1, 1, 0), ("F", 1, 1, 3, 0), ("down", 1, 1, 0, 0), ("F", 1, 0, 3, 0), ("down", 1, 1, 0, 1),
-    ("F", 1, 0, 2, 1), ("L", 1, 1, 2, 1), ("F", 1, 0, 0, 0), ("F", 1, 1, 1, 0), ("F", 1, 1, 0, 1), ("F", 1, 1, 1, 1),
-    ("L", 1, 0, 2, 0), ("F", 1, 0, 3, 1), ("L", 1, 1, 2, 0), ("F", 1, 0, 1, 1), ("F", 1, 0, 2, 0), ("F", 1, 0, 1, 0),
-    ("F", 1, 1, 2, 0), ("F", 1, 1, 2, 1), ("L", 1, 0, 2, 1), ("A", 0, 1, 0, 0), ("F", 1, 0, 0, 1), ("up", 2, 2, 0),
-    ("up", 2, 2, 1), ("A", 0, 1, 1, 0), ("down", 2, 2, 1, 0), ("F", 2, 1, 3, 0), ("F", 2, 1, 2, 0), ("R", 2, 1, 0, 0),
-    ("L", 2, 1, 1, 0), ("A", 1, 0, 2, 1), ("A", 1, 0, 3, 0), ("down", 2, 2, 0, 0), ("F", 2, 0, 2, 0),
-    ("F", 2, 0, 1, 0), ("A", 1, 0, 1, 1), ("R", 2, 0, 3, 0), ("R", 2, 0, 0, 0), ("A", 1, 0, 0, 0), ("F", 2, 0, 3, 0),
-    ("F", 2, 0, 0, 0), ("F", 2, 1, 0, 0), ("L", 2, 0, 1, 0), ("L", 2, 1, 2, 0), ("F", 2, 1, 1, 0), ("L", 2, 0, 2, 0),
-    ("R", 2, 1, 3, 0), ("A", 1, 1, 0, 1), ("A", 0, 1, 3, 0), ("A", 1, 0, 2, 0), ("A", 1, 1, 2, 0), ("A", 1, 0, 3, 1),
-    ("A", 1, 1, 2, 1), ("S", 0, 1, 1, 0), ("A", 1, 1, 3, 1), ("A", 1, 0, 0, 1), ("A", 2, 1, 3, 0), ("S", 1, 0, 2, 1),
-    ("A", 2, 1, 2, 0), ("S", 1, 0, 3, 0), ("A", 2, 0, 2, 0), ("S", 1, 0, 0, 0), ("A", 2, 1, 0, 0), ("A", 2, 0, 1, 0),
-    ("A", 2, 1, 1, 0), ("A", 1, 1, 1, 0), ("A", 2, 0, 3, 0), ("A", 1, 1, 1, 1), ("S", 1, 0, 1, 1), ("A", 1, 1, 3, 0),
-    ("F", 1, 1, 0, 0), ("A", 2, 0, 0, 0), ("A", 1, 0, 1, 0), ("S", 1, 1, 2, 0), ("A", 0, 1, 2, 0), ("S", 1, 1, 2, 1),
-    ("S", 1, 1, 3, 1), ("S", 1, 0, 2, 0), ("S", 1, 0, 3, 1), ("S", 2, 1, 2, 0), ("B", 1, 0, -1, 1), ("S", 2, 1, 3, 0),
-    ("S", 2, 0, 2, 0), ("B", 1, 0, 1, 1), ("A", 0, 0, 2, 0), ("S", 2, 0, 1, 0), ("S", 2, 1, 1, 0), ("A", 0, 0, 1, 0),
-    ("S", 2, 1, 0, 0), ("S", 1, 0, 0, 1), ("S", 1, 0, 1, 0), ("S", 1, 1, 1, 0), ("S", 2, 0, 3, 0), ("S", 1, 1, 3, 0),
-    ("B", 1, 1, -1, 0), ("B", 1, 1, -1, 1), ("S", 1, 1, 1, 1), ("R", 1, 1, 0, 1), ("S", 2, 0, 0, 0),
-    ("A", 1, 1, 0, 0), ("B", 1, 1, 1, 0), ("S", 0, 1, 2, 0), ("B", 1, 0, 1, 0), ("B", 1, 1, 1, 1), ("B", 1, 0, -1, 0),
-    ("A", 0, 0, 0, 0), ("S", 0, 0, 3, 0), ("S", 0, 1, 3, 0), ("Z", 1, 0, 1), ("S", 0, 0, 2, 0), ("Z", 2, 1, 0),
-    ("S", 0, 0, 1, 0), ("Z", 2, 0, 0), ("S", 1, 1, 0, 1), ("S", 1, 1, 0, 0), ("Z", 1, 1, 0), ("Z", 1, 0, 0),
-    ("Z", 1, 1, 1), ("S", 0, 1, 0, 0), ("S", 0, 0, 0, 0), ("Z", 0, 1, 0), ("X", 1, 0, 1), ("Z", 0, 0, 0),
-    ("X", 2, 1, 0), ("X", 0, 1, 0), ("X", 1, 1, 0), ("X", 2, 0, 0), ("X", 1, 0, 0), ("X", 0, 0, 0), ("X", 1, 1, 1),
+    ("own", 0), ("f", 0, 1, -1), ("f", 0, 0, -1), ("f", 0, 1, 1), ("f", 0, 0, 1), ("s", 0, 1, 0, -1),
+    ("s", 0, 0, 0, 1), ("s", 0, 0, 0, -1), ("s", 0, 1, 0, 1), ("r", 0, 1, -1), ("r", 0, 0, -1), ("r", 0, 1, 1),
+    ("s", 0, 1, 3, -1), ("r", 0, 0, 1), ("s", 0, 0, 3, 1), ("s", 0, 1, 3, 1), ("s", 0, 0, 1, -1), ("own", 1),
+    ("f", 1, 1, -1), ("f", 1, 1, 1), ("s", 1, 0, 0, 1), ("f", 1, 0, -1), ("f", 1, 0, 1), ("own", 2),
+    ("s", 1, 0, 0, -1), ("s", 0, 1, 1, 1), ("f", 2, 1, -1), ("s", 2, 0, 0, 1), ("s", 0, 0, 1, 1), ("t", 0, 1, 0),
+    ("s", 0, 1, 1, -1), ("f", 2, 0, -1), ("s", 0, 0, 2, -1), ("s", 0, 1, 2, -1), ("s", 1, 1, 0, -1), ("f", 2, 0, 1),
+    ("t", 0, 0, 0), ("s", 0, 0, 3, -1), ("s", 1, 1, 0, 1), ("r", 1, 1, -1), ("f", 2, 1, 1), ("s", 2, 1, 0, 1),
+    ("r", 1, 1, 1), ("s", 1, 0, 3, 1), ("r", 1, 0, -1), ("t", 0, 1, 1), ("r", 1, 0, 1), ("s", 1, 1, 3, 1),
+    ("s", 1, 0, 3, -1), ("s", 1, 0, 1, -1), ("s", 1, 1, 1, -1), ("s", 1, 1, 3, -1), ("s", 1, 1, 1, 1),
+    ("r", 2, 1, -1), ("r", 2, 0, 1), ("s", 1, 0, 1, 1), ("t", 0, 0, 1), ("r", 2, 1, 1), ("r", 2, 0, -1),
+    ("s", 1, 1, 2, -1), ("s", 2, 1, 3, 1), ("s", 0, 0, 2, 1), ("t", 0, 0, 3), ("t", 0, 1, 2), ("s", 0, 1, 2, 1),
+    ("s", 2, 1, 1, -1), ("s", 2, 0, 1, -1), ("s", 2, 0, 3, 1), ("t", 0, 1, 3), ("t", 2, 0, 0), ("t", 1, 1, 0),
+    ("t", 1, 0, 0), ("s", 1, 0, 2, -1), ("s", 2, 1, 1, 1), ("t", 1, 1, 1), ("s", 1, 1, 2, 1), ("t", 0, 0, 2),
+    ("s", 2, 0, 3, -1), ("s", 1, 0, 2, 1), ("t", 1, 1, 3), ("s", 2, 1, 2, -1), ("s", 2, 1, 0, -1), ("s", 2, 0, 2, -1),
+    ("up", 1, 0, 0), ("t", 1, 0, 1), ("up", 1, 0, 1), ("down", 1, 0, 1, 1), ("t", 1, 0, 2), ("t", 1, 0, 3),
+    ("t", 2, 1, 0), ("down", 1, 0, 0, 1), ("s", 2, 0, 1, 1), ("t", 1, 1, 2), ("s", 2, 1, 3, -1), ("R", 1, 0, 3, 1),
+    ("up", 0, 2, 0), ("R", 1, 1, 3, 1), ("up", 0, 2, 1), ("t", 2, 0, 1), ("t", 2, 0, 3), ("t", 2, 1, 3),
+    ("t", 2, 1, 1), ("s", 2, 1, 2, 1), ("down", 1, 0, 1, 0), ("s", 2, 0, 0, -1), ("s", 2, 0, 2, 1),
+    ("down", 1, 0, 0, 0), ("L", 1, 1, 1, 1), ("t", 2, 0, 2), ("t", 2, 1, 2), ("down", 0, 2, 1, 0), ("L", 1, 1, 1, 0),
+    ("down", 0, 2, 0, 0), ("L", 0, 0, 2, 0), ("F", 0, 1, 0, 0), ("F", 0, 1, 2, 0), ("F", 0, 0, 2, 0),
+    ("F", 0, 0, 3, 0), ("F", 0, 0, 1, 0), ("R", 0, 1, 0, 0), ("F", 0, 1, 1, 0), ("R", 0, 0, 0, 0), ("F", 0, 1, 3, 0),
+    ("L", 1, 0, 1, 0), ("R", 1, 1, 3, 0), ("R", 1, 0, 0, 0), ("L", 0, 1, 1, 0), ("F", 0, 0, 0, 0), ("up", 1, 1, 0),
+    ("up", 1, 1, 1), ("down", 1, 1, 1, 0), ("F", 1, 1, 3, 0), ("L", 1, 0, 1, 1), ("R", 0, 0, 3, 0),
+    ("down", 1, 1, 0, 0), ("F", 1, 1, 1, 0), ("F", 1, 0, 1, 0), ("down", 1, 1, 1, 1), ("F", 1, 1, 1, 1),
+    ("F", 1, 0, 2, 0), ("F", 1, 1, 2, 0), ("down", 1, 1, 0, 1), ("F", 1, 0, 0, 1), ("F", 1, 0, 0, 0),
+    ("F", 1, 0, 2, 1), ("F", 1, 1, 0, 1), ("F", 1, 1, 2, 1), ("up", 2, 2, 0), ("F", 1, 0, 1, 1), ("L", 0, 1, 2, 0),
+    ("up", 2, 2, 1), ("A", 0, 0, 3, 0), ("F", 1, 0, 3, 0), ("F", 1, 1, 3, 1), ("down", 2, 2, 1, 0), ("F", 2, 1, 2, 0),
+    ("L", 1, 0, 2, 0), ("F", 1, 0, 3, 1), ("F", 2, 1, 1, 0), ("F", 2, 1, 0, 0), ("A", 0, 1, 0, 0),
+    ("down", 2, 2, 0, 0), ("F", 2, 0, 3, 0), ("F", 2, 1, 3, 0), ("L", 1, 1, 2, 0), ("L", 2, 0, 2, 0),
+    ("L", 2, 0, 1, 0), ("F", 2, 0, 2, 0), ("R", 2, 1, 0, 0), ("L", 1, 1, 2, 1), ("F", 1, 1, 0, 0), ("R", 1, 0, 3, 0),
+    ("A", 0, 0, 2, 0), ("R", 0, 1, 3, 0), ("F", 2, 0, 1, 0), ("L", 1, 0, 2, 1), ("A", 1, 0, 1, 0), ("A", 1, 0, 2, 1),
+    ("A", 1, 1, 2, 1), ("A", 1, 1, 2, 0), ("A", 1, 0, 2, 0), ("A", 2, 1, 2, 0), ("R", 2, 1, 3, 0), ("L", 2, 1, 1, 0),
+    ("L", 2, 1, 2, 0), ("S", 0, 1, 0, 0), ("A", 1, 0, 0, 0), ("A", 2, 1, 3, 0), ("A", 2, 1, 0, 0), ("A", 1, 0, 0, 1),
+    ("A", 1, 0, 1, 1), ("A", 2, 0, 2, 0), ("A", 1, 1, 3, 1), ("A", 2, 1, 1, 0), ("A", 1, 0, 3, 1), ("A", 1, 1, 1, 1),
+    ("A", 2, 0, 1, 0), ("A", 1, 1, 3, 0), ("F", 2, 0, 0, 0), ("A", 1, 1, 1, 0), ("A", 2, 0, 3, 0), ("A", 1, 0, 3, 0),
+    ("R", 2, 0, 3, 0), ("A", 0, 1, 1, 0), ("S", 1, 1, 2, 0), ("S", 1, 0, 2, 1), ("S", 1, 0, 0, 0), ("A", 0, 1, 3, 0),
+    ("A", 0, 1, 2, 0), ("S", 1, 0, 2, 0), ("R", 1, 0, 0, 1), ("A", 1, 1, 0, 1), ("R", 1, 1, 0, 1), ("S", 1, 1, 2, 1),
+    ("S", 2, 1, 2, 0), ("S", 2, 1, 1, 0), ("S", 2, 1, 3, 0), ("S", 2, 0, 2, 0), ("R", 2, 0, 0, 0), ("A", 0, 0, 1, 0),
+    ("S", 1, 0, 1, 1), ("A", 2, 0, 0, 0), ("S", 1, 1, 3, 1), ("L", 0, 0, 1, 0), ("S", 2, 0, 3, 0), ("S", 2, 0, 1, 0),
+    ("S", 1, 1, 3, 0), ("S", 1, 0, 3, 1), ("B", 1, 0, 1, 1), ("B", 1, 0, -1, 1), ("S", 1, 1, 1, 1), ("S", 1, 1, 1, 0),
+    ("S", 2, 1, 0, 0), ("B", 1, 1, 1, 0), ("R", 1, 1, 0, 0), ("B", 1, 1, 1, 1), ("B", 1, 1, -1, 0), ("A", 1, 1, 0, 0),
+    ("A", 0, 0, 0, 0), ("B", 1, 1, -1, 1), ("S", 1, 0, 1, 0), ("S", 0, 1, 1, 0), ("S", 1, 0, 3, 0), ("S", 0, 1, 3, 0),
+    ("B", 1, 0, 1, 0), ("S", 0, 1, 2, 0), ("S", 1, 0, 0, 1), ("B", 1, 0, -1, 0), ("Z", 2, 1, 0), ("S", 0, 0, 2, 0),
+    ("S", 0, 0, 3, 0), ("S", 1, 1, 0, 1), ("S", 2, 0, 0, 0), ("Z", 2, 0, 0), ("S", 0, 0, 1, 0), ("Z", 1, 0, 1),
+    ("S", 1, 1, 0, 0), ("Z", 1, 1, 0), ("Z", 1, 1, 1), ("Z", 1, 0, 0), ("S", 0, 0, 0, 0), ("Z", 0, 0, 0),
+    ("Z", 0, 1, 0), ("X", 0, 0, 0), ("X", 1, 0, 1), ("X", 2, 0, 0), ("X", 2, 1, 0), ("X", 1, 1, 0), ("X", 1, 1, 1),
+    ("X", 0, 1, 0), ("X", 1, 0, 0),
 )
 
 

time: 62.8 us -> 61.4 us (0.978)
  Pallas kernels: 62.7 us -> 61.3 us
    pallas_call x1, Pallas kernels: 61.4 us -> 60 us  [per_device(): pl.pallas_call(kernel, out_shape=(pltpu.VMEM((8 * slot, width), F32), plt...]
where the time goes in v9:
time: 61.4 us; the launch traced here: 61.3 us
  Pallas kernels  61.3 us (100%)
    pallas_call x1, Pallas kernels, per_device(): pl.pallas_call(kernel, out_shape=(pltpu.VMEM((8 * slot, width), F32), plt...  60 us

profile of v9, /device:TPU:1, one launch (start us, length us, event | category | flops | bytes accessed | tf_op | source)
XLA Modules:
  0.0 61.3 jit_solution(4395850508836867934)
XLA Ops:
  0.0 60.0 %moe.1 = (f32[32,4096]{1,0:T(8,128)S(1)}, bf16[128,128]{1,0:T(8,128)(2,1)S(1)}) custom-call(s32[4,8]{1,0:T(4,128)} %bitcast.8, f32[4,8]{1,0:T(4,128)} %bitcast.9, bf16[128,4096]{1,0:T(8,128)(2,1)} %tok_ref.1, bf16[4096,512]{1,0:T(8,128)(2,1)} %bitcast.5, bf16[4096,512]{1,0:T(8,128)(2,1)} %bitcast.6, bf16[512,4096]{1,0:T(8,128)(2,1)} %bitcast.7), custom_call_target="tpu_custom_call" | custom-call | tf_op jit(solution)/shard_map/moe/pallas_call | solution.py:472
  60.1 1.2 %combine.1 = bf16[128,4096]{1,0:T(8,128)(2,1)} custom-call(f32[32,4096]{1,0:T(8,128)S(1)} %get-tuple-element.7.slots_ref, bf16[128,128]{1,0:T(8,128)(2,1)S(1)} %get-tuple-element.8.comb_ref), custom_call_target="tpu_custom_call" | custom-call | tf_op jit(solution)/shard_map/combine/pallas_call | solution.py:510
